TPU v7x, 512 devices: a whole 4x8x8 slice. The times are simulated.
512 devices in a mesh: section: 4 (over y_lo), dp: 32 (over y_hi, z, core), tensor: 4 (over x).
Axes of the slice: x: 4, y: 8 (y_hi: 2, y_lo: 4; y = y_hi * 4 + y_lo), z: 8, core: 2. Of those that a mesh axis runs over, the one named last changes fastest.
Arguments:
- cotangent: bfloat16 [2, 4096, 8192], P(None, 'dp', 'tensor'), may hold values from -6 to 6
- stash: bfloat16 [4, 2, 4096, 8192], P('section', None, 'dp', 'tensor'), may hold values from -0.0625 to 0.0625
- factor_a: bfloat16 [4, 1024, 8192], P('section', 'dp', 'tensor'), may hold values from -0.0625 to 0.0625
- factor_b: bfloat16 [4, 8192, 1024], P('section', ('tensor', 'dp')), may hold values from -0.1875 to 0.1875
- block_vals: bfloat16 [4, 128, 128, 128], P('section', ('dp', 'tensor')), may hold values from -0.25 to 0.25
- block_rows: int32 [4, 128], P('section'), may hold values from 0 to 63, as said below
- block_cols: int32 [4, 128], P('section'), may hold values from 0 to 63, as said below
Outputs:
- grad_in: bfloat16 [4, 2, 4096, 8192], P('section', None, 'dp', 'tensor')
- block_grad: float32 [4, 128, 128, 128], P('section', ('dp', 'tensor'))
Inputs may be any that keep to these rules, and one draw needn't show every extreme that they name: The support lies inside the diagonal part of each tensor shard. Within a section all (block_rows, block_cols) pairs are distinct. For every dp index o < 32, tensor index t < 4 and slot k < 1, the block at position (o * 4 + t) + k has both its row and its column block index in [t * 8192 // (128 * 4), (t + 1) * 8192 // (128 * 4)). `block_cols`: drawn together with block_rows; the same promise holds.
All inputs are finite; a program needn't handle non-finite values.
Results may differ from a plain program's by a relative error of at most 0.024.
Values may be sent and summed in bfloat16 or wider, within the bound.
No kernel may reach another device: no remote copies, remote signals or barrier semaphores. Data moves between devices by JAX's collectives and lax.ppermute only.
A program may use at most 128 MiB of HBM per device.

v0:
```python
import jax
import jax.numpy as jnp
from jax import lax
from jax.experimental import pallas as pl
from jax.experimental.pallas import tpu as pltpu
from jax.sharding import PartitionSpec as P

BF = jnp.bfloat16
F32 = jnp.float32
FAR = 2
CORES = 2
LIMIT = pltpu.CompilerParams(vmem_limit_bytes=20 * 1024 * 1024)


def contract_last(a, b):
    return lax.dot_general(a, b, (((1,), (1,)), ((), ())), preferred_element_type=F32)


def contract_first(a, b):
    return lax.dot_general(a, b, (((0,), (0,)), ((), ())), preferred_element_type=F32)


def block_at(pos, size):
    return pl.ds(pl.multiple_of(pos * size, size), size)


def whole(shape):
    zeros = (0,) * len(shape)
    return pl.BlockSpec(shape, lambda i: zeros)


SCALARS = pl.BlockSpec(memory_space=pltpu.SMEM)
GRID = 4


def cost(flops, size):
    return pl.CostEstimate(flops=flops, bytes_accessed=size, transcendentals=0)


def both_cores(core, mine_ref, other_ref, joined_ref):
    joined_ref[:, core] = mine_ref[...]
    joined_ref[:, 1 - core] = other_ref[...]
    _, _, _, width = joined_ref.shape
    return joined_ref[...].reshape(-1, width)


def rank_kernel(meta_ref, u_ref, mine_ref, other_ref, o_ref, joined_ref):
    weight = both_cores(meta_ref[0], mine_ref, other_ref, joined_ref)
    product = contract_last(u_ref[...], weight).astype(BF)
    for i in range(o_ref.shape[0]):
        o_ref[i] = product


def rank_partial(meta, u, mine, other, copies):
    tokens, width = u.shape
    pieces, rows, _ = mine.shape
    step = pieces // GRID
    rank = pieces * rows * CORES
    shard = pl.BlockSpec((step, rows, width), lambda i: (i, 0, 0))
    return pl.pallas_call(
        rank_kernel,
        grid=(GRID,),
        in_specs=[SCALARS, whole((tokens, width)), shard, shard],
        out_specs=pl.BlockSpec((copies, tokens, rank // GRID), lambda i: (0, 0, i)),
        out_shape=pltpu.HBM((copies, tokens, rank), BF),
        scratch_shapes=[pltpu.VMEM((step, CORES, rows, width), BF)],
        cost_estimate=cost(2 * tokens * width * rank, 2 * width * rank),
        compiler_params=LIMIT,
        name="rank_partial",
    )(meta, u, mine, other)


def sparse_kernel(meta_ref, rows_ref, cols_ref, u_ref, mine_ref, other_ref, o_ref, t_ref):
    pieces, _, width = mine_ref.shape
    size = t_ref.shape[1]
    core, shift, base = meta_ref[0], meta_ref[2], meta_ref[3]
    group = meta_ref[4]

    def product(k, carry):
        for ref, far in ((mine_ref, 0), (other_ref, 1)):
            value = jnp.concatenate(
                [ref[k, :, j * size : (j + 1) * size] for j in range(width // size)], axis=0
            )
            n = CORES * k + (core if far == 0 else 1 - core)
            at = block_at(cols_ref[n * group + shift] - base, size)
            t_ref[CORES * k + far] = contract_last(u_ref[:, at], value)
        return carry

    lax.fori_loop(0, pieces, product, 0, unroll=4)
    o_ref[...] = jnp.zeros_like(o_ref)

    def place(k, carry):
        for far in range(CORES):
            n = CORES * k + (core if far == 0 else 1 - core)
            at = block_at(rows_ref[n * group + shift] - base, size)
            o_ref[:, at] += t_ref[CORES * k + far]
        return carry

    lax.fori_loop(0, pieces, place, 0, unroll=2)


def sparse_product(meta, rows, cols, u, mine, other, size):
    tokens, width = u.shape
    pieces, total, rank = mine.shape
    sub = size * size // rank
    values = pl.BlockSpec((pieces, sub, rank), lambda i: (0, (total - sub) // sub, 0))
    return pl.pallas_call(
        sparse_kernel,
        grid=(1,),
        in_specs=[SCALARS, SCALARS, SCALARS, whole((tokens, width)), values, values],
        out_specs=whole((tokens, width)),
        out_shape=pltpu.HBM((tokens, width), F32),
        scratch_shapes=[pltpu.VMEM((CORES * pieces, tokens, size), F32)],
        cost_estimate=cost(2 * tokens * width * rank, 2 * width * rank),
        compiler_params=LIMIT,
        name="sparse_product",
    )(meta, rows, cols, u, mine, other)


def input_kernel(meta_ref, p_ref, mine_ref, other_ref, s_ref, o_ref, ra_ref, joined_ref):
    @pl.when(pl.program_id(0) == 0)
    def _():
        total = p_ref[0].astype(F32)
        for i in range(1, p_ref.shape[0]):
            total += p_ref[i].astype(F32)
        ra_ref[...] = total.astype(BF)

    weight = both_cores(meta_ref[0], mine_ref, other_ref, joined_ref)
    o_ref[...] = (contract_last(ra_ref[...], weight) + s_ref[...]).astype(BF)


def input_grad(meta, arrived, mine, other, sparse, size):
    copies, tokens, rank = arrived.shape
    pieces, total, _ = mine.shape
    rows = total - size * size // rank
    step = pieces // GRID
    width = CORES * pieces * rows
    shard = pl.BlockSpec((step, rows, rank), lambda i: (i, 0, 0))
    slab = pl.BlockSpec((tokens, width // GRID), lambda i: (0, i))
    return pl.pallas_call(
        input_kernel,
        grid=(GRID,),
        in_specs=[SCALARS, whole((copies, tokens, rank)), shard, shard, slab],
        out_specs=slab,
        out_shape=jax.ShapeDtypeStruct((tokens, width), BF),
        scratch_shapes=[
            pltpu.VMEM((tokens, rank), BF),
            pltpu.VMEM((step, CORES, rows, rank), BF),
        ],
        cost_estimate=cost(2 * tokens * width * rank, 2 * width * rank),
        compiler_params=LIMIT,
        name="input_grad",
    )(meta, arrived, mine, other, sparse)


def block_kernel(meta_ref, rows_ref, cols_ref, st_ref, u0_ref, u1_ref, o_ref):
    blocks, size, _ = o_ref.shape
    bits = blocks.bit_length() - 1
    place, shift, base, group = meta_ref[1], meta_ref[2], meta_ref[3], meta_ref[4]

    def one(n, carry):
        turned = jnp.int32(0)
        for bit in range(bits):
            turned = turned | (((n >> bit) & 1) << (bits - 1 - bit))
        index = (place ^ turned) * group + shift
        row_at = block_at(rows_ref[index] - base, size)
        col_at = block_at(cols_ref[index] - base, size)
        left = jnp.concatenate([st_ref[0, :, row_at], st_ref[1, :, row_at]], axis=0)
        right = jnp.concatenate([u0_ref[:, col_at], u1_ref[:, col_at]], axis=0)
        o_ref[n] = contract_first(left, right)
        return carry

    lax.fori_loop(0, blocks, one, 0, unroll=4)


def block_products(meta, rows, cols, stash, u0, u1, blocks, size):
    batches, tokens, width = stash.shape
    vmem = pl.BlockSpec(memory_space=pltpu.VMEM)
    return pl.pallas_call(
        block_kernel,
        in_specs=[SCALARS, SCALARS, SCALARS, vmem, vmem, vmem],
        out_specs=vmem,
        out_shape=jax.ShapeDtypeStruct((blocks, size, size), F32),
        cost_estimate=cost(2 * batches * tokens * size * size * blocks, 6 * tokens * width),
        compiler_params=LIMIT,
        name="block_products",
    )(meta, rows, cols, stash, u0, u1)


class Data:
    def __init__(self):
        self.count = lax.axis_size("dp")
        self.ring = self.count // (FAR * CORES)
        self.place = lax.axis_index("dp")
        self.core = lax.rem(self.place, CORES)
        self.z = lax.rem(lax.div(self.place, CORES), self.ring)
        self.far = lax.div(self.place, CORES * self.ring)

    def at(self, far, z, core):
        return (far * self.ring + z % self.ring) * CORES + core

    def every(self):
        return [
            (f, z, c) for f in range(FAR) for z in range(self.ring) for c in range(CORES)
        ]

    def along(self, value, steps):
        perm = [(self.at(f, z, c), self.at(f, z + steps, c)) for f, z, c in self.every()]
        return lax.ppermute(value, "dp", perm)

    def swapped(self, value, distance):
        return lax.ppermute(value, "dp", [(p, p ^ distance) for p in range(self.count)])

    def gather(self, shard):
        got = self.swapped(shard, self.count // FAR)
        first = self.far == 0
        pair = jnp.stack([jnp.where(first, shard, got), jnp.where(first, got, shard)])
        rows, width = shard.shape
        full = jnp.zeros((FAR, self.ring, rows, width), BF)

        def put(full, piece, far, z):
            spot = (far, lax.rem(z, self.ring), 0, 0)
            return lax.dynamic_update_slice(
                full, piece[:, None], spot, allow_negative_indices=False
            )

        full = put(full, pair, 0, self.z)
        up = down = pair
        half = self.ring // 2
        for k in range(1, half):
            up = self.along(up, 1)
            down = self.along(down, -1)
            full = put(full, up, 0, self.z - k + self.ring)
            full = put(full, down, 0, self.z + k)
        up = self.along(up[:1], 1)
        down = self.along(down[1:], -1)
        full = put(full, up, 0, self.z + half)
        full = put(full, down, 1, self.z + half)
        mine = full.reshape(-1, rows, width)
        other = self.swapped(mine, 1)
        return mine, other

    def sum_at_owner(self, blocks):
        distance = 1
        while distance < self.count:
            half = blocks.shape[0] // 2
            sent = blocks[half:].astype(BF)
            blocks = blocks[:half] + self.swapped(sent, distance).astype(F32)
            distance *= 2
        return blocks


def pass_back(value):
    sections = lax.axis_size("section")
    return lax.ppermute(value, "section", [(i, i - 1) for i in range(1, sections)])


def pick(choices, which):
    out = choices[-1]
    for i in range(len(choices) - 1):
        out = jnp.where(which == i, choices[i], out)
    return out


def whole_step(cotangent, stash, factor_a, factor_b, block_vals, block_rows, block_cols):
    sections = lax.axis_size("section")
    section_pos = lax.axis_index("section")
    tensor_pos = lax.axis_index("tensor")
    tensor_count = lax.axis_size("tensor")
    data = Data()
    size = block_vals.shape[-1]
    rank = factor_b.shape[-1]
    batches = stash.shape[1]
    local_blocks = stash.shape[3] // size

    sub = size * size // rank
    lanes = rank // size
    packed = block_vals[0, 0].reshape(lanes, sub, size).transpose(1, 0, 2).reshape(sub, rank)
    a_mine, a_other = data.gather(factor_a[0])
    bv_mine, bv_other = data.gather(jnp.concatenate([factor_b[0], packed], axis=0))
    meta = jnp.stack(
        [data.core, data.place, tensor_pos, tensor_pos * local_blocks, jnp.int32(tensor_count)]
    )
    rows, cols = block_rows[0], block_cols[0]

    ups = [[cotangent[m]] for m in range(batches)]
    grads = [[] for _ in range(batches)]
    for stage in range(sections):
        for m in range(batches):
            u = ups[m][stage]
            partial = rank_partial(meta, u, a_mine, a_other, tensor_count)
            arrived = lax.all_to_all(partial, "tensor", 0, 0, tiled=True)
            sparse = sparse_product(meta, rows, cols, u, bv_mine, bv_other, size)
            grad = input_grad(meta, arrived, bv_mine, bv_other, sparse, size)
            grads[m].append(grad)
            if stage + 1 < sections:
                ups[m].append(pass_back(grad))

    turn = sections - 1 - section_pos
    used = [pick(ups[m], turn) for m in range(batches)]
    blocks = block_products(
        meta, rows, cols, stash[0], used[0], used[1], data.count, size
    )
    block_grad = data.sum_at_owner(blocks)
    grads_in = jnp.stack([pick(grads[m], turn) for m in range(batches)])
    return grads_in[None], block_grad[None]


def solution(mesh):
    in_specs = (
        P(None, "dp", "tensor"),
        P("section", None, "dp", "tensor"),
        P("section", "dp", "tensor"),
        P("section", ("tensor", "dp"), None),
        P("section", ("dp", "tensor"), None, None),
        P("section", None),
        P("section", None),
    )
    out_specs = (P("section", None, "dp", "tensor"), P("section", ("dp", "tensor"), None, None))
    return jax.shard_map(
        whole_step, mesh=mesh, in_specs=in_specs, out_specs=out_specs, check_vma=False
    )
```

profile of v0, /device:TPU:40, one launch (start us, length us, event | category | flops | bytes accessed | tf_op | source)
XLA Modules:
  0.0 387.5 jit_solution(9238771170788037783)
XLA Ops:
  0.6 2.9 collective-permute-start
  5.3 6.8 %collective-permute-start.10 = (bf16[80,1024]{1,0:T(8,128)(2,1)S(1)}, bf16[80,1024]{1,0:T(8,128)(2,1)S(1)}, u32[]{:S(2)}, u32[]{:S(2)}) collective-permute-start(bf16[80,1024]{1,0:T(8,128)(2,1)S(1)} %pad_maximum_fusion.2), channel_id=1, source_target_pairs={{0,64},{4,68},{8,72},{12,76},{16,80},{20,84},{24,88},{28,92},{32,9... | collective-permute-start | bytes 491528 | tf_op jit(solution)/shard_map/ppermute | solution.py:212
  12.2 2.9 collective-permute-done
  16.1 4.3 %collective-permute-start.1 = (bf16[2,32,2048]{2,1,0:T(8,128)(2,1)S(1)}, bf16[2,32,2048]{2,1,0:T(8,128)(2,1)S(1)}, u32[]{:S(2)}, u32[]{:S(2)}) collective-permute-start(bf16[2,32,2048]{2,1,0:T(8,128)(2,1)S(1)} %pad_maximum_fusion.1), channel_id=1, source_target_pairs={{0,8},{4,12},{8,16},{12,20},{16,24},{20,28},{24,32},{28,36},{32,40... | collective-permute-start | bytes 786440 | tf_op jit(solution)/shard_map/ppermute | solution.py:209
  20.4 8.6 %collective-permute-start.2 = (bf16[2,32,2048]{2,1,0:T(8,128)(2,1)S(1)}, bf16[2,32,2048]{2,1,0:T(8,128)(2,1)S(1)}, u32[]{:S(2)}, u32[]{:S(2)}) collective-permute-start(bf16[2,32,2048]{2,1,0:T(8,128)(2,1)S(1)} %pad_maximum_fusion.1), channel_id=1, source_target_pairs={{0,56},{4,60},{8,0},{12,4},{16,8},{20,12},{24,16},{28,20},{32,24},... | collective-permute-start | bytes 786440 | tf_op jit(solution)/shard_map/ppermute | solution.py:209
  33.3 5.1 %collective-permute-start.12 = (bf16[2,80,1024]{2,1,0:T(8,128)(2,1)S(1)}, bf16[2,80,1024]{2,1,0:T(8,128)(2,1)S(1)}, u32[]{:S(2)}, u32[]{:S(2)}) collective-permute-start(bf16[2,80,1024]{2,1,0:T(8,128)(2,1)S(1)} %pad_maximum_fusion), channel_id=1, source_target_pairs={{0,56},{4,60},{8,0},{12,4},{16,8},{20,12},{24,16},{28,20},{32,24},... | collective-permute-start | bytes 983048 | tf_op jit(solution)/shard_map/ppermute | solution.py:209
  40.8 5.1 %collective-permute-start.4 = (bf16[2,32,2048]{2,1,0:T(8,128)(2,1)S(1)}, bf16[2,32,2048]{2,1,0:T(8,128)(2,1)S(1)}, u32[]{:S(2)}, u32[]{:S(2)}) collective-permute-start(bf16[2,32,2048]{2,1,0:T(8,128)(2,1)S(1)} %collective-permute-done.2), channel_id=1, source_target_pairs={{0,56},{4,60},{8,0},{12,4},{16,8},{20,12},{24,16},{28,20},{32,24},... | collective-permute-start | bytes 786440 | tf_op jit(solution)/shard_map/ppermute | solution.py:209
  49.3 5.1 %collective-permute-start.14 = (bf16[2,80,1024]{2,1,0:T(8,128)(2,1)S(1)}, bf16[2,80,1024]{2,1,0:T(8,128)(2,1)S(1)}, u32[]{:S(2)}, u32[]{:S(2)}) collective-permute-start(bf16[2,80,1024]{2,1,0:T(8,128)(2,1)S(1)} %collective-permute-done.12), channel_id=1, source_target_pairs={{0,56},{4,60},{8,0},{12,4},{16,8},{20,12},{24,16},{28,20},{32,24},... | collective-permute-start | bytes 983048 | tf_op jit(solution)/shard_map/ppermute | solution.py:209
  56.4 5.1 %collective-permute-start.6 = (bf16[2,32,2048]{2,1,0:T(8,128)(2,1)S(1)}, bf16[2,32,2048]{2,1,0:T(8,128)(2,1)S(1)}, u32[]{:S(2)}, u32[]{:S(2)}) collective-permute-start(bf16[2,32,2048]{2,1,0:T(8,128)(2,1)S(1)} %collective-permute-done.4), channel_id=1, source_target_pairs={{0,56},{4,60},{8,0},{12,4},{16,8},{20,12},{24,16},{28,20},{32,24},... | collective-permute-start | bytes 786440 | tf_op jit(solution)/shard_map/ppermute | solution.py:209
  65.0 5.1 %collective-permute-start.16 = (bf16[2,80,1024]{2,1,0:T(8,128)(2,1)S(1)}, bf16[2,80,1024]{2,1,0:T(8,128)(2,1)S(1)}, u32[]{:S(2)}, u32[]{:S(2)}) collective-permute-start(bf16[2,80,1024]{2,1,0:T(8,128)(2,1)S(1)} %collective-permute-done.14), channel_id=1, source_target_pairs={{0,56},{4,60},{8,0},{12,4},{16,8},{20,12},{24,16},{28,20},{32,24},... | collective-permute-start | bytes 983048 | tf_op jit(solution)/shard_map/ppermute | solution.py:209
  72.2 5.1 %collective-permute-start.8 = (bf16[1,32,2048]{2,1,0:T(8,128)(2,1)S(1)}, bf16[1,32,2048]{2,1,0:T(8,128)(2,1)S(1)}, u32[]{:S(2)}, u32[]{:S(2)}) collective-permute-start(bf16[1,32,2048]{2,1,0:T(8,128)(2,1)S(1)} %slice.70), channel_id=1, source_target_pairs={{0,56},{4,60},{8,0},{12,4},{16,8},{20,12},{24,16},{28,20},{32,24},... | collective-permute-start | bytes 393224 | tf_op jit(solution)/shard_map/ppermute | solution.py:209
  84.4 5.6 %collective-permute-start.18 = (bf16[1,80,1024]{2,1,0:T(8,128)(2,1)S(1)}, bf16[1,80,1024]{2,1,0:T(8,128)(2,1)S(1)}, u32[]{:S(2)}, u32[]{:S(2)}) collective-permute-start(bf16[1,80,1024]{2,1,0:T(8,128)(2,1)S(1)} %slice.72), channel_id=1, source_target_pairs={{0,56},{4,60},{8,0},{12,4},{16,8},{20,12},{24,16},{28,20},{32,24},... | collective-permute-start | bytes 491528 | tf_op jit(solution)/shard_map/ppermute | solution.py:209
  90.0 2.8 collective-permute-done.17
  97.4 5.2 %rank_partial.12 = bf16[4,128,1024]{2,1,0:T(8,128)(2,1)} custom-call(s32[5]{0:T(128)S(1)} %stack.46.meta_ref, bf16[128,2048]{1,0:T(8,128)(2,1)S(1)} %get-tuple-element.5.u_ref, bf16[16,32,2048]{2,1,0:T(8,128)(2,1)} %bitcast.24.mine_ref, bf16[16,32,2048]{2,1,0:T(8,128)(2,1)} %collective-permute-done.9.other_ref), custom_call_target="tpu_custom_call" | custom-call | flops 536870912 | bytes 4194304 | tf_op jit(solution)/shard_map/rank_partial/pallas_call | solution.py:60
  103.4 4.3 %all-to-all-start.4 = ((bf16[4,128,1024]{2,1,0:T(8,128)(2,1)}), bf16[4,128,1024]{2,1,0:T(8,128)(2,1)}, u32[]{:S(2)}, u32[]{:S(2)}) async-start(bf16[4,128,1024]{2,1,0:T(8,128)(2,1)} %rank_partial.12), calls=%async_computation.4 | async-start | bytes 2097152 | tf_op jit(solution)/shard_map/all_to_all | solution.py:292
  107.7 5.1 %rank_partial.8 = bf16[4,128,1024]{2,1,0:T(8,128)(2,1)} custom-call(s32[5]{0:T(128)S(1)} %stack.46.meta_ref, bf16[128,2048]{1,0:T(8,128)(2,1)S(1)} %get-tuple-element.4.u_ref, bf16[16,32,2048]{2,1,0:T(8,128)(2,1)} %bitcast.24.mine_ref, bf16[16,32,2048]{2,1,0:T(8,128)(2,1)} %collective-permute-done.9.other_ref), custom_call_target="tpu_custom_call" | custom-call | flops 536870912 | bytes 4194304 | tf_op jit(solution)/shard_map/rank_partial/pallas_call | solution.py:60
  112.8 11.0 %all-to-all-done.4.p_ref = bf16[4,128,1024]{2,1,0:T(8,128)(2,1)} async-done(((bf16[4,128,1024]{2,1,0:T(8,128)(2,1)}), bf16[4,128,1024]{2,1,0:T(8,128)(2,1)}, u32[]{:S(2)}, u32[]{:S(2)}) %all-to-all-start.4) | async-done | bytes 1048608 | tf_op jit(solution)/shard_map/all_to_all | solution.py:292
  123.8 4.3 %all-to-all-start = ((bf16[4,128,1024]{2,1,0:T(8,128)(2,1)}), bf16[4,128,1024]{2,1,0:T(8,128)(2,1)}, u32[]{:S(2)}, u32[]{:S(2)}) async-start(bf16[4,128,1024]{2,1,0:T(8,128)(2,1)} %rank_partial.8), calls=%async_computation | async-start | bytes 2097152 | tf_op jit(solution)/shard_map/all_to_all | solution.py:292
  128.1 3.8 sparse_product.12.s_ref
  133.1 4.5 %input_grad.12 = bf16[128,2048]{1,0:T(8,128)(2,1)S(1)} custom-call(s32[5]{0:T(128)S(1)} %stack.46.meta_ref, bf16[4,128,1024]{2,1,0:T(8,128)(2,1)} %all-to-all-done.4.p_ref, bf16[16,80,1024]{2,1,0:T(8,128)(2,1)S(1)} %bitcast.110, bf16[16,80,1024]{2,1,0:T(8,128)(2,1)} %collective-permute-done.19.other_ref, f32[128,2048]{1,0:T(8,128)S(1)} %copy-done.14), custom_call_target="tpu_custom_call" | custom-call | flops 536870912 | bytes 4194304 | tf_op jit(solution)/shard_map/input_grad/pallas_call | solution.py:140
  137.6 3.1 collective-permute-start.23
  140.7 12.2 %collective-permute-done.23.u_ref = bf16[128,2048]{1,0:T(8,128)(2,1)S(1)} collective-permute-done((bf16[128,2048]{1,0:T(8,128)(2,1)S(1)}, bf16[128,2048]{1,0:T(8,128)(2,1)S(1)}, u32[]{:S(2)}, u32[]{:S(2)}) %collective-permute-start.23) | collective-permute-done | bytes 524320 | tf_op jit(solution)/shard_map/ppermute | solution.py:255
  152.9 5.0 %rank_partial.13 = bf16[4,128,1024]{2,1,0:T(8,128)(2,1)} custom-call(s32[5]{0:T(128)S(1)} %stack.46.meta_ref, bf16[128,2048]{1,0:T(8,128)(2,1)S(1)} %collective-permute-done.23.u_ref, bf16[16,32,2048]{2,1,0:T(8,128)(2,1)} %bitcast.24.mine_ref, bf16[16,32,2048]{2,1,0:T(8,128)(2,1)} %collective-permute-done.9.other_ref), custom_call_target="tpu_custom_call" | custom-call | flops 536870912 | bytes 4194304 | tf_op jit(solution)/shard_map/rank_partial/pallas_call | solution.py:60
  157.9 4.4 %all-to-all-start.5 = ((bf16[4,128,1024]{2,1,0:T(8,128)(2,1)}), bf16[4,128,1024]{2,1,0:T(8,128)(2,1)}, u32[]{:S(2)}, u32[]{:S(2)}) async-start(bf16[4,128,1024]{2,1,0:T(8,128)(2,1)} %rank_partial.13), calls=%async_computation.5 | async-start | bytes 2097152 | tf_op jit(solution)/shard_map/all_to_all | solution.py:292
  163.4 3.8 sparse_product.8.s_ref
  168.4 4.5 %input_grad.8 = bf16[128,2048]{1,0:T(8,128)(2,1)S(1)} custom-call(s32[5]{0:T(128)S(1)} %stack.46.meta_ref, bf16[4,128,1024]{2,1,0:T(8,128)(2,1)} %all-to-all-done.p_ref, bf16[16,80,1024]{2,1,0:T(8,128)(2,1)S(1)} %bitcast.112, bf16[16,80,1024]{2,1,0:T(8,128)(2,1)} %collective-permute-done.19.other_ref, f32[128,2048]{1,0:T(8,128)S(1)} %copy-done.15), custom_call_target="tpu_custom_call" | custom-call | flops 536870912 | bytes 4194304 | tf_op jit(solution)/shard_map/input_grad/pallas_call | solution.py:140
  173.7 3.1 collective-permute-start.20
  176.8 11.1 %collective-permute-done.20.u_ref = bf16[128,2048]{1,0:T(8,128)(2,1)S(1)} collective-permute-done((bf16[128,2048]{1,0:T(8,128)(2,1)S(1)}, bf16[128,2048]{1,0:T(8,128)(2,1)S(1)}, u32[]{:S(2)}, u32[]{:S(2)}) %collective-permute-start.20) | collective-permute-done | bytes 524320 | tf_op jit(solution)/shard_map/ppermute | solution.py:255
  188.0 5.0 %rank_partial.9 = bf16[4,128,1024]{2,1,0:T(8,128)(2,1)} custom-call(s32[5]{0:T(128)S(1)} %stack.46.meta_ref, bf16[128,2048]{1,0:T(8,128)(2,1)S(1)} %collective-permute-done.20.u_ref, bf16[16,32,2048]{2,1,0:T(8,128)(2,1)} %bitcast.24.mine_ref, bf16[16,32,2048]{2,1,0:T(8,128)(2,1)} %collective-permute-done.9.other_ref), custom_call_target="tpu_custom_call" | custom-call | flops 536870912 | bytes 4194304 | tf_op jit(solution)/shard_map/rank_partial/pallas_call | solution.py:60
  193.8 4.4 %all-to-all-start.1 = ((bf16[4,128,1024]{2,1,0:T(8,128)(2,1)}), bf16[4,128,1024]{2,1,0:T(8,128)(2,1)}, u32[]{:S(2)}, u32[]{:S(2)}) async-start(bf16[4,128,1024]{2,1,0:T(8,128)(2,1)} %rank_partial.9), calls=%async_computation.1 | async-start | bytes 2097152 | tf_op jit(solution)/shard_map/all_to_all | solution.py:292
  198.3 3.8 sparse_product.13.s_ref
  203.3 4.5 %input_grad.13 = bf16[128,2048]{1,0:T(8,128)(2,1)S(1)} custom-call(s32[5]{0:T(128)S(1)} %stack.46.meta_ref, bf16[4,128,1024]{2,1,0:T(8,128)(2,1)} %all-to-all-done.5.p_ref, bf16[16,80,1024]{2,1,0:T(8,128)(2,1)S(1)} %bitcast.114, bf16[16,80,1024]{2,1,0:T(8,128)(2,1)} %collective-permute-done.19.other_ref, f32[128,2048]{1,0:T(8,128)S(1)} %copy-done.17), custom_call_target="tpu_custom_call" | custom-call | flops 536870912 | bytes 4194304 | tf_op jit(solution)/shard_map/input_grad/pallas_call | solution.py:140
  208.6 3.0 collective-permute-start.24
  211.6 10.2 %collective-permute-done.24.u_ref = bf16[128,2048]{1,0:T(8,128)(2,1)S(1)} collective-permute-done((bf16[128,2048]{1,0:T(8,128)(2,1)S(1)}, bf16[128,2048]{1,0:T(8,128)(2,1)S(1)}, u32[]{:S(2)}, u32[]{:S(2)}) %collective-permute-start.24) | collective-permute-done | bytes 524320 | tf_op jit(solution)/shard_map/ppermute | solution.py:255
  221.8 5.0 %rank_partial.14 = bf16[4,128,1024]{2,1,0:T(8,128)(2,1)} custom-call(s32[5]{0:T(128)S(1)} %stack.46.meta_ref, bf16[128,2048]{1,0:T(8,128)(2,1)S(1)} %collective-permute-done.24.u_ref, bf16[16,32,2048]{2,1,0:T(8,128)(2,1)} %bitcast.24.mine_ref, bf16[16,32,2048]{2,1,0:T(8,128)(2,1)} %collective-permute-done.9.other_ref), custom_call_target="tpu_custom_call" | custom-call | flops 536870912 | bytes 4194304 | tf_op jit(solution)/shard_map/rank_partial/pallas_call | solution.py:60
  227.6 4.4 %all-to-all-start.6 = ((bf16[4,128,1024]{2,1,0:T(8,128)(2,1)}), bf16[4,128,1024]{2,1,0:T(8,128)(2,1)}, u32[]{:S(2)}, u32[]{:S(2)}) async-start(bf16[4,128,1024]{2,1,0:T(8,128)(2,1)} %rank_partial.14), calls=%async_computation.6 | async-start | bytes 2097152 | tf_op jit(solution)/shard_map/all_to_all | solution.py:292
  233.1 3.8 sparse_product.9.s_ref
  238.2 4.5 %input_grad.9 = bf16[128,2048]{1,0:T(8,128)(2,1)S(1)} custom-call(s32[5]{0:T(128)S(1)} %stack.46.meta_ref, bf16[4,128,1024]{2,1,0:T(8,128)(2,1)} %all-to-all-done.1.p_ref, bf16[16,80,1024]{2,1,0:T(8,128)(2,1)S(1)} %bitcast.116, bf16[16,80,1024]{2,1,0:T(8,128)(2,1)} %collective-permute-done.19.other_ref, f32[128,2048]{1,0:T(8,128)S(1)} %copy-done.18), custom_call_target="tpu_custom_call" | custom-call | flops 536870912 | bytes 4194304 | tf_op jit(solution)/shard_map/input_grad/pallas_call | solution.py:140
  242.7 3.0 collective-permute-start.21
  245.8 9.2 %collective-permute-done.21.u_ref = bf16[128,2048]{1,0:T(8,128)(2,1)S(1)} collective-permute-done((bf16[128,2048]{1,0:T(8,128)(2,1)S(1)}, bf16[128,2048]{1,0:T(8,128)(2,1)S(1)}, u32[]{:S(2)}, u32[]{:S(2)}) %collective-permute-start.21) | collective-permute-done | bytes 524320 | tf_op jit(solution)/shard_map/ppermute | solution.py:255
  254.9 5.1 %rank_partial.10 = bf16[4,128,1024]{2,1,0:T(8,128)(2,1)} custom-call(s32[5]{0:T(128)S(1)} %stack.46.meta_ref, bf16[128,2048]{1,0:T(8,128)(2,1)S(1)} %collective-permute-done.21.u_ref, bf16[16,32,2048]{2,1,0:T(8,128)(2,1)} %bitcast.24.mine_ref, bf16[16,32,2048]{2,1,0:T(8,128)(2,1)} %collective-permute-done.9.other_ref), custom_call_target="tpu_custom_call" | custom-call | flops 536870912 | bytes 4194304 | tf_op jit(solution)/shard_map/rank_partial/pallas_call | solution.py:60
  260.9 4.4 %all-to-all-start.2 = ((bf16[4,128,1024]{2,1,0:T(8,128)(2,1)}), bf16[4,128,1024]{2,1,0:T(8,128)(2,1)}, u32[]{:S(2)}, u32[]{:S(2)}) async-start(bf16[4,128,1024]{2,1,0:T(8,128)(2,1)} %rank_partial.10), calls=%async_computation.2 | async-start | bytes 2097152 | tf_op jit(solution)/shard_map/all_to_all | solution.py:292
  266.4 3.8 sparse_product.14.s_ref
  270.2 3.9 sparse_product.10.s_ref
  274.1 5.2 %input_grad.14 = bf16[128,2048]{1,0:T(8,128)(2,1)} custom-call(s32[5]{0:T(128)S(1)} %stack.46.meta_ref, bf16[4,128,1024]{2,1,0:T(8,128)(2,1)} %all-to-all-done.6.p_ref, bf16[16,80,1024]{2,1,0:T(8,128)(2,1)S(1)} %bitcast.119, bf16[16,80,1024]{2,1,0:T(8,128)(2,1)} %collective-permute-done.19.other_ref, f32[128,2048]{1,0:T(8,128)S(1)} %copy-done.16), custom_call_target="tpu_custom_call" | custom-call | flops 536870912 | bytes 4194304 | tf_op jit(solution)/shard_map/input_grad/pallas_call | solution.py:140
  279.2 3.1 collective-permute-start.25
  283.5 5.2 %input_grad.10 = bf16[128,2048]{1,0:T(8,128)(2,1)} custom-call(s32[5]{0:T(128)S(1)} %stack.46.meta_ref, bf16[4,128,1024]{2,1,0:T(8,128)(2,1)} %all-to-all-done.2.p_ref, bf16[16,80,1024]{2,1,0:T(8,128)(2,1)S(1)} %bitcast.120, bf16[16,80,1024]{2,1,0:T(8,128)(2,1)} %collective-permute-done.19.other_ref, f32[128,2048]{1,0:T(8,128)S(1)} %copy-done.13), custom_call_target="tpu_custom_call" | custom-call | flops 536870912 | bytes 4194304 | tf_op jit(solution)/shard_map/input_grad/pallas_call | solution.py:140
  290.7 2.3 collective-permute-done.25.u_ref
  293.0 9.2 %collective-permute-done.22.u_ref = bf16[128,2048]{1,0:T(8,128)(2,1)} collective-permute-done((bf16[128,2048]{1,0:T(8,128)(2,1)}, bf16[128,2048]{1,0:T(8,128)(2,1)}, u32[]{:S(2)}, u32[]{:S(2)}) %collective-permute-start.22) | collective-permute-done | bytes 524320 | tf_op jit(solution)/shard_map/ppermute | solution.py:255
  304.2 3.1 block_products.1
  311.5 5.2 %rank_partial.15 = bf16[4,128,1024]{2,1,0:T(8,128)(2,1)} custom-call(s32[5]{0:T(128)S(1)} %stack.46.meta_ref, bf16[128,2048]{1,0:T(8,128)(2,1)} %collective-permute-done.25.u_ref, bf16[16,32,2048]{2,1,0:T(8,128)(2,1)} %bitcast.24.mine_ref, bf16[16,32,2048]{2,1,0:T(8,128)(2,1)} %collective-permute-done.9.other_ref), custom_call_target="tpu_custom_call" | custom-call | flops 536870912 | bytes 4194304 | tf_op jit(solution)/shard_map/rank_partial/pallas_call | solution.py:60
  316.6 4.5 %all-to-all-start.7 = ((bf16[4,128,1024]{2,1,0:T(8,128)(2,1)}), bf16[4,128,1024]{2,1,0:T(8,128)(2,1)}, u32[]{:S(2)}, u32[]{:S(2)}) async-start(bf16[4,128,1024]{2,1,0:T(8,128)(2,1)} %rank_partial.15), calls=%async_computation.7 | async-start | bytes 2097152 | tf_op jit(solution)/shard_map/all_to_all | solution.py:292
  323.5 4.0 %collective-permute-start.27 = (bf16[8,128,128]{2,1,0:T(8,128)(2,1)S(1)}, bf16[8,128,128]{2,1,0:T(8,128)(2,1)S(1)}, u32[]{:S(2)}, u32[]{:S(2)}) collective-permute-start(bf16[8,128,128]{2,1,0:T(8,128)(2,1)S(1)} %slice.102), channel_id=1, source_target_pairs={{0,8},{4,12},{8,0},{12,4},{16,24},{20,28},{24,16},{28,20},{32,40},... | collective-permute-start | bytes 786440 | tf_op jit(solution)/shard_map/ppermute | solution.py:212
  327.5 3.9 %sparse_product.15.s_ref = f32[128,2048]{1,0:T(8,128)} custom-call(s32[5]{0:T(128)S(1)} %stack.46.meta_ref, s32[128]{0:T(128)S(1)} %bitcast.133, s32[128]{0:T(128)S(1)} %bitcast.142, bf16[128,2048]{1,0:T(8,128)(2,1)} %collective-permute-done.25.u_ref, bf16[16,80,1024]{2,1,0:T(8,128)(2,1)S(1)} %bitcast.121, ...), custom_call_target="tpu_custom_call" | custom-call | flops 536870912 | bytes 4194304 | tf_op jit(solution)/shard_map/sparse_product/pallas_call | solution.py:107
  331.4 5.2 %rank_partial.11 = bf16[4,128,1024]{2,1,0:T(8,128)(2,1)} custom-call(s32[5]{0:T(128)S(1)} %stack.46.meta_ref, bf16[128,2048]{1,0:T(8,128)(2,1)} %collective-permute-done.22.u_ref, bf16[16,32,2048]{2,1,0:T(8,128)(2,1)} %bitcast.24.mine_ref, bf16[16,32,2048]{2,1,0:T(8,128)(2,1)} %collective-permute-done.9.other_ref), custom_call_target="tpu_custom_call" | custom-call | flops 536870912 | bytes 4194304 | tf_op jit(solution)/shard_map/rank_partial/pallas_call | solution.py:60
  336.6 3.9 %sparse_product.11.s_ref = f32[128,2048]{1,0:T(8,128)} custom-call(s32[5]{0:T(128)S(1)} %stack.46.meta_ref, s32[128]{0:T(128)S(1)} %bitcast.134, s32[128]{0:T(128)S(1)} %bitcast.143, bf16[128,2048]{1,0:T(8,128)(2,1)} %collective-permute-done.22.u_ref, bf16[16,80,1024]{2,1,0:T(8,128)(2,1)S(1)} %bitcast.122, ...), custom_call_target="tpu_custom_call" | custom-call | flops 536870912 | bytes 4194304 | tf_op jit(solution)/shard_map/sparse_product/pallas_call | solution.py:107
  340.5 4.8 %all-to-all-start.3 = ((bf16[4,128,1024]{2,1,0:T(8,128)(2,1)}), bf16[4,128,1024]{2,1,0:T(8,128)(2,1)}, u32[]{:S(2)}, u32[]{:S(2)}) async-start(bf16[4,128,1024]{2,1,0:T(8,128)(2,1)} %rank_partial.11), calls=%async_computation.3 | async-start | bytes 2097152 | tf_op jit(solution)/shard_map/all_to_all | solution.py:292
  347.3 4.8 %collective-permute-start.28 = (bf16[4,128,128]{2,1,0:T(8,128)(2,1)S(1)}, bf16[4,128,128]{2,1,0:T(8,128)(2,1)S(1)}, u32[]{:S(2)}, u32[]{:S(2)}) collective-permute-start(bf16[4,128,128]{2,1,0:T(8,128)(2,1)S(1)} %slice.103), channel_id=1, source_target_pairs={{0,16},{4,20},{8,24},{12,28},{16,0},{20,4},{24,8},{28,12},{32,48},... | collective-permute-start | bytes 393224 | tf_op jit(solution)/shard_map/ppermute | solution.py:212
  352.1 4.5 %input_grad.15 = bf16[128,2048]{1,0:T(8,128)(2,1)S(1)} custom-call(s32[5]{0:T(128)S(1)} %stack.46.meta_ref, bf16[4,128,1024]{2,1,0:T(8,128)(2,1)} %all-to-all-done.7.p_ref, bf16[16,80,1024]{2,1,0:T(8,128)(2,1)S(1)} %bitcast.123, bf16[16,80,1024]{2,1,0:T(8,128)(2,1)} %collective-permute-done.19.other_ref, f32[128,2048]{1,0:T(8,128)S(1)} %copy-done.12), custom_call_target="tpu_custom_call" | custom-call | flops 536870912 | bytes 4194304 | tf_op jit(solution)/shard_map/input_grad/pallas_call | solution.py:140
  357.9 2.5 all-to-all-done.3.p_ref
  361.6 4.6 %input_grad.11 = bf16[128,2048]{1,0:T(8,128)(2,1)S(1)} custom-call(s32[5]{0:T(128)S(1)} %stack.46.meta_ref, bf16[4,128,1024]{2,1,0:T(8,128)(2,1)} %all-to-all-done.3.p_ref, bf16[16,80,1024]{2,1,0:T(8,128)(2,1)S(1)} %bitcast.124, bf16[16,80,1024]{2,1,0:T(8,128)(2,1)} %collective-permute-done.19.other_ref, f32[128,2048]{1,0:T(8,128)S(1)} %copy-done.11), custom_call_target="tpu_custom_call" | custom-call | flops 536870912 | bytes 4194304 | tf_op jit(solution)/shard_map/input_grad/pallas_call | solution.py:140
  366.3 4.7 %collective-permute-start.29 = (bf16[2,128,128]{2,1,0:T(8,128)(2,1)S(1)}, bf16[2,128,128]{2,1,0:T(8,128)(2,1)S(1)}, u32[]{:S(2)}, u32[]{:S(2)}) collective-permute-start(bf16[2,128,128]{2,1,0:T(8,128)(2,1)S(1)} %slice.104), channel_id=1, source_target_pairs={{0,32},{4,36},{8,40},{12,44},{16,48},{20,52},{24,56},{28,60},{32,0... | collective-permute-start | bytes 196616 | tf_op jit(solution)/shard_map/ppermute | solution.py:212
  372.2 4.9 %collective-permute-done.29 = bf16[2,128,128]{2,1,0:T(8,128)(2,1)S(1)} collective-permute-done((bf16[2,128,128]{2,1,0:T(8,128)(2,1)S(1)}, bf16[2,128,128]{2,1,0:T(8,128)(2,1)S(1)}, u32[]{:S(2)}, u32[]{:S(2)}) %collective-permute-start.29) | collective-permute-done | bytes 65568 | tf_op jit(solution)/shard_map/ppermute | solution.py:212
  380.2 6.6 %collective-permute-done.30 = bf16[1,128,128]{2,1,0:T(8,128)(2,1)S(1)} collective-permute-done((bf16[1,128,128]{2,1,0:T(8,128)(2,1)S(1)}, bf16[1,128,128]{2,1,0:T(8,128)(2,1)S(1)}, u32[]{:S(2)}, u32[]{:S(2)}) %collective-permute-start.30) | collective-permute-done | bytes 32800 | tf_op jit(solution)/shard_map/ppermute | solution.py:212
  (153 shorter events, 65.5 us)
Async XLA Ops:
  0.6 14.5 %collective-permute-start = (bf16[32,2048]{1,0:T(8,128)(2,1)}, bf16[32,2048]{1,0:T(8,128)(2,1)S(1)}, u32[]{:S(2)}, u32[]{:S(2)}) collective-permute-start(bf16[32,2048]{1,0:T(8,128)(2,1)} %bitcast.148), channel_id=1, source_target_pairs={{0,64},{4,68},{8,72},{12,76},{16,80},{20,84},{24,88},{28,92},{32,9... | collective-permute-start | bytes 393224 | tf_op jit(solution)/shard_map/ppermute | solution.py:212
  3.6 27.7 %copy-start.33 = (bf16[1,64,1024]{2,1,0:T(8,128)(2,1)S(1)}, bf16[1,64,1024]{2,1,0:T(8,128)(2,1)}, u32[]{:S(2)}) copy-start(bf16[1,64,1024]{2,1,0:T(8,128)(2,1)} %param.10) | copy-start | bytes 393220
  5.3 26.0 %collective-permute-start.10 = (bf16[80,1024]{1,0:T(8,128)(2,1)S(1)}, bf16[80,1024]{1,0:T(8,128)(2,1)S(1)}, u32[]{:S(2)}, u32[]{:S(2)}) collective-permute-start(bf16[80,1024]{1,0:T(8,128)(2,1)S(1)} %pad_maximum_fusion.2), channel_id=1, source_target_pairs={{0,64},{4,68},{8,72},{12,76},{16,80},{20,84},{24,88},{28,92},{32,9... | collective-permute-start | bytes 491528 | tf_op jit(solution)/shard_map/ppermute | solution.py:212
  16.1 22.7 %collective-permute-start.1 = (bf16[2,32,2048]{2,1,0:T(8,128)(2,1)S(1)}, bf16[2,32,2048]{2,1,0:T(8,128)(2,1)S(1)}, u32[]{:S(2)}, u32[]{:S(2)}) collective-permute-start(bf16[2,32,2048]{2,1,0:T(8,128)(2,1)S(1)} %pad_maximum_fusion.1), channel_id=1, source_target_pairs={{0,8},{4,12},{8,16},{12,20},{16,24},{20,28},{24,32},{28,36},{32,40... | collective-permute-start | bytes 786440 | tf_op jit(solution)/shard_map/ppermute | solution.py:209
  20.4 20.4 %collective-permute-start.2 = (bf16[2,32,2048]{2,1,0:T(8,128)(2,1)S(1)}, bf16[2,32,2048]{2,1,0:T(8,128)(2,1)S(1)}, u32[]{:S(2)}, u32[]{:S(2)}) collective-permute-start(bf16[2,32,2048]{2,1,0:T(8,128)(2,1)S(1)} %pad_maximum_fusion.1), channel_id=1, source_target_pairs={{0,56},{4,60},{8,0},{12,4},{16,8},{20,12},{24,16},{28,20},{32,24},... | collective-permute-start | bytes 786440 | tf_op jit(solution)/shard_map/ppermute | solution.py:209
  31.4 16.0 %collective-permute-start.11 = (bf16[2,80,1024]{2,1,0:T(8,128)(2,1)S(1)}, bf16[2,80,1024]{2,1,0:T(8,128)(2,1)S(1)}, u32[]{:S(2)}, u32[]{:S(2)}) collective-permute-start(bf16[2,80,1024]{2,1,0:T(8,128)(2,1)S(1)} %pad_maximum_fusion), channel_id=1, source_target_pairs={{0,8},{4,12},{8,16},{12,20},{16,24},{20,28},{24,32},{28,36},{32,40... | collective-permute-start | bytes 983048 | tf_op jit(solution)/shard_map/ppermute | solution.py:209
  33.3 16.0 %collective-permute-start.12 = (bf16[2,80,1024]{2,1,0:T(8,128)(2,1)S(1)}, bf16[2,80,1024]{2,1,0:T(8,128)(2,1)S(1)}, u32[]{:S(2)}, u32[]{:S(2)}) collective-permute-start(bf16[2,80,1024]{2,1,0:T(8,128)(2,1)S(1)} %pad_maximum_fusion), channel_id=1, source_target_pairs={{0,56},{4,60},{8,0},{12,4},{16,8},{20,12},{24,16},{28,20},{32,24},... | collective-permute-start | bytes 983048 | tf_op jit(solution)/shard_map/ppermute | solution.py:209
  38.8 15.7 %collective-permute-start.3 = (bf16[2,32,2048]{2,1,0:T(8,128)(2,1)S(1)}, bf16[2,32,2048]{2,1,0:T(8,128)(2,1)S(1)}, u32[]{:S(2)}, u32[]{:S(2)}) collective-permute-start(bf16[2,32,2048]{2,1,0:T(8,128)(2,1)S(1)} %collective-permute-done.1), channel_id=1, source_target_pairs={{0,8},{4,12},{8,16},{12,20},{16,24},{20,28},{24,32},{28,36},{32,40... | collective-permute-start | bytes 786440 | tf_op jit(solution)/shard_map/ppermute | solution.py:209
  40.8 15.7 %collective-permute-start.4 = (bf16[2,32,2048]{2,1,0:T(8,128)(2,1)S(1)}, bf16[2,32,2048]{2,1,0:T(8,128)(2,1)S(1)}, u32[]{:S(2)}, u32[]{:S(2)}) collective-permute-start(bf16[2,32,2048]{2,1,0:T(8,128)(2,1)S(1)} %collective-permute-done.2), channel_id=1, source_target_pairs={{0,56},{4,60},{8,0},{12,4},{16,8},{20,12},{24,16},{28,20},{32,24},... | collective-permute-start | bytes 786440 | tf_op jit(solution)/shard_map/ppermute | solution.py:209
  47.4 15.7 %collective-permute-start.13 = (bf16[2,80,1024]{2,1,0:T(8,128)(2,1)S(1)}, bf16[2,80,1024]{2,1,0:T(8,128)(2,1)S(1)}, u32[]{:S(2)}, u32[]{:S(2)}) collective-permute-start(bf16[2,80,1024]{2,1,0:T(8,128)(2,1)S(1)} %collective-permute-done.11), channel_id=1, source_target_pairs={{0,8},{4,12},{8,16},{12,20},{16,24},{20,28},{24,32},{28,36},{32,40... | collective-permute-start | bytes 983048 | tf_op jit(solution)/shard_map/ppermute | solution.py:209
  49.3 15.7 %collective-permute-start.14 = (bf16[2,80,1024]{2,1,0:T(8,128)(2,1)S(1)}, bf16[2,80,1024]{2,1,0:T(8,128)(2,1)S(1)}, u32[]{:S(2)}, u32[]{:S(2)}) collective-permute-start(bf16[2,80,1024]{2,1,0:T(8,128)(2,1)S(1)} %collective-permute-done.12), channel_id=1, source_target_pairs={{0,56},{4,60},{8,0},{12,4},{16,8},{20,12},{24,16},{28,20},{32,24},... | collective-permute-start | bytes 983048 | tf_op jit(solution)/shard_map/ppermute | solution.py:209
  54.5 15.7 %collective-permute-start.5 = (bf16[2,32,2048]{2,1,0:T(8,128)(2,1)S(1)}, bf16[2,32,2048]{2,1,0:T(8,128)(2,1)S(1)}, u32[]{:S(2)}, u32[]{:S(2)}) collective-permute-start(bf16[2,32,2048]{2,1,0:T(8,128)(2,1)S(1)} %collective-permute-done.3), channel_id=1, source_target_pairs={{0,8},{4,12},{8,16},{12,20},{16,24},{20,28},{24,32},{28,36},{32,40... | collective-permute-start | bytes 786440 | tf_op jit(solution)/shard_map/ppermute | solution.py:209
  56.4 15.7 %collective-permute-start.6 = (bf16[2,32,2048]{2,1,0:T(8,128)(2,1)S(1)}, bf16[2,32,2048]{2,1,0:T(8,128)(2,1)S(1)}, u32[]{:S(2)}, u32[]{:S(2)}) collective-permute-start(bf16[2,32,2048]{2,1,0:T(8,128)(2,1)S(1)} %collective-permute-done.4), channel_id=1, source_target_pairs={{0,56},{4,60},{8,0},{12,4},{16,8},{20,12},{24,16},{28,20},{32,24},... | collective-permute-start | bytes 786440 | tf_op jit(solution)/shard_map/ppermute | solution.py:209
  63.0 19.4 %collective-permute-start.15 = (bf16[2,80,1024]{2,1,0:T(8,128)(2,1)S(1)}, bf16[2,80,1024]{2,1,0:T(8,128)(2,1)S(1)}, u32[]{:S(2)}, u32[]{:S(2)}) collective-permute-start(bf16[2,80,1024]{2,1,0:T(8,128)(2,1)S(1)} %collective-permute-done.13), channel_id=1, source_target_pairs={{0,8},{4,12},{8,16},{12,20},{16,24},{20,28},{24,32},{28,36},{32,40... | collective-permute-start | bytes 983048 | tf_op jit(solution)/shard_map/ppermute | solution.py:209
  65.0 19.3 %collective-permute-start.16 = (bf16[2,80,1024]{2,1,0:T(8,128)(2,1)S(1)}, bf16[2,80,1024]{2,1,0:T(8,128)(2,1)S(1)}, u32[]{:S(2)}, u32[]{:S(2)}) collective-permute-start(bf16[2,80,1024]{2,1,0:T(8,128)(2,1)S(1)} %collective-permute-done.14), channel_id=1, source_target_pairs={{0,56},{4,60},{8,0},{12,4},{16,8},{20,12},{24,16},{28,20},{32,24},... | collective-permute-start | bytes 983048 | tf_op jit(solution)/shard_map/ppermute | solution.py:209
  70.2 8.6 %collective-permute-start.7 = (bf16[1,32,2048]{2,1,0:T(8,128)(2,1)S(1)}, bf16[1,32,2048]{2,1,0:T(8,128)(2,1)S(1)}, u32[]{:S(2)}, u32[]{:S(2)}) collective-permute-start(bf16[1,32,2048]{2,1,0:T(8,128)(2,1)S(1)} %slice.69), channel_id=1, source_target_pairs={{0,8},{4,12},{8,16},{12,20},{16,24},{20,28},{24,32},{28,36},{32,40... | collective-permute-start | bytes 393224 | tf_op jit(solution)/shard_map/ppermute | solution.py:209
  72.2 7.6 %collective-permute-start.8 = (bf16[1,32,2048]{2,1,0:T(8,128)(2,1)S(1)}, bf16[1,32,2048]{2,1,0:T(8,128)(2,1)S(1)}, u32[]{:S(2)}, u32[]{:S(2)}) collective-permute-start(bf16[1,32,2048]{2,1,0:T(8,128)(2,1)S(1)} %slice.70), channel_id=1, source_target_pairs={{0,56},{4,60},{8,0},{12,4},{16,8},{20,12},{24,16},{28,20},{32,24},... | collective-permute-start | bytes 393224 | tf_op jit(solution)/shard_map/ppermute | solution.py:209
  80.5 16.9 %collective-permute-start.9 = (bf16[16,32,2048]{2,1,0:T(8,128)(2,1)}, bf16[16,32,2048]{2,1,0:T(8,128)(2,1)}, u32[]{:S(2)}, u32[]{:S(2)}) collective-permute-start(bf16[16,32,2048]{2,1,0:T(8,128)(2,1)} %bitcast.24.mine_ref), channel_id=1, source_target_pairs={{0,4},{4,0},{8,12},{12,8},{16,20},{20,16},{24,28},{28,24},{32,36},... | collective-permute-start | bytes 6291464 | tf_op jit(solution)/shard_map/ppermute | solution.py:212
  82.4 10.4 %collective-permute-start.17 = (bf16[1,80,1024]{2,1,0:T(8,128)(2,1)S(1)}, bf16[1,80,1024]{2,1,0:T(8,128)(2,1)S(1)}, u32[]{:S(2)}, u32[]{:S(2)}) collective-permute-start(bf16[1,80,1024]{2,1,0:T(8,128)(2,1)S(1)} %slice.71), channel_id=1, source_target_pairs={{0,8},{4,12},{8,16},{12,20},{16,24},{20,28},{24,32},{28,36},{32,40... | collective-permute-start | bytes 491528 | tf_op jit(solution)/shard_map/ppermute | solution.py:209
  84.4 9.7 %collective-permute-start.18 = (bf16[1,80,1024]{2,1,0:T(8,128)(2,1)S(1)}, bf16[1,80,1024]{2,1,0:T(8,128)(2,1)S(1)}, u32[]{:S(2)}, u32[]{:S(2)}) collective-permute-start(bf16[1,80,1024]{2,1,0:T(8,128)(2,1)S(1)} %slice.72), channel_id=1, source_target_pairs={{0,56},{4,60},{8,0},{12,4},{16,8},{20,12},{24,16},{28,20},{32,24},... | collective-permute-start | bytes 491528 | tf_op jit(solution)/shard_map/ppermute | solution.py:209
  94.1 34.0 %collective-permute-start.19 = (bf16[16,80,1024]{2,1,0:T(8,128)(2,1)S(1)}, bf16[16,80,1024]{2,1,0:T(8,128)(2,1)}, u32[]{:S(2)}, u32[]{:S(2)}) collective-permute-start(bf16[16,80,1024]{2,1,0:T(8,128)(2,1)S(1)} %bitcast.108), channel_id=1, source_target_pairs={{0,4},{4,0},{8,12},{12,8},{16,20},{20,16},{24,28},{28,24},{32,36},... | collective-permute-start | bytes 7864328 | tf_op jit(solution)/shard_map/ppermute | solution.py:212
  97.4 10.3 %copy-start.7 = (bf16[128,2048]{1,0:T(8,128)(2,1)}, bf16[128,2048]{1,0:T(8,128)(2,1)S(1)}, u32[]{:S(2)}) copy-start(bf16[128,2048]{1,0:T(8,128)(2,1)S(1)} %get-tuple-element.4.u_ref) | copy-start | bytes 1572868
  103.4 20.4 %all-to-all-start.4 = ((bf16[4,128,1024]{2,1,0:T(8,128)(2,1)}), bf16[4,128,1024]{2,1,0:T(8,128)(2,1)}, u32[]{:S(2)}, u32[]{:S(2)}) async-start(bf16[4,128,1024]{2,1,0:T(8,128)(2,1)} %rank_partial.12), calls=%async_computation.4 | async-start | bytes 2097152 | tf_op jit(solution)/shard_map/all_to_all | solution.py:292
  112.8 15.2 %copy-start.10 = (bf16[128,2048]{1,0:T(8,128)(2,1)S(1)}, bf16[128,2048]{1,0:T(8,128)(2,1)}, u32[]{:S(2)}) copy-start(bf16[128,2048]{1,0:T(8,128)(2,1)} %copy-done.9) | copy-start | bytes 1572868
  112.8 15.3 %copy-start.28 = (s32[1,128]{1,0:T(1,128)S(1)}, s32[1,128]{1,0:T(1,128)}, u32[]{:S(2)}) copy-start(s32[1,128]{1,0:T(1,128)} %param.12) | copy-start | bytes 1540
  112.8 15.3 %copy-start.29 = (s32[1,128]{1,0:T(1,128)S(1)}, s32[1,128]{1,0:T(1,128)}, u32[]{:S(2)}) copy-start(s32[1,128]{1,0:T(1,128)} %param.13) | copy-start | bytes 1540
  123.8 34.1 %all-to-all-start = ((bf16[4,128,1024]{2,1,0:T(8,128)(2,1)}), bf16[4,128,1024]{2,1,0:T(8,128)(2,1)}, u32[]{:S(2)}, u32[]{:S(2)}) async-start(bf16[4,128,1024]{2,1,0:T(8,128)(2,1)} %rank_partial.8), calls=%async_computation | async-start | bytes 2097152 | tf_op jit(solution)/shard_map/all_to_all | solution.py:292
  131.9 1.2 copy-start.14
  137.6 15.3 %copy-start.21 = (bf16[128,2048]{1,0:T(8,128)(2,1)}, bf16[128,2048]{1,0:T(8,128)(2,1)S(1)}, u32[]{:S(2)}) copy-start(bf16[128,2048]{1,0:T(8,128)(2,1)S(1)} %input_grad.12) | copy-start | bytes 1572868
  137.6 15.3 %collective-permute-start.23 = (bf16[128,2048]{1,0:T(8,128)(2,1)S(1)}, bf16[128,2048]{1,0:T(8,128)(2,1)S(1)}, u32[]{:S(2)}, u32[]{:S(2)}) collective-permute-start(bf16[128,2048]{1,0:T(8,128)(2,1)S(1)} %input_grad.12), channel_id=1, source_target_pairs={{128,0},{256,128},{384,256},{129,1},{257,129},{385,257},{130,2},{2... | collective-permute-start | bytes 1572872 | tf_op jit(solution)/shard_map/ppermute | solution.py:255
  157.9 35.9 %all-to-all-start.5 = ((bf16[4,128,1024]{2,1,0:T(8,128)(2,1)}), bf16[4,128,1024]{2,1,0:T(8,128)(2,1)}, u32[]{:S(2)}, u32[]{:S(2)}) async-start(bf16[4,128,1024]{2,1,0:T(8,128)(2,1)} %rank_partial.13), calls=%async_computation.5 | async-start | bytes 2097152 | tf_op jit(solution)/shard_map/all_to_all | solution.py:292
  162.3 1.0 copy-start.8
  167.1 1.2 copy-start.15
  173.7 14.3 %collective-permute-start.20 = (bf16[128,2048]{1,0:T(8,128)(2,1)S(1)}, bf16[128,2048]{1,0:T(8,128)(2,1)S(1)}, u32[]{:S(2)}, u32[]{:S(2)}) collective-permute-start(bf16[128,2048]{1,0:T(8,128)(2,1)S(1)} %input_grad.8), channel_id=1, source_target_pairs={{128,0},{256,128},{384,256},{129,1},{257,129},{385,257},{130,2},{2... | collective-permute-start | bytes 1572872 | tf_op jit(solution)/shard_map/ppermute | solution.py:255
  193.8 33.8 %all-to-all-start.1 = ((bf16[4,128,1024]{2,1,0:T(8,128)(2,1)}), bf16[4,128,1024]{2,1,0:T(8,128)(2,1)}, u32[]{:S(2)}, u32[]{:S(2)}) async-start(bf16[4,128,1024]{2,1,0:T(8,128)(2,1)} %rank_partial.9), calls=%async_computation.1 | async-start | bytes 2097152 | tf_op jit(solution)/shard_map/all_to_all | solution.py:292
  202.0 1.2 copy-start.17
  208.6 13.2 %collective-permute-start.24 = (bf16[128,2048]{1,0:T(8,128)(2,1)S(1)}, bf16[128,2048]{1,0:T(8,128)(2,1)S(1)}, u32[]{:S(2)}, u32[]{:S(2)}) collective-permute-start(bf16[128,2048]{1,0:T(8,128)(2,1)S(1)} %input_grad.13), channel_id=1, source_target_pairs={{128,0},{256,128},{384,256},{129,1},{257,129},{385,257},{130,2},{2... | collective-permute-start | bytes 1572872 | tf_op jit(solution)/shard_map/ppermute | solution.py:255
  227.6 33.2 %all-to-all-start.6 = ((bf16[4,128,1024]{2,1,0:T(8,128)(2,1)}), bf16[4,128,1024]{2,1,0:T(8,128)(2,1)}, u32[]{:S(2)}, u32[]{:S(2)}) async-start(bf16[4,128,1024]{2,1,0:T(8,128)(2,1)} %rank_partial.14), calls=%async_computation.6 | async-start | bytes 2097152 | tf_op jit(solution)/shard_map/all_to_all | solution.py:292
  232.1 1.0 copy-start.2
  236.9 1.2 copy-start.18
  242.7 12.2 %copy-start.23 = (bf16[128,2048]{1,0:T(8,128)(2,1)}, bf16[128,2048]{1,0:T(8,128)(2,1)S(1)}, u32[]{:S(2)}) copy-start(bf16[128,2048]{1,0:T(8,128)(2,1)S(1)} %input_grad.9) | copy-start | bytes 1572868
  242.7 12.2 %collective-permute-start.21 = (bf16[128,2048]{1,0:T(8,128)(2,1)S(1)}, bf16[128,2048]{1,0:T(8,128)(2,1)S(1)}, u32[]{:S(2)}, u32[]{:S(2)}) collective-permute-start(bf16[128,2048]{1,0:T(8,128)(2,1)S(1)} %input_grad.9), channel_id=1, source_target_pairs={{128,0},{256,128},{384,256},{129,1},{257,129},{385,257},{130,2},{2... | collective-permute-start | bytes 1572872 | tf_op jit(solution)/shard_map/ppermute | solution.py:255
  260.9 21.4 %all-to-all-start.2 = ((bf16[4,128,1024]{2,1,0:T(8,128)(2,1)}), bf16[4,128,1024]{2,1,0:T(8,128)(2,1)}, u32[]{:S(2)}, u32[]{:S(2)}) async-start(bf16[4,128,1024]{2,1,0:T(8,128)(2,1)} %rank_partial.10), calls=%async_computation.2 | async-start | bytes 2097152 | tf_op jit(solution)/shard_map/all_to_all | solution.py:292
  266.4 3.8 copy-start.6
  270.2 3.9 copy-start.16
  279.2 13.7 %collective-permute-start.25 = (bf16[128,2048]{1,0:T(8,128)(2,1)}, bf16[128,2048]{1,0:T(8,128)(2,1)}, u32[]{:S(2)}, u32[]{:S(2)}) collective-permute-start(bf16[128,2048]{1,0:T(8,128)(2,1)} %input_grad.14), channel_id=1, source_target_pairs={{128,0},{256,128},{384,256},{129,1},{257,129},{385,257},{130,2},{2... | collective-permute-start | bytes 1572872 | tf_op jit(solution)/shard_map/ppermute | solution.py:255
  282.3 1.2 copy-start.13
  288.7 13.5 %collective-permute-start.22 = (bf16[128,2048]{1,0:T(8,128)(2,1)}, bf16[128,2048]{1,0:T(8,128)(2,1)}, u32[]{:S(2)}, u32[]{:S(2)}) collective-permute-start(bf16[128,2048]{1,0:T(8,128)(2,1)} %input_grad.10), channel_id=1, source_target_pairs={{128,0},{256,128},{384,256},{129,1},{257,129},{385,257},{130,2},{2... | collective-permute-start | bytes 1572872 | tf_op jit(solution)/shard_map/ppermute | solution.py:255
  290.7 13.5 %copy-start.27 = (bf16[1,2,128,2048]{3,2,1,0:T(8,128)(2,1)S(1)}, bf16[1,2,128,2048]{3,2,1,0:T(8,128)(2,1)}, u32[]{:S(2)}) copy-start(bf16[1,2,128,2048]{3,2,1,0:T(8,128)(2,1)} %param.8) | copy-start | bytes 3145732
  307.3 1.3 copy-start
  309.5 11.6 %collective-permute-start.26 = (bf16[16,128,128]{2,1,0:T(8,128)(2,1)}, bf16[16,128,128]{2,1,0:T(8,128)(2,1)S(1)}, u32[]{:S(2)}, u32[]{:S(2)}) collective-permute-start(bf16[16,128,128]{2,1,0:T(8,128)(2,1)} %slice.101), channel_id=1, source_target_pairs={{0,4},{4,0},{8,12},{12,8},{16,20},{20,16},{24,28},{28,24},{32,36},... | collective-permute-start | bytes 1572872 | tf_op jit(solution)/shard_map/ppermute | solution.py:212
  316.6 23.9 %all-to-all-start.7 = ((bf16[4,128,1024]{2,1,0:T(8,128)(2,1)}), bf16[4,128,1024]{2,1,0:T(8,128)(2,1)}, u32[]{:S(2)}, u32[]{:S(2)}) async-start(bf16[4,128,1024]{2,1,0:T(8,128)(2,1)} %rank_partial.15), calls=%async_computation.7 | async-start | bytes 2097152 | tf_op jit(solution)/shard_map/all_to_all | solution.py:292
  323.5 21.8 %collective-permute-start.27 = (bf16[8,128,128]{2,1,0:T(8,128)(2,1)S(1)}, bf16[8,128,128]{2,1,0:T(8,128)(2,1)S(1)}, u32[]{:S(2)}, u32[]{:S(2)}) collective-permute-start(bf16[8,128,128]{2,1,0:T(8,128)(2,1)S(1)} %slice.102), channel_id=1, source_target_pairs={{0,8},{4,12},{8,0},{12,4},{16,24},{20,28},{24,16},{28,20},{32,40},... | collective-permute-start | bytes 786440 | tf_op jit(solution)/shard_map/ppermute | solution.py:212
  340.5 19.9 %all-to-all-start.3 = ((bf16[4,128,1024]{2,1,0:T(8,128)(2,1)}), bf16[4,128,1024]{2,1,0:T(8,128)(2,1)}, u32[]{:S(2)}, u32[]{:S(2)}) async-start(bf16[4,128,1024]{2,1,0:T(8,128)(2,1)} %rank_partial.11), calls=%async_computation.3 | async-start | bytes 2097152 | tf_op jit(solution)/shard_map/all_to_all | solution.py:292
  345.3 6.8 %copy-start.12 = (f32[128,2048]{1,0:T(8,128)S(1)}, f32[128,2048]{1,0:T(8,128)}, u32[]{:S(2)}) copy-start(f32[128,2048]{1,0:T(8,128)} %sparse_product.15.s_ref) | copy-start | bytes 3145732
  347.3 9.4 %copy-start.22 = (bf16[128,2048]{1,0:T(8,128)(2,1)S(1)}, bf16[128,2048]{1,0:T(8,128)(2,1)}, u32[]{:S(2)}) copy-start(bf16[128,2048]{1,0:T(8,128)(2,1)} %copy-done.21) | copy-start | bytes 1572868
  347.3 9.4 %copy-start.26 = (bf16[128,2048]{1,0:T(8,128)(2,1)S(1)}, bf16[128,2048]{1,0:T(8,128)(2,1)}, u32[]{:S(2)}) copy-start(bf16[128,2048]{1,0:T(8,128)(2,1)} %copy-done.25) | copy-start | bytes 1572868
  347.3 19.0 %collective-permute-start.28 = (bf16[4,128,128]{2,1,0:T(8,128)(2,1)S(1)}, bf16[4,128,128]{2,1,0:T(8,128)(2,1)S(1)}, u32[]{:S(2)}, u32[]{:S(2)}) collective-permute-start(bf16[4,128,128]{2,1,0:T(8,128)(2,1)S(1)} %slice.103), channel_id=1, source_target_pairs={{0,16},{4,20},{8,24},{12,28},{16,0},{20,4},{24,8},{28,12},{32,48},... | collective-permute-start | bytes 393224 | tf_op jit(solution)/shard_map/ppermute | solution.py:212
  360.4 1.2 copy-start.11
  361.6 4.6 %copy-start.32 = (f32[8,128,128]{2,1,0:T(8,128)S(1)}, f32[8,128,128]{2,1,0:T(8,128)}, u32[]{:S(2)}) copy-start(f32[8,128,128]{2,1,0:T(8,128)} %copy-done.31) | copy-start | bytes 1572868
  361.6 9.4 %copy-start.20 = (bf16[128,2048]{1,0:T(8,128)(2,1)S(1)}, bf16[128,2048]{1,0:T(8,128)(2,1)}, u32[]{:S(2)}) copy-start(bf16[128,2048]{1,0:T(8,128)(2,1)} %copy-done.19) | copy-start | bytes 1572868
  361.6 9.4 %copy-start.24 = (bf16[128,2048]{1,0:T(8,128)(2,1)S(1)}, bf16[128,2048]{1,0:T(8,128)(2,1)}, u32[]{:S(2)}) copy-start(bf16[128,2048]{1,0:T(8,128)(2,1)} %copy-done.23) | copy-start | bytes 1572868
  366.3 10.8 %collective-permute-start.29 = (bf16[2,128,128]{2,1,0:T(8,128)(2,1)S(1)}, bf16[2,128,128]{2,1,0:T(8,128)(2,1)S(1)}, u32[]{:S(2)}, u32[]{:S(2)}) collective-permute-start(bf16[2,128,128]{2,1,0:T(8,128)(2,1)S(1)} %slice.104), channel_id=1, source_target_pairs={{0,32},{4,36},{8,40},{12,44},{16,48},{20,52},{24,56},{28,60},{32,0... | collective-permute-start | bytes 196616 | tf_op jit(solution)/shard_map/ppermute | solution.py:212
  377.1 9.7 %collective-permute-start.30 = (bf16[1,128,128]{2,1,0:T(8,128)(2,1)S(1)}, bf16[1,128,128]{2,1,0:T(8,128)(2,1)S(1)}, u32[]{:S(2)}, u32[]{:S(2)}) collective-permute-start(bf16[1,128,128]{2,1,0:T(8,128)(2,1)S(1)} %slice.105), channel_id=1, source_target_pairs={{0,64},{4,68},{8,72},{12,76},{16,80},{20,84},{24,88},{28,92},{32,9... | collective-permute-start | bytes 98312 | tf_op jit(solution)/shard_map/ppermute | solution.py:212
  (9 other events, 7.7 us)
where the time goes:
time: 391 us; the launch traced here: 387 us
  starting transfers between devices  146 us (37%)
  Pallas kernels  112 us (29%)
  waiting for transfers between devices  86.6 us (22%)
  local copies, waits for them, and re-layouts  29.4 us (8%)
  other arithmetic  11.4 us (3%)
    ppermute x16, starting transfers between devices, along(): return lax.ppermute(value, 'dp', perm)  62.6 us
    ppermute x6, waiting for transfers between devices, pass_back(): lax.ppermute(value, 'section', [(i, i - 1) for i in range(1, sections)])  54.2 us
    pallas_call x8, Pallas kernels, rank_partial(): pl.pallas_call(rank_kernel, grid=(GRID,), in_specs=[SCALARS, whole((token...  40.8 us
    pallas_call x8, Pallas kernels, input_grad(): pl.pallas_call(input_kernel, grid=(GRID,), in_specs=[SCALARS, whole((copi...  37.6 us
    all_to_all x8, starting transfers between devices, whole_step(): arrived = lax.all_to_all(partial, 'tensor', 0, 0, tiled=True)  35.6 us
    ppermute x9, starting transfers between devices, swapped(): lax.ppermute(value, 'dp', [(p, p ^ distance) for p in range(self.count)])  31 us
    pallas_call x8, Pallas kernels, sparse_product(): pl.pallas_call(sparse_kernel, grid=(1,), in_specs=[SCALARS, SCALARS, SCAL...  30.7 us
    unnamed x68, local copies, waits for them, and re-layouts  18.5 us
  transfers between devices with their start and end apart: 39, of which 14 were waited for; matrix products, arithmetic and copies ran while one was open for 5% of the time, Pallas kernels for 28%

commit v1 on v0

--- a/solution.py
+++ b/solution.py
@@ -9,7 +9,13 @@
 F32 = jnp.float32
 FAR = 2
 CORES = 2
-LIMIT = pltpu.CompilerParams(vmem_limit_bytes=20 * 1024 * 1024)
+
+
+def granted(mib):
+    return pltpu.CompilerParams(vmem_limit_bytes=mib * 1024 * 1024)
+
+
+LIMIT = granted(20)
 
 
 def contract_last(a, b):
@@ -24,133 +30,184 @@
     return pl.ds(pl.multiple_of(pos * size, size), size)
 
 
-def whole(shape):
-    zeros = (0,) * len(shape)
-    return pl.BlockSpec(shape, lambda i: zeros)
-
-
 SCALARS = pl.BlockSpec(memory_space=pltpu.SMEM)
-GRID = 4
 
 
 def cost(flops, size):
     return pl.CostEstimate(flops=flops, bytes_accessed=size, transcendentals=0)
 
 
-def both_cores(core, mine_ref, other_ref, joined_ref):
-    joined_ref[:, core] = mine_ref[...]
-    joined_ref[:, 1 - core] = other_ref[...]
-    _, _, _, width = joined_ref.shape
-    return joined_ref[...].reshape(-1, width)
-
-
-def rank_kernel(meta_ref, u_ref, mine_ref, other_ref, o_ref, joined_ref):
-    weight = both_cores(meta_ref[0], mine_ref, other_ref, joined_ref)
-    product = contract_last(u_ref[...], weight).astype(BF)
-    for i in range(o_ref.shape[0]):
-        o_ref[i] = product
-
-
-def rank_partial(meta, u, mine, other, copies):
+VMEM = pl.BlockSpec(memory_space=pltpu.VMEM)
+HBM = pl.BlockSpec(memory_space=pltpu.HBM)
+
+
+def join_kernel(meta_ref, mine_ref, other_ref, *outs):
+    core = meta_ref[0]
+    at = 0
+    for out in outs:
+        rows = out.shape[2]
+        out[:, core] = mine_ref[:, at : at + rows]
+        out[:, 1 - core] = other_ref[:, at : at + rows]
+        at += rows
+
+
+def joined(meta, mine, other, parts):
+    pieces, _, width = mine.shape
+    out = pl.pallas_call(
+        join_kernel,
+        in_specs=[SCALARS, VMEM, VMEM],
+        out_specs=[VMEM] * len(parts),
+        out_shape=[pltpu.HBM((pieces, CORES, rows, width), BF) for rows in parts],
+        cost_estimate=cost(0, 2 * mine.size * CORES * 2),
+        compiler_params=LIMIT,
+        name="joined",
+    )(meta, mine, other)
+    return [x.reshape(pieces * CORES, x.shape[2], width) for x in out]
+
+
+def fetched(source, target, sems, first=0):
+    count = target.shape[0]
+    copies = [
+        pltpu.make_async_copy(source.at[i], target.at[i], sems.at[first + i])
+        for i in range(count)
+    ]
+    for copy in copies:
+        copy.start()
+    return copies
+
+
+def rank_kernel(u_ref, a_ref, o_ref, weight, result, sems, out_sems):
+    chunks, copies = weight.shape[0], o_ref.shape[0]
+    fetched(a_ref, weight, sems)
+    part = result.shape[2]
+
+    def store(i, j):
+        at = o_ref.at[j, :, block_at(i, part)]
+        return pltpu.make_async_copy(result.at[i], at, out_sems.at[i, j])
+
+    def one(i, carry):
+        pltpu.make_async_copy(a_ref.at[i], weight.at[i], sems.at[i]).wait()
+        chunk = weight[i].reshape(part, -1)
+        result[i] = contract_last(u_ref[...], chunk).astype(BF)
+        for j in range(copies):
+            store(i, j).start()
+        return carry
+
+    lax.fori_loop(0, chunks, one, 0)
+    for i in range(chunks):
+        for j in range(copies):
+            store(i, j).wait()
+
+
+def rank_partial(u, weight, copies):
     tokens, width = u.shape
-    pieces, rows, _ = mine.shape
-    step = pieces // GRID
-    rank = pieces * rows * CORES
-    shard = pl.BlockSpec((step, rows, width), lambda i: (i, 0, 0))
+    pieces, rows, _ = weight.shape
+    rank = pieces * rows
+    chunks = 4
+    weight = weight.reshape(chunks, pieces // chunks, rows, width)
     return pl.pallas_call(
         rank_kernel,
-        grid=(GRID,),
-        in_specs=[SCALARS, whole((tokens, width)), shard, shard],
-        out_specs=pl.BlockSpec((copies, tokens, rank // GRID), lambda i: (0, 0, i)),
+        in_specs=[VMEM, HBM],
+        out_specs=HBM,
         out_shape=pltpu.HBM((copies, tokens, rank), BF),
-        scratch_shapes=[pltpu.VMEM((step, CORES, rows, width), BF)],
+        scratch_shapes=[
+            pltpu.VMEM(weight.shape, BF),
+            pltpu.VMEM((chunks, tokens, rank // chunks), BF),
+            pltpu.SemaphoreType.DMA((chunks,)),
+            pltpu.SemaphoreType.DMA((chunks, copies)),
+        ],
         cost_estimate=cost(2 * tokens * width * rank, 2 * width * rank),
-        compiler_params=LIMIT,
+        compiler_params=granted(60),
         name="rank_partial",
-    )(meta, u, mine, other)
-
-
-def sparse_kernel(meta_ref, rows_ref, cols_ref, u_ref, mine_ref, other_ref, o_ref, t_ref):
-    pieces, _, width = mine_ref.shape
+    )(u, weight)
+
+
+def sparse_kernel(meta_ref, rows_ref, cols_ref, u_ref, v_ref, o_ref, t_ref):
+    blocks, _, width = v_ref.shape
     size = t_ref.shape[1]
-    core, shift, base = meta_ref[0], meta_ref[2], meta_ref[3]
-    group = meta_ref[4]
-
-    def product(k, carry):
-        for ref, far in ((mine_ref, 0), (other_ref, 1)):
-            value = jnp.concatenate(
-                [ref[k, :, j * size : (j + 1) * size] for j in range(width // size)], axis=0
-            )
-            n = CORES * k + (core if far == 0 else 1 - core)
-            at = block_at(cols_ref[n * group + shift] - base, size)
-            t_ref[CORES * k + far] = contract_last(u_ref[:, at], value)
-        return carry
-
-    lax.fori_loop(0, pieces, product, 0, unroll=4)
+    shift, base, group = meta_ref[2], meta_ref[3], meta_ref[4]
+
+    def product(n, carry):
+        value = jnp.concatenate(
+            [v_ref[n, :, j * size : (j + 1) * size] for j in range(width // size)], axis=0
+        )
+        at = block_at(cols_ref[n * group + shift] - base, size)
+        t_ref[n] = contract_last(u_ref[:, at], value)
+        return carry
+
+    lax.fori_loop(0, blocks, product, 0, unroll=8)
     o_ref[...] = jnp.zeros_like(o_ref)
 
-    def place(k, carry):
-        for far in range(CORES):
-            n = CORES * k + (core if far == 0 else 1 - core)
-            at = block_at(rows_ref[n * group + shift] - base, size)
-            o_ref[:, at] += t_ref[CORES * k + far]
-        return carry
-
-    lax.fori_loop(0, pieces, place, 0, unroll=2)
-
-
-def sparse_product(meta, rows, cols, u, mine, other, size):
+    def place(n, carry):
+        at = block_at(rows_ref[n * group + shift] - base, size)
+        o_ref[:, at] += t_ref[n]
+        return carry
+
+    lax.fori_loop(0, blocks, place, 0, unroll=4)
+
+
+def sparse_product(meta, rows, cols, u, values, size):
     tokens, width = u.shape
-    pieces, total, rank = mine.shape
-    sub = size * size // rank
-    values = pl.BlockSpec((pieces, sub, rank), lambda i: (0, (total - sub) // sub, 0))
+    blocks, _, rank = values.shape
     return pl.pallas_call(
         sparse_kernel,
-        grid=(1,),
-        in_specs=[SCALARS, SCALARS, SCALARS, whole((tokens, width)), values, values],
-        out_specs=whole((tokens, width)),
+        in_specs=[SCALARS, SCALARS, SCALARS, VMEM, VMEM],
+        out_specs=VMEM,
         out_shape=pltpu.HBM((tokens, width), F32),
-        scratch_shapes=[pltpu.VMEM((CORES * pieces, tokens, size), F32)],
+        scratch_shapes=[pltpu.VMEM((blocks, tokens, size), F32)],
         cost_estimate=cost(2 * tokens * width * rank, 2 * width * rank),
         compiler_params=LIMIT,
         name="sparse_product",
-    )(meta, rows, cols, u, mine, other)
-
-
-def input_kernel(meta_ref, p_ref, mine_ref, other_ref, s_ref, o_ref, ra_ref, joined_ref):
-    @pl.when(pl.program_id(0) == 0)
-    def _():
-        total = p_ref[0].astype(F32)
-        for i in range(1, p_ref.shape[0]):
-            total += p_ref[i].astype(F32)
-        ra_ref[...] = total.astype(BF)
-
-    weight = both_cores(meta_ref[0], mine_ref, other_ref, joined_ref)
-    o_ref[...] = (contract_last(ra_ref[...], weight) + s_ref[...]).astype(BF)
-
-
-def input_grad(meta, arrived, mine, other, sparse, size):
+    )(meta, rows, cols, u, values)
+
+
+def input_kernel(p_ref, b_ref, s_ref, o_ref, parts, weight, sparse, sems, sparse_sem):
+    copies, chunks = parts.shape[0], weight.shape[0]
+    arrivals = fetched(p_ref, parts, sems)
+    fetched(b_ref, weight, sems, copies)
+    last = pltpu.make_async_copy(s_ref, sparse, sparse_sem)
+    last.start()
+    total = None
+    for i, arrival in enumerate(arrivals):
+        arrival.wait()
+        part = parts[i].astype(F32)
+        total = part if total is None else total + part
+    act = total.astype(BF)
+    last.wait()
+    size = o_ref.shape[1] // chunks
+
+    def one(i, carry):
+        pltpu.make_async_copy(b_ref.at[i], weight.at[i], sems.at[copies + i]).wait()
+        at = block_at(i, size)
+        dense = contract_last(act, weight[i].reshape(size, -1))
+        o_ref[:, at] = (dense + sparse[:, at]).astype(BF)
+        return carry
+
+    lax.fori_loop(0, chunks, one, 0)
+
+
+def input_grad(arrived, weight, sparse):
     copies, tokens, rank = arrived.shape
-    pieces, total, _ = mine.shape
-    rows = total - size * size // rank
-    step = pieces // GRID
-    width = CORES * pieces * rows
-    shard = pl.BlockSpec((step, rows, rank), lambda i: (i, 0, 0))
-    slab = pl.BlockSpec((tokens, width // GRID), lambda i: (0, i))
+    pieces, rows, _ = weight.shape
+    chunks = 4
+    weight = weight.reshape(chunks, pieces // chunks, rows, rank)
+    width = pieces * rows
     return pl.pallas_call(
         input_kernel,
-        grid=(GRID,),
-        in_specs=[SCALARS, whole((copies, tokens, rank)), shard, shard, slab],
-        out_specs=slab,
+        in_specs=[HBM] * 3,
+        out_specs=VMEM,
         out_shape=jax.ShapeDtypeStruct((tokens, width), BF),
         scratch_shapes=[
-            pltpu.VMEM((tokens, rank), BF),
-            pltpu.VMEM((step, CORES, rows, rank), BF),
+            pltpu.VMEM(arrived.shape, BF),
+            pltpu.VMEM(weight.shape, BF),
+            pltpu.VMEM(sparse.shape, F32),
+            pltpu.SemaphoreType.DMA((copies + chunks,)),
+            pltpu.SemaphoreType.DMA,
         ],
         cost_estimate=cost(2 * tokens * width * rank, 2 * width * rank),
-        compiler_params=LIMIT,
+        compiler_params=granted(63),
         name="input_grad",
-    )(meta, arrived, mine, other, sparse)
+    )(arrived, weight, sparse)
 
 
 def block_kernel(meta_ref, rows_ref, cols_ref, st_ref, u0_ref, u1_ref, o_ref):
@@ -244,8 +301,8 @@
         distance = 1
         while distance < self.count:
             half = blocks.shape[0] // 2
-            sent = blocks[half:].astype(BF)
-            blocks = blocks[:half] + self.swapped(sent, distance).astype(F32)
+            got = self.swapped(blocks[half:].astype(BF), distance)
+            blocks = blocks[:half] + got.astype(F32)
             distance *= 2
         return blocks
 
@@ -282,16 +339,18 @@
         [data.core, data.place, tensor_pos, tensor_pos * local_blocks, jnp.int32(tensor_count)]
     )
     rows, cols = block_rows[0], block_cols[0]
+    (a_full,) = joined(meta, a_mine, a_other, (factor_a.shape[1],))
+    b_full, values = joined(meta, bv_mine, bv_other, (factor_b.shape[1], sub))
 
     ups = [[cotangent[m]] for m in range(batches)]
     grads = [[] for _ in range(batches)]
     for stage in range(sections):
         for m in range(batches):
             u = ups[m][stage]
-            partial = rank_partial(meta, u, a_mine, a_other, tensor_count)
+            partial = rank_partial(u, a_full, tensor_count)
             arrived = lax.all_to_all(partial, "tensor", 0, 0, tiled=True)
-            sparse = sparse_product(meta, rows, cols, u, bv_mine, bv_other, size)
-            grad = input_grad(meta, arrived, bv_mine, bv_other, sparse, size)
+            sparse = sparse_product(meta, rows, cols, u, values, size)
+            grad = input_grad(arrived, b_full, sparse)
             grads[m].append(grad)
             if stage + 1 < sections:
                 ups[m].append(pass_back(grad))

time: 391 us -> 394 us (level)
  Pallas kernels: 112 us -> 125 us
  local copies, waits for them, and re-layouts: 29.4 us -> 18.4 us
    pallas_call x24 -> x26, Pallas kernels: 109 us -> 122 us  [the longest x8 45.2 us: input_grad(): pl.pallas_call(input_kernel, in_specs=[HBM] * 3, out_specs=VMEM, out_shap...]
    unnamed x68 -> x50, local copies, waits for them, and re-layouts: 18.5 us -> 6.34 us
  transfers between devices with their start and end apart: 39 -> 39, of which waited for: 14 -> 14; matrix products, arithmetic and copies ran while one was open for 5% -> 5% of each run, Pallas kernels for 28% -> 31%
where the time goes in v1:
time: 394 us; the launch traced here: 392 us
  starting transfers between devices  147 us (37%)
  Pallas kernels  125 us (32%)
  waiting for transfers between devices  88.4 us (22%)
  local copies, waits for them, and re-layouts  18.4 us (5%)
  other arithmetic  11.3 us (3%)
    ppermute x16, starting transfers between devices, along(): return lax.ppermute(value, 'dp', perm)  62.6 us
    ppermute x6, waiting for transfers between devices, pass_back(): lax.ppermute(value, 'section', [(i, i - 1) for i in range(1, sections)])  56.6 us
    pallas_call x8, Pallas kernels, input_grad(): pl.pallas_call(input_kernel, in_specs=[HBM] * 3, out_specs=VMEM, out_shap...  45.2 us
    pallas_call x8, Pallas kernels, rank_partial(): pl.pallas_call(rank_kernel, in_specs=[VMEM, HBM], out_specs=HBM, out_shap...  40.9 us
    all_to_all x8, starting transfers between devices, whole_step(): arrived = lax.all_to_all(partial, 'tensor', 0, 0, tiled=True)  35.8 us
    ppermute x9, starting transfers between devices, swapped(): lax.ppermute(value, 'dp', [(p, p ^ distance) for p in range(self.count)])  31.4 us
    pallas_call x8, Pallas kernels, sparse_product(): pl.pallas_call(sparse_kernel, in_specs=[SCALARS, SCALARS, SCALARS, VMEM,...  26.7 us
    ppermute x6, starting transfers between devices, pass_back(): lax.ppermute(value, 'section', [(i, i - 1) for i in range(1, sections)])  17.3 us
  transfers between devices with their start and end apart: 39, of which 14 were waited for; matrix products, arithmetic and copies ran while one was open for 5% of the time, Pallas kernels for 31%

profile of v1, /device:TPU:40, one launch (start us, length us, event | category | flops | bytes accessed | tf_op | source)
XLA Modules:
  0.0 391.8 jit_solution(2129354042458489439)
XLA Ops:
  0.6 3.0 collective-permute-start
  5.4 6.8 %collective-permute-start.10 = (bf16[80,1024]{1,0:T(8,128)(2,1)S(1)}, bf16[80,1024]{1,0:T(8,128)(2,1)S(1)}, u32[]{:S(2)}, u32[]{:S(2)}) collective-permute-start(bf16[80,1024]{1,0:T(8,128)(2,1)S(1)} %pad_maximum_fusion.2), channel_id=1, source_target_pairs={{0,64},{4,68},{8,72},{12,76},{16,80},{20,84},{24,88},{28,92},{32,9... | collective-permute-start | bytes 491528 | tf_op jit(solution)/shard_map/ppermute | solution.py:269
  12.3 3.0 collective-permute-done
  16.2 4.3 %collective-permute-start.1 = (bf16[2,32,2048]{2,1,0:T(8,128)(2,1)S(1)}, bf16[2,32,2048]{2,1,0:T(8,128)(2,1)S(1)}, u32[]{:S(2)}, u32[]{:S(2)}) collective-permute-start(bf16[2,32,2048]{2,1,0:T(8,128)(2,1)S(1)} %pad_maximum_fusion.1), channel_id=1, source_target_pairs={{0,8},{4,12},{8,16},{12,20},{16,24},{20,28},{24,32},{28,36},{32,40... | collective-permute-start | bytes 786440 | tf_op jit(solution)/shard_map/ppermute | solution.py:266
  20.5 8.6 %collective-permute-start.2 = (bf16[2,32,2048]{2,1,0:T(8,128)(2,1)S(1)}, bf16[2,32,2048]{2,1,0:T(8,128)(2,1)S(1)}, u32[]{:S(2)}, u32[]{:S(2)}) collective-permute-start(bf16[2,32,2048]{2,1,0:T(8,128)(2,1)S(1)} %pad_maximum_fusion.1), channel_id=1, source_target_pairs={{0,56},{4,60},{8,0},{12,4},{16,8},{20,12},{24,16},{28,20},{32,24},... | collective-permute-start | bytes 786440 | tf_op jit(solution)/shard_map/ppermute | solution.py:266
  33.5 5.1 %collective-permute-start.12 = (bf16[2,80,1024]{2,1,0:T(8,128)(2,1)S(1)}, bf16[2,80,1024]{2,1,0:T(8,128)(2,1)S(1)}, u32[]{:S(2)}, u32[]{:S(2)}) collective-permute-start(bf16[2,80,1024]{2,1,0:T(8,128)(2,1)S(1)} %pad_maximum_fusion), channel_id=1, source_target_pairs={{0,56},{4,60},{8,0},{12,4},{16,8},{20,12},{24,16},{28,20},{32,24},... | collective-permute-start | bytes 983048 | tf_op jit(solution)/shard_map/ppermute | solution.py:266
  41.0 5.1 %collective-permute-start.4 = (bf16[2,32,2048]{2,1,0:T(8,128)(2,1)S(1)}, bf16[2,32,2048]{2,1,0:T(8,128)(2,1)S(1)}, u32[]{:S(2)}, u32[]{:S(2)}) collective-permute-start(bf16[2,32,2048]{2,1,0:T(8,128)(2,1)S(1)} %collective-permute-done.2), channel_id=1, source_target_pairs={{0,56},{4,60},{8,0},{12,4},{16,8},{20,12},{24,16},{28,20},{32,24},... | collective-permute-start | bytes 786440 | tf_op jit(solution)/shard_map/ppermute | solution.py:266
  49.6 5.1 %collective-permute-start.14 = (bf16[2,80,1024]{2,1,0:T(8,128)(2,1)S(1)}, bf16[2,80,1024]{2,1,0:T(8,128)(2,1)S(1)}, u32[]{:S(2)}, u32[]{:S(2)}) collective-permute-start(bf16[2,80,1024]{2,1,0:T(8,128)(2,1)S(1)} %collective-permute-done.12), channel_id=1, source_target_pairs={{0,56},{4,60},{8,0},{12,4},{16,8},{20,12},{24,16},{28,20},{32,24},... | collective-permute-start | bytes 983048 | tf_op jit(solution)/shard_map/ppermute | solution.py:266
  56.7 5.1 %collective-permute-start.6 = (bf16[2,32,2048]{2,1,0:T(8,128)(2,1)S(1)}, bf16[2,32,2048]{2,1,0:T(8,128)(2,1)S(1)}, u32[]{:S(2)}, u32[]{:S(2)}) collective-permute-start(bf16[2,32,2048]{2,1,0:T(8,128)(2,1)S(1)} %collective-permute-done.4), channel_id=1, source_target_pairs={{0,56},{4,60},{8,0},{12,4},{16,8},{20,12},{24,16},{28,20},{32,24},... | collective-permute-start | bytes 786440 | tf_op jit(solution)/shard_map/ppermute | solution.py:266
  65.3 5.1 %collective-permute-start.16 = (bf16[2,80,1024]{2,1,0:T(8,128)(2,1)S(1)}, bf16[2,80,1024]{2,1,0:T(8,128)(2,1)S(1)}, u32[]{:S(2)}, u32[]{:S(2)}) collective-permute-start(bf16[2,80,1024]{2,1,0:T(8,128)(2,1)S(1)} %collective-permute-done.14), channel_id=1, source_target_pairs={{0,56},{4,60},{8,0},{12,4},{16,8},{20,12},{24,16},{28,20},{32,24},... | collective-permute-start | bytes 983048 | tf_op jit(solution)/shard_map/ppermute | solution.py:266
  72.5 5.1 %collective-permute-start.8 = (bf16[1,32,2048]{2,1,0:T(8,128)(2,1)S(1)}, bf16[1,32,2048]{2,1,0:T(8,128)(2,1)S(1)}, u32[]{:S(2)}, u32[]{:S(2)}) collective-permute-start(bf16[1,32,2048]{2,1,0:T(8,128)(2,1)S(1)} %slice.70), channel_id=1, source_target_pairs={{0,56},{4,60},{8,0},{12,4},{16,8},{20,12},{24,16},{28,20},{32,24},... | collective-permute-start | bytes 393224 | tf_op jit(solution)/shard_map/ppermute | solution.py:266
  84.7 5.5 %collective-permute-start.18 = (bf16[1,80,1024]{2,1,0:T(8,128)(2,1)S(1)}, bf16[1,80,1024]{2,1,0:T(8,128)(2,1)S(1)}, u32[]{:S(2)}, u32[]{:S(2)}) collective-permute-start(bf16[1,80,1024]{2,1,0:T(8,128)(2,1)S(1)} %slice.72), channel_id=1, source_target_pairs={{0,56},{4,60},{8,0},{12,4},{16,8},{20,12},{24,16},{28,20},{32,24},... | collective-permute-start | bytes 491528 | tf_op jit(solution)/shard_map/ppermute | solution.py:266
  98.7 4.5 %joined.2 = bf16[16,2,32,2048]{3,2,1,0:T(8,128)(2,1)} custom-call(s32[5]{0:T(128)S(1)} %stack.46.meta_ref, bf16[16,32,2048]{2,1,0:T(8,128)(2,1)} %bitcast.24.mine_ref, bf16[16,32,2048]{2,1,0:T(8,128)(2,1)} %collective-permute-done.9.other_ref), custom_call_target="tpu_custom_call" | custom-call | bytes 8388608 | tf_op jit(solution)/shard_map/joined/pallas_call | solution.py:56
  103.2 5.1 %rank_partial.12 = bf16[4,128,1024]{2,1,0:T(8,128)(2,1)} custom-call(bf16[128,2048]{1,0:T(8,128)(2,1)} %get-tuple-element.9.u_ref, bf16[4,8,32,2048]{3,2,1,0:T(8,128)(2,1)} %bitcast.140), custom_call_target="tpu_custom_call" | custom-call | flops 536870912 | bytes 4194304 | tf_op jit(solution)/shard_map/rank_partial/pallas_call | solution.py:108
  108.3 4.3 %all-to-all-start.4 = ((bf16[4,128,1024]{2,1,0:T(8,128)(2,1)}), bf16[4,128,1024]{2,1,0:T(8,128)(2,1)}, u32[]{:S(2)}, u32[]{:S(2)}) async-start(bf16[4,128,1024]{2,1,0:T(8,128)(2,1)} %rank_partial.12), calls=%async_computation.4 | async-start | bytes 2097152 | tf_op jit(solution)/shard_map/all_to_all | solution.py:351
  112.6 5.1 %rank_partial.8 = bf16[4,128,1024]{2,1,0:T(8,128)(2,1)} custom-call(bf16[128,2048]{1,0:T(8,128)(2,1)} %get-tuple-element.8.u_ref, bf16[4,8,32,2048]{3,2,1,0:T(8,128)(2,1)} %bitcast.141), custom_call_target="tpu_custom_call" | custom-call | flops 536870912 | bytes 4194304 | tf_op jit(solution)/shard_map/rank_partial/pallas_call | solution.py:108
  117.7 11.0 %all-to-all-done.4.p_ref = bf16[4,128,1024]{2,1,0:T(8,128)(2,1)} async-done(((bf16[4,128,1024]{2,1,0:T(8,128)(2,1)}), bf16[4,128,1024]{2,1,0:T(8,128)(2,1)}, u32[]{:S(2)}, u32[]{:S(2)}) %all-to-all-start.4) | async-done | bytes 1048608 | tf_op jit(solution)/shard_map/all_to_all | solution.py:351
  128.7 4.3 %all-to-all-start = ((bf16[4,128,1024]{2,1,0:T(8,128)(2,1)}), bf16[4,128,1024]{2,1,0:T(8,128)(2,1)}, u32[]{:S(2)}, u32[]{:S(2)}) async-start(bf16[4,128,1024]{2,1,0:T(8,128)(2,1)} %rank_partial.8), calls=%async_computation | async-start | bytes 2097152 | tf_op jit(solution)/shard_map/all_to_all | solution.py:351
  133.0 4.5 %joined.3 = (bf16[16,2,64,1024]{3,2,1,0:T(8,128)(2,1)}, bf16[16,2,16,1024]{3,2,1,0:T(8,128)(2,1)}) custom-call(s32[5]{0:T(128)S(1)} %stack.46.meta_ref, bf16[16,80,1024]{2,1,0:T(8,128)(2,1)S(1)} %bitcast.120, bf16[16,80,1024]{2,1,0:T(8,128)(2,1)} %collective-permute-done.19.other_ref), custom_call_target="tpu_custom_call" | custom-call | bytes 10485760 | tf_op jit(solution)/shard_map/joined/pallas_call | solution.py:56
  138.7 3.2 sparse_product.12.s_ref
  141.9 5.7 %input_grad.12 = bf16[128,2048]{1,0:T(8,128)(2,1)} custom-call(bf16[4,128,1024]{2,1,0:T(8,128)(2,1)} %all-to-all-done.4.p_ref, bf16[4,8,64,1024]{3,2,1,0:T(8,128)(2,1)} %bitcast.148, f32[128,2048]{1,0:T(8,128)} %sparse_product.12.s_ref), custom_call_target="tpu_custom_call" | custom-call | flops 536870912 | bytes 4194304 | tf_op jit(solution)/shard_map/input_grad/pallas_call | solution.py:195
  147.6 3.2 collective-permute-start.23
  150.8 12.5 %collective-permute-done.23.u_ref = bf16[128,2048]{1,0:T(8,128)(2,1)S(1)} collective-permute-done((bf16[128,2048]{1,0:T(8,128)(2,1)}, bf16[128,2048]{1,0:T(8,128)(2,1)S(1)}, u32[]{:S(2)}, u32[]{:S(2)}) %collective-permute-start.23) | collective-permute-done | bytes 524320 | tf_op jit(solution)/shard_map/ppermute | solution.py:312
  164.0 5.1 %rank_partial.13 = bf16[4,128,1024]{2,1,0:T(8,128)(2,1)} custom-call(bf16[128,2048]{1,0:T(8,128)(2,1)} %copy-done.6, bf16[4,8,32,2048]{3,2,1,0:T(8,128)(2,1)} %bitcast.142), custom_call_target="tpu_custom_call" | custom-call | flops 536870912 | bytes 4194304 | tf_op jit(solution)/shard_map/rank_partial/pallas_call | solution.py:108
  169.2 4.4 %all-to-all-start.5 = ((bf16[4,128,1024]{2,1,0:T(8,128)(2,1)}), bf16[4,128,1024]{2,1,0:T(8,128)(2,1)}, u32[]{:S(2)}, u32[]{:S(2)}) async-start(bf16[4,128,1024]{2,1,0:T(8,128)(2,1)} %rank_partial.13), calls=%async_computation.5 | async-start | bytes 2097152 | tf_op jit(solution)/shard_map/all_to_all | solution.py:351
  173.6 3.2 sparse_product.8.s_ref
  176.9 5.6 %input_grad.8 = bf16[128,2048]{1,0:T(8,128)(2,1)} custom-call(bf16[4,128,1024]{2,1,0:T(8,128)(2,1)} %all-to-all-done.p_ref, bf16[4,8,64,1024]{3,2,1,0:T(8,128)(2,1)} %bitcast.149, f32[128,2048]{1,0:T(8,128)} %sparse_product.8.s_ref), custom_call_target="tpu_custom_call" | custom-call | flops 536870912 | bytes 4194304 | tf_op jit(solution)/shard_map/input_grad/pallas_call | solution.py:195
  182.5 3.2 collective-permute-start.20
  185.7 11.5 %collective-permute-done.20.u_ref = bf16[128,2048]{1,0:T(8,128)(2,1)S(1)} collective-permute-done((bf16[128,2048]{1,0:T(8,128)(2,1)}, bf16[128,2048]{1,0:T(8,128)(2,1)S(1)}, u32[]{:S(2)}, u32[]{:S(2)}) %collective-permute-start.20) | collective-permute-done | bytes 524320 | tf_op jit(solution)/shard_map/ppermute | solution.py:312
  198.0 5.1 %rank_partial.9 = bf16[4,128,1024]{2,1,0:T(8,128)(2,1)} custom-call(bf16[128,2048]{1,0:T(8,128)(2,1)} %copy-done.8, bf16[4,8,32,2048]{3,2,1,0:T(8,128)(2,1)} %bitcast.143), custom_call_target="tpu_custom_call" | custom-call | flops 536870912 | bytes 4194304 | tf_op jit(solution)/shard_map/rank_partial/pallas_call | solution.py:108
  203.1 4.4 %all-to-all-start.1 = ((bf16[4,128,1024]{2,1,0:T(8,128)(2,1)}), bf16[4,128,1024]{2,1,0:T(8,128)(2,1)}, u32[]{:S(2)}, u32[]{:S(2)}) async-start(bf16[4,128,1024]{2,1,0:T(8,128)(2,1)} %rank_partial.9), calls=%async_computation.1 | async-start | bytes 2097152 | tf_op jit(solution)/shard_map/all_to_all | solution.py:351
  207.6 3.3 sparse_product.13.s_ref
  210.9 5.7 %input_grad.13 = bf16[128,2048]{1,0:T(8,128)(2,1)} custom-call(bf16[4,128,1024]{2,1,0:T(8,128)(2,1)} %all-to-all-done.5.p_ref, bf16[4,8,64,1024]{3,2,1,0:T(8,128)(2,1)} %bitcast.150, f32[128,2048]{1,0:T(8,128)} %sparse_product.13.s_ref), custom_call_target="tpu_custom_call" | custom-call | flops 536870912 | bytes 4194304 | tf_op jit(solution)/shard_map/input_grad/pallas_call | solution.py:195
  216.6 3.1 collective-permute-start.24
  219.7 10.6 %collective-permute-done.24.u_ref = bf16[128,2048]{1,0:T(8,128)(2,1)S(1)} collective-permute-done((bf16[128,2048]{1,0:T(8,128)(2,1)}, bf16[128,2048]{1,0:T(8,128)(2,1)S(1)}, u32[]{:S(2)}, u32[]{:S(2)}) %collective-permute-start.24) | collective-permute-done | bytes 524320 | tf_op jit(solution)/shard_map/ppermute | solution.py:312
  231.1 5.1 %rank_partial.14 = bf16[4,128,1024]{2,1,0:T(8,128)(2,1)} custom-call(bf16[128,2048]{1,0:T(8,128)(2,1)} %copy-done.10, bf16[4,8,32,2048]{3,2,1,0:T(8,128)(2,1)} %bitcast.144), custom_call_target="tpu_custom_call" | custom-call | flops 536870912 | bytes 4194304 | tf_op jit(solution)/shard_map/rank_partial/pallas_call | solution.py:108
  236.2 4.4 %all-to-all-start.6 = ((bf16[4,128,1024]{2,1,0:T(8,128)(2,1)}), bf16[4,128,1024]{2,1,0:T(8,128)(2,1)}, u32[]{:S(2)}, u32[]{:S(2)}) async-start(bf16[4,128,1024]{2,1,0:T(8,128)(2,1)} %rank_partial.14), calls=%async_computation.6 | async-start | bytes 2097152 | tf_op jit(solution)/shard_map/all_to_all | solution.py:351
  240.7 3.3 sparse_product.9.s_ref
  243.9 5.7 %input_grad.9 = bf16[128,2048]{1,0:T(8,128)(2,1)} custom-call(bf16[4,128,1024]{2,1,0:T(8,128)(2,1)} %all-to-all-done.1.p_ref, bf16[4,8,64,1024]{3,2,1,0:T(8,128)(2,1)} %bitcast.151, f32[128,2048]{1,0:T(8,128)} %sparse_product.9.s_ref), custom_call_target="tpu_custom_call" | custom-call | flops 536870912 | bytes 4194304 | tf_op jit(solution)/shard_map/input_grad/pallas_call | solution.py:195
  249.6 3.1 collective-permute-start.21
  252.7 9.6 %collective-permute-done.21.u_ref = bf16[128,2048]{1,0:T(8,128)(2,1)S(1)} collective-permute-done((bf16[128,2048]{1,0:T(8,128)(2,1)}, bf16[128,2048]{1,0:T(8,128)(2,1)S(1)}, u32[]{:S(2)}, u32[]{:S(2)}) %collective-permute-start.21) | collective-permute-done | bytes 524320 | tf_op jit(solution)/shard_map/ppermute | solution.py:312
  263.2 5.1 %rank_partial.10 = bf16[4,128,1024]{2,1,0:T(8,128)(2,1)} custom-call(bf16[128,2048]{1,0:T(8,128)(2,1)} %copy-done.12, bf16[4,8,32,2048]{3,2,1,0:T(8,128)(2,1)} %bitcast.145), custom_call_target="tpu_custom_call" | custom-call | flops 536870912 | bytes 4194304 | tf_op jit(solution)/shard_map/rank_partial/pallas_call | solution.py:108
  268.3 4.6 %all-to-all-start.2 = ((bf16[4,128,1024]{2,1,0:T(8,128)(2,1)}), bf16[4,128,1024]{2,1,0:T(8,128)(2,1)}, u32[]{:S(2)}, u32[]{:S(2)}) async-start(bf16[4,128,1024]{2,1,0:T(8,128)(2,1)} %rank_partial.10), calls=%async_computation.2 | async-start | bytes 2097152 | tf_op jit(solution)/shard_map/all_to_all | solution.py:351
  272.9 3.2 sparse_product.14.s_ref
  276.1 3.3 sparse_product.10.s_ref
  279.5 5.7 %input_grad.14 = bf16[128,2048]{1,0:T(8,128)(2,1)} custom-call(bf16[4,128,1024]{2,1,0:T(8,128)(2,1)} %all-to-all-done.6.p_ref, bf16[4,8,64,1024]{3,2,1,0:T(8,128)(2,1)} %bitcast.152, f32[128,2048]{1,0:T(8,128)} %sparse_product.14.s_ref), custom_call_target="tpu_custom_call" | custom-call | flops 536870912 | bytes 4194304 | tf_op jit(solution)/shard_map/input_grad/pallas_call | solution.py:195
  285.1 2.8 collective-permute-start.25
  288.0 5.6 %input_grad.10 = bf16[128,2048]{1,0:T(8,128)(2,1)} custom-call(bf16[4,128,1024]{2,1,0:T(8,128)(2,1)} %all-to-all-done.2.p_ref, bf16[4,8,64,1024]{3,2,1,0:T(8,128)(2,1)} %bitcast.153, f32[128,2048]{1,0:T(8,128)} %sparse_product.10.s_ref), custom_call_target="tpu_custom_call" | custom-call | flops 536870912 | bytes 4194304 | tf_op jit(solution)/shard_map/input_grad/pallas_call | solution.py:195
  295.6 4.3 %collective-permute-done.25.u_ref = bf16[128,2048]{1,0:T(8,128)(2,1)} collective-permute-done((bf16[128,2048]{1,0:T(8,128)(2,1)}, bf16[128,2048]{1,0:T(8,128)(2,1)}, u32[]{:S(2)}, u32[]{:S(2)}) %collective-permute-start.25) | collective-permute-done | bytes 524320 | tf_op jit(solution)/shard_map/ppermute | solution.py:312
  299.9 8.1 %collective-permute-done.22.u_ref = bf16[128,2048]{1,0:T(8,128)(2,1)S(1)} collective-permute-done((bf16[128,2048]{1,0:T(8,128)(2,1)}, bf16[128,2048]{1,0:T(8,128)(2,1)S(1)}, u32[]{:S(2)}, u32[]{:S(2)}) %collective-permute-start.22) | collective-permute-done | bytes 524320 | tf_op jit(solution)/shard_map/ppermute | solution.py:312
  310.0 3.1 block_products.1
  315.9 5.1 %rank_partial.15 = bf16[4,128,1024]{2,1,0:T(8,128)(2,1)} custom-call(bf16[128,2048]{1,0:T(8,128)(2,1)} %collective-permute-done.25.u_ref, bf16[4,8,32,2048]{3,2,1,0:T(8,128)(2,1)} %bitcast.146), custom_call_target="tpu_custom_call" | custom-call | flops 536870912 | bytes 4194304 | tf_op jit(solution)/shard_map/rank_partial/pallas_call | solution.py:108
  321.1 4.6 %all-to-all-start.7 = ((bf16[4,128,1024]{2,1,0:T(8,128)(2,1)}), bf16[4,128,1024]{2,1,0:T(8,128)(2,1)}, u32[]{:S(2)}, u32[]{:S(2)}) async-start(bf16[4,128,1024]{2,1,0:T(8,128)(2,1)} %rank_partial.15), calls=%async_computation.7 | async-start | bytes 2097152 | tf_op jit(solution)/shard_map/all_to_all | solution.py:351
  328.0 3.9 collective-permute-start.27
  331.8 3.8 sparse_product.15.s_ref
  335.6 5.2 %rank_partial.11 = bf16[4,128,1024]{2,1,0:T(8,128)(2,1)} custom-call(bf16[128,2048]{1,0:T(8,128)(2,1)} %copy-done.14, bf16[4,8,32,2048]{3,2,1,0:T(8,128)(2,1)} %bitcast.147), custom_call_target="tpu_custom_call" | custom-call | flops 536870912 | bytes 4194304 | tf_op jit(solution)/shard_map/rank_partial/pallas_call | solution.py:108
  340.9 3.3 sparse_product.11.s_ref
  344.1 4.7 %all-to-all-start.3 = ((bf16[4,128,1024]{2,1,0:T(8,128)(2,1)}), bf16[4,128,1024]{2,1,0:T(8,128)(2,1)}, u32[]{:S(2)}, u32[]{:S(2)}) async-start(bf16[4,128,1024]{2,1,0:T(8,128)(2,1)} %rank_partial.11), calls=%async_computation.3 | async-start | bytes 2097152 | tf_op jit(solution)/shard_map/all_to_all | solution.py:351
  349.7 4.6 %collective-permute-start.28 = (bf16[4,128,128]{2,1,0:T(8,128)(2,1)S(1)}, bf16[4,128,128]{2,1,0:T(8,128)(2,1)S(1)}, u32[]{:S(2)}, u32[]{:S(2)}) collective-permute-start(bf16[4,128,128]{2,1,0:T(8,128)(2,1)S(1)} %slice.103), channel_id=1, source_target_pairs={{0,16},{4,20},{8,24},{12,28},{16,0},{20,4},{24,8},{28,12},{32,48},... | collective-permute-start | bytes 393224 | tf_op jit(solution)/shard_map/ppermute | solution.py:269
  354.3 5.6 %input_grad.15 = bf16[128,2048]{1,0:T(8,128)(2,1)} custom-call(bf16[4,128,1024]{2,1,0:T(8,128)(2,1)} %all-to-all-done.7.p_ref, bf16[4,8,64,1024]{3,2,1,0:T(8,128)(2,1)} %bitcast.154, f32[128,2048]{1,0:T(8,128)} %sparse_product.15.s_ref), custom_call_target="tpu_custom_call" | custom-call | flops 536870912 | bytes 4194304 | tf_op jit(solution)/shard_map/input_grad/pallas_call | solution.py:195
  363.9 5.6 %input_grad.11 = bf16[128,2048]{1,0:T(8,128)(2,1)} custom-call(bf16[4,128,1024]{2,1,0:T(8,128)(2,1)} %all-to-all-done.3.p_ref, bf16[4,8,64,1024]{3,2,1,0:T(8,128)(2,1)} %bitcast.155, f32[128,2048]{1,0:T(8,128)} %sparse_product.11.s_ref), custom_call_target="tpu_custom_call" | custom-call | flops 536870912 | bytes 4194304 | tf_op jit(solution)/shard_map/input_grad/pallas_call | solution.py:195
  370.6 4.7 %collective-permute-start.29 = (bf16[2,128,128]{2,1,0:T(8,128)(2,1)S(1)}, bf16[2,128,128]{2,1,0:T(8,128)(2,1)S(1)}, u32[]{:S(2)}, u32[]{:S(2)}) collective-permute-start(bf16[2,128,128]{2,1,0:T(8,128)(2,1)S(1)} %slice.104), channel_id=1, source_target_pairs={{0,32},{4,36},{8,40},{12,44},{16,48},{20,52},{24,56},{28,60},{32,0... | collective-permute-start | bytes 196616 | tf_op jit(solution)/shard_map/ppermute | solution.py:269
  376.6 4.8 %collective-permute-done.29 = bf16[2,128,128]{2,1,0:T(8,128)(2,1)S(1)} collective-permute-done((bf16[2,128,128]{2,1,0:T(8,128)(2,1)S(1)}, bf16[2,128,128]{2,1,0:T(8,128)(2,1)S(1)}, u32[]{:S(2)}, u32[]{:S(2)}) %collective-permute-start.29) | collective-permute-done | bytes 65568 | tf_op jit(solution)/shard_map/ppermute | solution.py:269
  385.1 6.0 %collective-permute-done.30 = bf16[1,128,128]{2,1,0:T(8,128)(2,1)S(1)} collective-permute-done((bf16[1,128,128]{2,1,0:T(8,128)(2,1)S(1)}, bf16[1,128,128]{2,1,0:T(8,128)(2,1)S(1)}, u32[]{:S(2)}, u32[]{:S(2)}) %collective-permute-start.30) | collective-permute-done | bytes 32800 | tf_op jit(solution)/shard_map/ppermute | solution.py:269
  (137 shorter events, 60.5 us)
Async XLA Ops:
  0.6 30.9 %copy-start.24 = (bf16[1,64,1024]{2,1,0:T(8,128)(2,1)S(1)}, bf16[1,64,1024]{2,1,0:T(8,128)(2,1)}, u32[]{:S(2)}) copy-start(bf16[1,64,1024]{2,1,0:T(8,128)(2,1)} %param.10) | copy-start | bytes 393220
  0.6 14.6 %collective-permute-start = (bf16[32,2048]{1,0:T(8,128)(2,1)}, bf16[32,2048]{1,0:T(8,128)(2,1)S(1)}, u32[]{:S(2)}, u32[]{:S(2)}) collective-permute-start(bf16[32,2048]{1,0:T(8,128)(2,1)} %bitcast.160), channel_id=1, source_target_pairs={{0,64},{4,68},{8,72},{12,76},{16,80},{20,84},{24,88},{28,92},{32,9... | collective-permute-start | bytes 393224 | tf_op jit(solution)/shard_map/ppermute | solution.py:269
  5.4 26.1 %collective-permute-start.10 = (bf16[80,1024]{1,0:T(8,128)(2,1)S(1)}, bf16[80,1024]{1,0:T(8,128)(2,1)S(1)}, u32[]{:S(2)}, u32[]{:S(2)}) collective-permute-start(bf16[80,1024]{1,0:T(8,128)(2,1)S(1)} %pad_maximum_fusion.2), channel_id=1, source_target_pairs={{0,64},{4,68},{8,72},{12,76},{16,80},{20,84},{24,88},{28,92},{32,9... | collective-permute-start | bytes 491528 | tf_op jit(solution)/shard_map/ppermute | solution.py:269
  16.2 22.8 %collective-permute-start.1 = (bf16[2,32,2048]{2,1,0:T(8,128)(2,1)S(1)}, bf16[2,32,2048]{2,1,0:T(8,128)(2,1)S(1)}, u32[]{:S(2)}, u32[]{:S(2)}) collective-permute-start(bf16[2,32,2048]{2,1,0:T(8,128)(2,1)S(1)} %pad_maximum_fusion.1), channel_id=1, source_target_pairs={{0,8},{4,12},{8,16},{12,20},{16,24},{20,28},{24,32},{28,36},{32,40... | collective-permute-start | bytes 786440 | tf_op jit(solution)/shard_map/ppermute | solution.py:266
  20.5 20.5 %collective-permute-start.2 = (bf16[2,32,2048]{2,1,0:T(8,128)(2,1)S(1)}, bf16[2,32,2048]{2,1,0:T(8,128)(2,1)S(1)}, u32[]{:S(2)}, u32[]{:S(2)}) collective-permute-start(bf16[2,32,2048]{2,1,0:T(8,128)(2,1)S(1)} %pad_maximum_fusion.1), channel_id=1, source_target_pairs={{0,56},{4,60},{8,0},{12,4},{16,8},{20,12},{24,16},{28,20},{32,24},... | collective-permute-start | bytes 786440 | tf_op jit(solution)/shard_map/ppermute | solution.py:266
  31.6 16.0 %collective-permute-start.11 = (bf16[2,80,1024]{2,1,0:T(8,128)(2,1)S(1)}, bf16[2,80,1024]{2,1,0:T(8,128)(2,1)S(1)}, u32[]{:S(2)}, u32[]{:S(2)}) collective-permute-start(bf16[2,80,1024]{2,1,0:T(8,128)(2,1)S(1)} %pad_maximum_fusion), channel_id=1, source_target_pairs={{0,8},{4,12},{8,16},{12,20},{16,24},{20,28},{24,32},{28,36},{32,40... | collective-permute-start | bytes 983048 | tf_op jit(solution)/shard_map/ppermute | solution.py:266
  33.5 16.0 %collective-permute-start.12 = (bf16[2,80,1024]{2,1,0:T(8,128)(2,1)S(1)}, bf16[2,80,1024]{2,1,0:T(8,128)(2,1)S(1)}, u32[]{:S(2)}, u32[]{:S(2)}) collective-permute-start(bf16[2,80,1024]{2,1,0:T(8,128)(2,1)S(1)} %pad_maximum_fusion), channel_id=1, source_target_pairs={{0,56},{4,60},{8,0},{12,4},{16,8},{20,12},{24,16},{28,20},{32,24},... | collective-permute-start | bytes 983048 | tf_op jit(solution)/shard_map/ppermute | solution.py:266
  39.1 15.7 %collective-permute-start.3 = (bf16[2,32,2048]{2,1,0:T(8,128)(2,1)S(1)}, bf16[2,32,2048]{2,1,0:T(8,128)(2,1)S(1)}, u32[]{:S(2)}, u32[]{:S(2)}) collective-permute-start(bf16[2,32,2048]{2,1,0:T(8,128)(2,1)S(1)} %collective-permute-done.1), channel_id=1, source_target_pairs={{0,8},{4,12},{8,16},{12,20},{16,24},{20,28},{24,32},{28,36},{32,40... | collective-permute-start | bytes 786440 | tf_op jit(solution)/shard_map/ppermute | solution.py:266
  41.0 15.7 %collective-permute-start.4 = (bf16[2,32,2048]{2,1,0:T(8,128)(2,1)S(1)}, bf16[2,32,2048]{2,1,0:T(8,128)(2,1)S(1)}, u32[]{:S(2)}, u32[]{:S(2)}) collective-permute-start(bf16[2,32,2048]{2,1,0:T(8,128)(2,1)S(1)} %collective-permute-done.2), channel_id=1, source_target_pairs={{0,56},{4,60},{8,0},{12,4},{16,8},{20,12},{24,16},{28,20},{32,24},... | collective-permute-start | bytes 786440 | tf_op jit(solution)/shard_map/ppermute | solution.py:266
  47.6 15.7 %collective-permute-start.13 = (bf16[2,80,1024]{2,1,0:T(8,128)(2,1)S(1)}, bf16[2,80,1024]{2,1,0:T(8,128)(2,1)S(1)}, u32[]{:S(2)}, u32[]{:S(2)}) collective-permute-start(bf16[2,80,1024]{2,1,0:T(8,128)(2,1)S(1)} %collective-permute-done.11), channel_id=1, source_target_pairs={{0,8},{4,12},{8,16},{12,20},{16,24},{20,28},{24,32},{28,36},{32,40... | collective-permute-start | bytes 983048 | tf_op jit(solution)/shard_map/ppermute | solution.py:266
  49.6 15.7 %collective-permute-start.14 = (bf16[2,80,1024]{2,1,0:T(8,128)(2,1)S(1)}, bf16[2,80,1024]{2,1,0:T(8,128)(2,1)S(1)}, u32[]{:S(2)}, u32[]{:S(2)}) collective-permute-start(bf16[2,80,1024]{2,1,0:T(8,128)(2,1)S(1)} %collective-permute-done.12), channel_id=1, source_target_pairs={{0,56},{4,60},{8,0},{12,4},{16,8},{20,12},{24,16},{28,20},{32,24},... | collective-permute-start | bytes 983048 | tf_op jit(solution)/shard_map/ppermute | solution.py:266
  54.8 15.7 %collective-permute-start.5 = (bf16[2,32,2048]{2,1,0:T(8,128)(2,1)S(1)}, bf16[2,32,2048]{2,1,0:T(8,128)(2,1)S(1)}, u32[]{:S(2)}, u32[]{:S(2)}) collective-permute-start(bf16[2,32,2048]{2,1,0:T(8,128)(2,1)S(1)} %collective-permute-done.3), channel_id=1, source_target_pairs={{0,8},{4,12},{8,16},{12,20},{16,24},{20,28},{24,32},{28,36},{32,40... | collective-permute-start | bytes 786440 | tf_op jit(solution)/shard_map/ppermute | solution.py:266
  56.7 15.7 %collective-permute-start.6 = (bf16[2,32,2048]{2,1,0:T(8,128)(2,1)S(1)}, bf16[2,32,2048]{2,1,0:T(8,128)(2,1)S(1)}, u32[]{:S(2)}, u32[]{:S(2)}) collective-permute-start(bf16[2,32,2048]{2,1,0:T(8,128)(2,1)S(1)} %collective-permute-done.4), channel_id=1, source_target_pairs={{0,56},{4,60},{8,0},{12,4},{16,8},{20,12},{24,16},{28,20},{32,24},... | collective-permute-start | bytes 786440 | tf_op jit(solution)/shard_map/ppermute | solution.py:266
  63.3 19.4 %collective-permute-start.15 = (bf16[2,80,1024]{2,1,0:T(8,128)(2,1)S(1)}, bf16[2,80,1024]{2,1,0:T(8,128)(2,1)S(1)}, u32[]{:S(2)}, u32[]{:S(2)}) collective-permute-start(bf16[2,80,1024]{2,1,0:T(8,128)(2,1)S(1)} %collective-permute-done.13), channel_id=1, source_target_pairs={{0,8},{4,12},{8,16},{12,20},{16,24},{20,28},{24,32},{28,36},{32,40... | collective-permute-start | bytes 983048 | tf_op jit(solution)/shard_map/ppermute | solution.py:266
  65.3 19.4 %collective-permute-start.16 = (bf16[2,80,1024]{2,1,0:T(8,128)(2,1)S(1)}, bf16[2,80,1024]{2,1,0:T(8,128)(2,1)S(1)}, u32[]{:S(2)}, u32[]{:S(2)}) collective-permute-start(bf16[2,80,1024]{2,1,0:T(8,128)(2,1)S(1)} %collective-permute-done.14), channel_id=1, source_target_pairs={{0,56},{4,60},{8,0},{12,4},{16,8},{20,12},{24,16},{28,20},{32,24},... | collective-permute-start | bytes 983048 | tf_op jit(solution)/shard_map/ppermute | solution.py:266
  70.5 8.6 %collective-permute-start.7 = (bf16[1,32,2048]{2,1,0:T(8,128)(2,1)S(1)}, bf16[1,32,2048]{2,1,0:T(8,128)(2,1)S(1)}, u32[]{:S(2)}, u32[]{:S(2)}) collective-permute-start(bf16[1,32,2048]{2,1,0:T(8,128)(2,1)S(1)} %slice.69), channel_id=1, source_target_pairs={{0,8},{4,12},{8,16},{12,20},{16,24},{20,28},{24,32},{28,36},{32,40... | collective-permute-start | bytes 393224 | tf_op jit(solution)/shard_map/ppermute | solution.py:266
  72.5 7.6 %collective-permute-start.8 = (bf16[1,32,2048]{2,1,0:T(8,128)(2,1)S(1)}, bf16[1,32,2048]{2,1,0:T(8,128)(2,1)S(1)}, u32[]{:S(2)}, u32[]{:S(2)}) collective-permute-start(bf16[1,32,2048]{2,1,0:T(8,128)(2,1)S(1)} %slice.70), channel_id=1, source_target_pairs={{0,56},{4,60},{8,0},{12,4},{16,8},{20,12},{24,16},{28,20},{32,24},... | collective-permute-start | bytes 393224 | tf_op jit(solution)/shard_map/ppermute | solution.py:266
  80.8 17.9 %collective-permute-start.9 = (bf16[16,32,2048]{2,1,0:T(8,128)(2,1)}, bf16[16,32,2048]{2,1,0:T(8,128)(2,1)}, u32[]{:S(2)}, u32[]{:S(2)}) collective-permute-start(bf16[16,32,2048]{2,1,0:T(8,128)(2,1)} %bitcast.24.mine_ref), channel_id=1, source_target_pairs={{0,4},{4,0},{8,12},{12,8},{16,20},{20,16},{24,28},{28,24},{32,36},... | collective-permute-start | bytes 6291464 | tf_op jit(solution)/shard_map/ppermute | solution.py:269
  82.7 10.4 %collective-permute-start.17 = (bf16[1,80,1024]{2,1,0:T(8,128)(2,1)S(1)}, bf16[1,80,1024]{2,1,0:T(8,128)(2,1)S(1)}, u32[]{:S(2)}, u32[]{:S(2)}) collective-permute-start(bf16[1,80,1024]{2,1,0:T(8,128)(2,1)S(1)} %slice.71), channel_id=1, source_target_pairs={{0,8},{4,12},{8,16},{12,20},{16,24},{20,28},{24,32},{28,36},{32,40... | collective-permute-start | bytes 491528 | tf_op jit(solution)/shard_map/ppermute | solution.py:266
  84.7 9.6 %collective-permute-start.18 = (bf16[1,80,1024]{2,1,0:T(8,128)(2,1)S(1)}, bf16[1,80,1024]{2,1,0:T(8,128)(2,1)S(1)}, u32[]{:S(2)}, u32[]{:S(2)}) collective-permute-start(bf16[1,80,1024]{2,1,0:T(8,128)(2,1)S(1)} %slice.72), channel_id=1, source_target_pairs={{0,56},{4,60},{8,0},{12,4},{16,8},{20,12},{24,16},{28,20},{32,24},... | collective-permute-start | bytes 491528 | tf_op jit(solution)/shard_map/ppermute | solution.py:266
  94.3 38.6 %collective-permute-start.19 = (bf16[16,80,1024]{2,1,0:T(8,128)(2,1)S(1)}, bf16[16,80,1024]{2,1,0:T(8,128)(2,1)}, u32[]{:S(2)}, u32[]{:S(2)}) collective-permute-start(bf16[16,80,1024]{2,1,0:T(8,128)(2,1)S(1)} %bitcast.119), channel_id=1, source_target_pairs={{0,4},{4,0},{8,12},{12,8},{16,20},{20,16},{24,28},{28,24},{32,36},... | collective-permute-start | bytes 7864328 | tf_op jit(solution)/shard_map/ppermute | solution.py:269
  108.3 20.4 %all-to-all-start.4 = ((bf16[4,128,1024]{2,1,0:T(8,128)(2,1)}), bf16[4,128,1024]{2,1,0:T(8,128)(2,1)}, u32[]{:S(2)}, u32[]{:S(2)}) async-start(bf16[4,128,1024]{2,1,0:T(8,128)(2,1)} %rank_partial.12), calls=%async_computation.4 | async-start | bytes 2097152 | tf_op jit(solution)/shard_map/all_to_all | solution.py:351
  128.7 40.5 %all-to-all-start = ((bf16[4,128,1024]{2,1,0:T(8,128)(2,1)}), bf16[4,128,1024]{2,1,0:T(8,128)(2,1)}, u32[]{:S(2)}, u32[]{:S(2)}) async-start(bf16[4,128,1024]{2,1,0:T(8,128)(2,1)} %rank_partial.8), calls=%async_computation | async-start | bytes 2097152 | tf_op jit(solution)/shard_map/all_to_all | solution.py:351
  132.9 4.5 %copy-start.17 = (bf16[128,2048]{1,0:T(8,128)(2,1)S(1)}, bf16[128,2048]{1,0:T(8,128)(2,1)}, u32[]{:S(2)}) copy-start(bf16[128,2048]{1,0:T(8,128)(2,1)} %get-tuple-element.9.u_ref) | copy-start | bytes 1572868
  133.0 4.5 %copy-start.19 = (s32[1,128]{1,0:T(1,128)S(1)}, s32[1,128]{1,0:T(1,128)}, u32[]{:S(2)}) copy-start(s32[1,128]{1,0:T(1,128)} %param.12) | copy-start | bytes 1540
  133.0 4.5 %copy-start.20 = (s32[1,128]{1,0:T(1,128)S(1)}, s32[1,128]{1,0:T(1,128)}, u32[]{:S(2)}) copy-start(s32[1,128]{1,0:T(1,128)} %param.13) | copy-start | bytes 1540
  137.5 1.2 copy-start
  147.6 26.1 %copy-start.1 = (bf16[16,2,16,1024]{3,2,1,0:T(8,128)(2,1)S(1)}, bf16[16,2,16,1024]{3,2,1,0:T(8,128)(2,1)}, u32[]{:S(2)}) copy-start(bf16[16,2,16,1024]{3,2,1,0:T(8,128)(2,1)} %get-tuple-element.5) | copy-start | bytes 3145732
  147.6 26.1 %copy-start.16 = (bf16[128,2048]{1,0:T(8,128)(2,1)S(1)}, bf16[128,2048]{1,0:T(8,128)(2,1)}, u32[]{:S(2)}) copy-start(bf16[128,2048]{1,0:T(8,128)(2,1)} %get-tuple-element.8.u_ref) | copy-start | bytes 1572868
  147.6 15.7 %collective-permute-start.23 = (bf16[128,2048]{1,0:T(8,128)(2,1)}, bf16[128,2048]{1,0:T(8,128)(2,1)S(1)}, u32[]{:S(2)}, u32[]{:S(2)}) collective-permute-start(bf16[128,2048]{1,0:T(8,128)(2,1)} %input_grad.12), channel_id=1, source_target_pairs={{128,0},{256,128},{384,256},{129,1},{257,129},{385,257},{130,2},{2... | collective-permute-start | bytes 1572872 | tf_op jit(solution)/shard_map/ppermute | solution.py:312
  163.3 0.8 copy-start.6
  169.2 33.9 %all-to-all-start.5 = ((bf16[4,128,1024]{2,1,0:T(8,128)(2,1)}), bf16[4,128,1024]{2,1,0:T(8,128)(2,1)}, u32[]{:S(2)}, u32[]{:S(2)}) async-start(bf16[4,128,1024]{2,1,0:T(8,128)(2,1)} %rank_partial.13), calls=%async_computation.5 | async-start | bytes 2097152 | tf_op jit(solution)/shard_map/all_to_all | solution.py:351
  182.5 25.0 %copy-start.2 = (bf16[16,2,16,1024]{3,2,1,0:T(8,128)(2,1)S(1)}, bf16[16,2,16,1024]{3,2,1,0:T(8,128)(2,1)}, u32[]{:S(2)}) copy-start(bf16[16,2,16,1024]{3,2,1,0:T(8,128)(2,1)} %get-tuple-element.5) | copy-start | bytes 3145732
  182.5 25.0 %copy-start.7 = (bf16[128,2048]{1,0:T(8,128)(2,1)S(1)}, bf16[128,2048]{1,0:T(8,128)(2,1)}, u32[]{:S(2)}) copy-start(bf16[128,2048]{1,0:T(8,128)(2,1)} %copy-done.6) | copy-start | bytes 1572868
  182.5 14.7 %collective-permute-start.20 = (bf16[128,2048]{1,0:T(8,128)(2,1)}, bf16[128,2048]{1,0:T(8,128)(2,1)S(1)}, u32[]{:S(2)}, u32[]{:S(2)}) collective-permute-start(bf16[128,2048]{1,0:T(8,128)(2,1)} %input_grad.8), channel_id=1, source_target_pairs={{128,0},{256,128},{384,256},{129,1},{257,129},{385,257},{130,2},{2... | collective-permute-start | bytes 1572872 | tf_op jit(solution)/shard_map/ppermute | solution.py:312
  197.2 0.8 copy-start.8
  203.1 33.1 %all-to-all-start.1 = ((bf16[4,128,1024]{2,1,0:T(8,128)(2,1)}), bf16[4,128,1024]{2,1,0:T(8,128)(2,1)}, u32[]{:S(2)}, u32[]{:S(2)}) async-start(bf16[4,128,1024]{2,1,0:T(8,128)(2,1)} %rank_partial.9), calls=%async_computation.1 | async-start | bytes 2097152 | tf_op jit(solution)/shard_map/all_to_all | solution.py:351
  216.6 24.1 %copy-start.3 = (bf16[16,2,16,1024]{3,2,1,0:T(8,128)(2,1)S(1)}, bf16[16,2,16,1024]{3,2,1,0:T(8,128)(2,1)}, u32[]{:S(2)}) copy-start(bf16[16,2,16,1024]{3,2,1,0:T(8,128)(2,1)} %get-tuple-element.5) | copy-start | bytes 3145732
  216.6 24.1 %copy-start.9 = (bf16[128,2048]{1,0:T(8,128)(2,1)S(1)}, bf16[128,2048]{1,0:T(8,128)(2,1)}, u32[]{:S(2)}) copy-start(bf16[128,2048]{1,0:T(8,128)(2,1)} %copy-done.8) | copy-start | bytes 1572868
  216.6 13.7 %collective-permute-start.24 = (bf16[128,2048]{1,0:T(8,128)(2,1)}, bf16[128,2048]{1,0:T(8,128)(2,1)S(1)}, u32[]{:S(2)}, u32[]{:S(2)}) collective-permute-start(bf16[128,2048]{1,0:T(8,128)(2,1)} %input_grad.13), channel_id=1, source_target_pairs={{128,0},{256,128},{384,256},{129,1},{257,129},{385,257},{130,2},{2... | collective-permute-start | bytes 1572872 | tf_op jit(solution)/shard_map/ppermute | solution.py:312
  230.3 0.8 copy-start.10
  236.2 32.0 %all-to-all-start.6 = ((bf16[4,128,1024]{2,1,0:T(8,128)(2,1)}), bf16[4,128,1024]{2,1,0:T(8,128)(2,1)}, u32[]{:S(2)}, u32[]{:S(2)}) async-start(bf16[4,128,1024]{2,1,0:T(8,128)(2,1)} %rank_partial.14), calls=%async_computation.6 | async-start | bytes 2097152 | tf_op jit(solution)/shard_map/all_to_all | solution.py:351
  249.6 23.3 %copy-start.4 = (bf16[16,2,16,1024]{3,2,1,0:T(8,128)(2,1)S(1)}, bf16[16,2,16,1024]{3,2,1,0:T(8,128)(2,1)}, u32[]{:S(2)}) copy-start(bf16[16,2,16,1024]{3,2,1,0:T(8,128)(2,1)} %get-tuple-element.5) | copy-start | bytes 3145732
  249.6 23.3 %copy-start.11 = (bf16[128,2048]{1,0:T(8,128)(2,1)S(1)}, bf16[128,2048]{1,0:T(8,128)(2,1)}, u32[]{:S(2)}) copy-start(bf16[128,2048]{1,0:T(8,128)(2,1)} %copy-done.10) | copy-start | bytes 1572868
  249.6 12.7 %collective-permute-start.21 = (bf16[128,2048]{1,0:T(8,128)(2,1)}, bf16[128,2048]{1,0:T(8,128)(2,1)S(1)}, u32[]{:S(2)}, u32[]{:S(2)}) collective-permute-start(bf16[128,2048]{1,0:T(8,128)(2,1)} %input_grad.9), channel_id=1, source_target_pairs={{128,0},{256,128},{384,256},{129,1},{257,129},{385,257},{130,2},{2... | collective-permute-start | bytes 1572872 | tf_op jit(solution)/shard_map/ppermute | solution.py:312
  262.4 0.8 copy-start.12
  268.3 7.9 %copy-start.13 = (bf16[128,2048]{1,0:T(8,128)(2,1)S(1)}, bf16[128,2048]{1,0:T(8,128)(2,1)}, u32[]{:S(2)}) copy-start(bf16[128,2048]{1,0:T(8,128)(2,1)} %copy-done.12) | copy-start | bytes 1572868
  268.3 19.7 %all-to-all-start.2 = ((bf16[4,128,1024]{2,1,0:T(8,128)(2,1)}), bf16[4,128,1024]{2,1,0:T(8,128)(2,1)}, u32[]{:S(2)}, u32[]{:S(2)}) async-start(bf16[4,128,1024]{2,1,0:T(8,128)(2,1)} %rank_partial.10), calls=%async_computation.2 | async-start | bytes 2097152 | tf_op jit(solution)/shard_map/all_to_all | solution.py:351
  285.1 14.7 %collective-permute-start.25 = (bf16[128,2048]{1,0:T(8,128)(2,1)}, bf16[128,2048]{1,0:T(8,128)(2,1)}, u32[]{:S(2)}, u32[]{:S(2)}) collective-permute-start(bf16[128,2048]{1,0:T(8,128)(2,1)} %input_grad.14), channel_id=1, source_target_pairs={{128,0},{256,128},{384,256},{129,1},{257,129},{385,257},{130,2},{2... | collective-permute-start | bytes 1572872 | tf_op jit(solution)/shard_map/ppermute | solution.py:312
  293.6 14.3 %collective-permute-start.22 = (bf16[128,2048]{1,0:T(8,128)(2,1)}, bf16[128,2048]{1,0:T(8,128)(2,1)S(1)}, u32[]{:S(2)}, u32[]{:S(2)}) collective-permute-start(bf16[128,2048]{1,0:T(8,128)(2,1)} %input_grad.10), channel_id=1, source_target_pairs={{128,0},{256,128},{384,256},{129,1},{257,129},{385,257},{130,2},{2... | collective-permute-start | bytes 1572872 | tf_op jit(solution)/shard_map/ppermute | solution.py:312
  295.6 14.4 %copy-start.18 = (bf16[1,2,128,2048]{3,2,1,0:T(8,128)(2,1)S(1)}, bf16[1,2,128,2048]{3,2,1,0:T(8,128)(2,1)}, u32[]{:S(2)}) copy-start(bf16[1,2,128,2048]{3,2,1,0:T(8,128)(2,1)} %param.8) | copy-start | bytes 3145732
  307.9 2.1 copy-start.14
  314.0 11.7 %collective-permute-start.26 = (bf16[16,128,128]{2,1,0:T(8,128)(2,1)}, bf16[16,128,128]{2,1,0:T(8,128)(2,1)}, u32[]{:S(2)}, u32[]{:S(2)}) collective-permute-start(bf16[16,128,128]{2,1,0:T(8,128)(2,1)} %slice.101), channel_id=1, source_target_pairs={{0,4},{4,0},{8,12},{12,8},{16,20},{20,16},{24,28},{28,24},{32,36},... | collective-permute-start | bytes 1572872 | tf_op jit(solution)/shard_map/ppermute | solution.py:269
  321.0 10.8 %copy-start.5 = (bf16[16,2,16,1024]{3,2,1,0:T(8,128)(2,1)S(1)}, bf16[16,2,16,1024]{3,2,1,0:T(8,128)(2,1)}, u32[]{:S(2)}) copy-start(bf16[16,2,16,1024]{3,2,1,0:T(8,128)(2,1)} %get-tuple-element.5) | copy-start | bytes 3145732
  321.1 23.1 %all-to-all-start.7 = ((bf16[4,128,1024]{2,1,0:T(8,128)(2,1)}), bf16[4,128,1024]{2,1,0:T(8,128)(2,1)}, u32[]{:S(2)}, u32[]{:S(2)}) async-start(bf16[4,128,1024]{2,1,0:T(8,128)(2,1)} %rank_partial.15), calls=%async_computation.7 | async-start | bytes 2097152 | tf_op jit(solution)/shard_map/all_to_all | solution.py:351
  326.9 1.1 copy-start.21
  328.0 20.9 %collective-permute-start.27 = (bf16[8,128,128]{2,1,0:T(8,128)(2,1)S(1)}, bf16[8,128,128]{2,1,0:T(8,128)(2,1)S(1)}, u32[]{:S(2)}, u32[]{:S(2)}) collective-permute-start(bf16[8,128,128]{2,1,0:T(8,128)(2,1)S(1)} %slice.102), channel_id=1, source_target_pairs={{0,8},{4,12},{8,0},{12,4},{16,24},{20,28},{24,16},{28,20},{32,40},... | collective-permute-start | bytes 786440 | tf_op jit(solution)/shard_map/ppermute | solution.py:269
  335.6 5.2 %copy-start.15 = (bf16[128,2048]{1,0:T(8,128)(2,1)S(1)}, bf16[128,2048]{1,0:T(8,128)(2,1)}, u32[]{:S(2)}) copy-start(bf16[128,2048]{1,0:T(8,128)(2,1)} %copy-done.14) | copy-start | bytes 1572868
  340.8 8.0 %copy-start.22 = (f32[16,128,128]{2,1,0:T(8,128)S(1)}, f32[16,128,128]{2,1,0:T(8,128)}, u32[]{:S(2)}) copy-start(f32[16,128,128]{2,1,0:T(8,128)} %copy-done.21) | copy-start | bytes 3145732
  344.1 19.8 %all-to-all-start.3 = ((bf16[4,128,1024]{2,1,0:T(8,128)(2,1)}), bf16[4,128,1024]{2,1,0:T(8,128)(2,1)}, u32[]{:S(2)}, u32[]{:S(2)}) async-start(bf16[4,128,1024]{2,1,0:T(8,128)(2,1)} %rank_partial.11), calls=%async_computation.3 | async-start | bytes 2097152 | tf_op jit(solution)/shard_map/all_to_all | solution.py:351
  348.9 0.8 copy-start.23
  349.7 19.8 %collective-permute-start.28 = (bf16[4,128,128]{2,1,0:T(8,128)(2,1)S(1)}, bf16[4,128,128]{2,1,0:T(8,128)(2,1)S(1)}, u32[]{:S(2)}, u32[]{:S(2)}) collective-permute-start(bf16[4,128,128]{2,1,0:T(8,128)(2,1)S(1)} %slice.103), channel_id=1, source_target_pairs={{0,16},{4,20},{8,24},{12,28},{16,0},{20,4},{24,8},{28,12},{32,48},... | collective-permute-start | bytes 393224 | tf_op jit(solution)/shard_map/ppermute | solution.py:269
  370.6 10.8 %collective-permute-start.29 = (bf16[2,128,128]{2,1,0:T(8,128)(2,1)S(1)}, bf16[2,128,128]{2,1,0:T(8,128)(2,1)S(1)}, u32[]{:S(2)}, u32[]{:S(2)}) collective-permute-start(bf16[2,128,128]{2,1,0:T(8,128)(2,1)S(1)} %slice.104), channel_id=1, source_target_pairs={{0,32},{4,36},{8,40},{12,44},{16,48},{20,52},{24,56},{28,60},{32,0... | collective-permute-start | bytes 196616 | tf_op jit(solution)/shard_map/ppermute | solution.py:269
  381.4 9.7 %collective-permute-start.30 = (bf16[1,128,128]{2,1,0:T(8,128)(2,1)S(1)}, bf16[1,128,128]{2,1,0:T(8,128)(2,1)S(1)}, u32[]{:S(2)}, u32[]{:S(2)}) collective-permute-start(bf16[1,128,128]{2,1,0:T(8,128)(2,1)S(1)} %slice.105), channel_id=1, source_target_pairs={{0,64},{4,68},{8,72},{12,76},{16,80},{20,84},{24,88},{28,92},{32,9... | collective-permute-start | bytes 98312 | tf_op jit(solution)/shard_map/ppermute | solution.py:269

commit v2 on v1

v2 whole, which is shorter than its diff:
```python
import functools

import jax
import jax.numpy as jnp
from jax import lax
from jax.experimental import pallas as pl
from jax.experimental.pallas import tpu as pltpu
from jax.sharding import PartitionSpec as P

BF = jnp.bfloat16
F32 = jnp.float32
FAR = 2
CORES = 2


def granted(mib):
    return pltpu.CompilerParams(vmem_limit_bytes=int(mib * 1024 * 1024))


def times(a, b):
    return jnp.dot(a, b, preferred_element_type=F32)


def block_at(pos, size):
    return pl.ds(pl.multiple_of(pos * size, size), size)


SCALARS = pl.BlockSpec(memory_space=pltpu.SMEM)


def cost(flops, size):
    return pl.CostEstimate(flops=flops, bytes_accessed=size, transcendentals=0)


VMEM = pl.BlockSpec(memory_space=pltpu.VMEM)
HBM = pl.BlockSpec(memory_space=pltpu.HBM)


def shard_copies(core, mine_ref, other_ref, joined, sems, rows):
    chunks, step = joined.shape[0], joined.shape[1]
    sides = ((mine_ref, core), (other_ref, 1 - core))

    def copy(i, side):
        ref, at = sides[side]
        return pltpu.make_async_copy(
            ref.at[pl.ds(i * step, step), rows], joined.at[i, :, at], sems.at[i, side]
        )

    for i in range(chunks):
        for side in range(CORES):
            copy(i, side).start()

    def wait(i):
        for side in range(CORES):
            copy(i, side).wait()

    return wait


def rank_kernel(meta_ref, u_ref, mine_ref, other_ref, o_ref, u, joined, result, *sems):
    u_sem, sems, out_sems = sems
    whole = pltpu.make_async_copy(u_ref, u, u_sem)
    whole.start()
    rows = pl.ds(0, joined.shape[3])
    wait = shard_copies(meta_ref[0], mine_ref, other_ref, joined, sems, rows)
    chunks, part, _ = result.shape
    copies = o_ref.shape[0]

    def store(i, j):
        return pltpu.make_async_copy(
            result.at[i], o_ref.at[j, pl.ds(i * part, part)], out_sems.at[i, j]
        )

    whole.wait()

    def one(i, carry):
        wait(i)
        result[i] = times(joined[i].reshape(part, -1), u[...]).astype(BF)
        for j in range(copies):
            store(i, j).start()
        return carry

    lax.fori_loop(0, chunks, one, 0)
    for i in range(chunks):
        for j in range(copies):
            store(i, j).wait()


def rank_partial(meta, u, mine, other, copies):
    width, tokens = u.shape
    pieces, rows, _ = mine.shape
    rank = CORES * pieces * rows
    chunks = 2
    return pl.pallas_call(
        rank_kernel,
        in_specs=[SCALARS, HBM, HBM, HBM],
        out_specs=HBM,
        out_shape=pltpu.HBM((copies, rank, tokens), BF),
        scratch_shapes=[
            pltpu.VMEM(u.shape, BF),
            pltpu.VMEM((chunks, pieces // chunks, CORES, rows, width), BF),
            pltpu.VMEM((chunks, rank // chunks, tokens), BF),
            pltpu.SemaphoreType.DMA,
            pltpu.SemaphoreType.DMA((chunks, CORES)),
            pltpu.SemaphoreType.DMA((chunks, copies)),
        ],
        cost_estimate=cost(2 * tokens * width * rank, 2 * width * rank),
        compiler_params=granted(63),
        name="rank_partial",
    )(meta, u, mine, other)


def sparse_kernel(meta_ref, rows_ref, cols_ref, u_ref, mine_ref, other_ref, o_ref, *scratch):
    u, joined, terms, total, u_sem, sems, out_sem = scratch
    blocks, size, _ = terms.shape
    _, _, _, sub, width = joined.shape
    whole = pltpu.make_async_copy(u_ref, u, u_sem)
    whole.start()
    rows = pl.ds(mine_ref.shape[1] - sub, sub)
    wait = shard_copies(meta_ref[0], mine_ref, other_ref, joined, sems, rows)
    shift, base, group = meta_ref[2], meta_ref[3], meta_ref[4]
    total[...] = jnp.zeros_like(total)
    whole.wait()
    wait(0)

    def product(n, carry):
        value = jnp.concatenate(
            [
                joined[0, n >> 1, n & 1, :, j * size : (j + 1) * size]
                for j in range(width // size)
            ],
            axis=0,
        )
        at = block_at(cols_ref[n * group + shift] - base, size)
        terms[n] = times(value, u[at, :])
        return carry

    lax.fori_loop(0, blocks, product, 0, unroll=4)

    def place(n, carry):
        at = block_at(rows_ref[n * group + shift] - base, size)
        total[at, :] += terms[n]
        return carry

    lax.fori_loop(0, blocks, place, 0, unroll=4)
    back = pltpu.make_async_copy(total, o_ref, out_sem)
    back.start()
    back.wait()


def sparse_product(meta, rows, cols, u, mine, other, size):
    width, tokens = u.shape
    pieces, _, rank = mine.shape
    sub = size * size // rank
    return pl.pallas_call(
        sparse_kernel,
        in_specs=[SCALARS, SCALARS, SCALARS, HBM, HBM, HBM],
        out_specs=HBM,
        out_shape=pltpu.HBM((width, tokens), F32),
        scratch_shapes=[
            pltpu.VMEM(u.shape, BF),
            pltpu.VMEM((1, pieces, CORES, sub, rank), BF),
            pltpu.VMEM((CORES * pieces, size, tokens), F32),
            pltpu.VMEM((width, tokens), F32),
            pltpu.SemaphoreType.DMA,
            pltpu.SemaphoreType.DMA((1, CORES)),
            pltpu.SemaphoreType.DMA,
        ],
        cost_estimate=cost(2 * tokens * width * rank, 2 * width * rank),
        compiler_params=granted(63),
        name="sparse_product",
    )(meta, rows, cols, u, mine, other)


def input_kernel(meta_ref, p_ref, mine_ref, other_ref, s_ref, o_ref, *scratch):
    parts, joined, sparse, result, part_sems, sems, sparse_sem, out_sems = scratch
    copies = parts.shape[0]
    arrivals = [
        pltpu.make_async_copy(p_ref.at[i], parts.at[i], part_sems.at[i]) for i in range(copies)
    ]
    for arrival in arrivals:
        arrival.start()
    rows = pl.ds(0, joined.shape[3])
    wait = shard_copies(meta_ref[0], mine_ref, other_ref, joined, sems, rows)
    last = pltpu.make_async_copy(s_ref, sparse, sparse_sem)
    last.start()
    total = None
    for i, arrival in enumerate(arrivals):
        arrival.wait()
        part = parts[i].astype(F32)
        total = part if total is None else total + part
    act = total.astype(BF)
    chunks, size, _ = result.shape

    def store(i):
        return pltpu.make_async_copy(
            result.at[i], o_ref.at[pl.ds(i * size, size)], out_sems.at[i]
        )

    last.wait()

    def one(i, carry):
        wait(i)
        dense = times(joined[i].reshape(size, -1), act)
        result[i] = (dense + sparse[block_at(i, size), :]).astype(BF)
        store(i).start()
        return carry

    lax.fori_loop(0, chunks, one, 0)
    for i in range(chunks):
        store(i).wait()


def input_grad(meta, arrived, mine, other, sparse, size):
    copies, rank, tokens = arrived.shape
    pieces, total, _ = mine.shape
    rows = total - size * size // rank
    chunks = 4
    width = CORES * pieces * rows
    return pl.pallas_call(
        input_kernel,
        in_specs=[SCALARS, HBM, HBM, HBM, HBM],
        out_specs=HBM,
        out_shape=pltpu.HBM((width, tokens), BF),
        scratch_shapes=[
            pltpu.VMEM(arrived.shape, BF),
            pltpu.VMEM((chunks, pieces // chunks, CORES, rows, rank), BF),
            pltpu.VMEM(sparse.shape, F32),
            pltpu.VMEM((chunks, width // chunks, tokens), BF),
            pltpu.SemaphoreType.DMA((copies,)),
            pltpu.SemaphoreType.DMA((chunks, CORES)),
            pltpu.SemaphoreType.DMA,
            pltpu.SemaphoreType.DMA((chunks,)),
        ],
        cost_estimate=cost(2 * tokens * width * rank, 2 * width * rank),
        compiler_params=granted(63),
        name="input_grad",
    )(meta, arrived, mine, other, sparse)


def block_kernel(meta_ref, rows_ref, cols_ref, st_ref, u0_ref, u1_ref, o_ref):
    blocks, size, _ = o_ref.shape
    bits = blocks.bit_length() - 1
    place, shift, base, group = meta_ref[1], meta_ref[2], meta_ref[3], meta_ref[4]

    def one(n, carry):
        turned = jnp.int32(0)
        for bit in range(bits):
            turned = turned | (((n >> bit) & 1) << (bits - 1 - bit))
        index = (place ^ turned) * group + shift
        row_at = block_at(rows_ref[index] - base, size)
        col_at = block_at(cols_ref[index] - base, size)
        left = jnp.concatenate([u0_ref[col_at, :], u1_ref[col_at, :]], axis=1)
        right = jnp.concatenate([st_ref[0, :, row_at], st_ref[1, :, row_at]], axis=0)
        o_ref[n] = times(left, right)
        return carry

    lax.fori_loop(0, blocks, one, 0, unroll=4)


def block_products(meta, rows, cols, stash, u0, u1, blocks, size):
    batches, tokens, width = stash.shape
    return pl.pallas_call(
        block_kernel,
        in_specs=[SCALARS, SCALARS, SCALARS, VMEM, VMEM, VMEM],
        out_specs=VMEM,
        out_shape=jax.ShapeDtypeStruct((blocks, size, size), F32),
        cost_estimate=cost(2 * batches * tokens * size * size * blocks, 6 * tokens * width),
        compiler_params=granted(20),
        name="block_products",
    )(meta, rows, cols, stash, u0, u1)


def finish_kernel(slot, choices, meta_ref, *refs):
    sources, o_ref, chosen, turned, sem, out_sem = refs[:choices], *refs[-5:]
    for k, source in enumerate(sources):

        @pl.when(meta_ref[5] == k)
        def _():
            copy = pltpu.make_async_copy(source, chosen, sem)
            copy.start()
            copy.wait()

    turned[...] = chosen[...].T
    out = pltpu.make_async_copy(turned, o_ref.at[slot], out_sem)
    out.start()
    out.wait()


def finished(meta, grads, slot, slots, before):
    width, tokens = grads[0].shape
    earlier = [] if before is None else [before]
    return pl.pallas_call(
        functools.partial(finish_kernel, slot, len(grads)),
        in_specs=[SCALARS] + [HBM] * (len(grads) + len(earlier)),
        out_specs=HBM,
        out_shape=pltpu.HBM((slots, tokens, width), BF),
        scratch_shapes=[
            pltpu.VMEM((width, tokens), BF),
            pltpu.VMEM((tokens, width), BF),
            pltpu.SemaphoreType.DMA,
            pltpu.SemaphoreType.DMA,
        ],
        input_output_aliases={1 + len(grads): 0} if earlier else {},
        cost_estimate=cost(0, 4 * width * tokens),
        compiler_params=granted(63),
        name="finished",
    )(meta, *grads, *earlier)


class Data:
    def __init__(self):
        self.count = lax.axis_size("dp")
        self.ring = self.count // (FAR * CORES)
        self.place = lax.axis_index("dp")
        self.core = lax.rem(self.place, CORES)
        self.z = lax.rem(lax.div(self.place, CORES), self.ring)
        self.far = lax.div(self.place, CORES * self.ring)

    def at(self, far, z, core):
        return (far * self.ring + z % self.ring) * CORES + core

    def every(self):
        return [
            (f, z, c) for f in range(FAR) for z in range(self.ring) for c in range(CORES)
        ]

    def along(self, value, steps):
        perm = [(self.at(f, z, c), self.at(f, z + steps, c)) for f, z, c in self.every()]
        return lax.ppermute(value, "dp", perm)

    def swapped(self, value, distance):
        return lax.ppermute(value, "dp", [(p, p ^ distance) for p in range(self.count)])

    def gather(self, shard):
        got = self.swapped(shard, self.count // FAR)
        first = self.far == 0
        pair = jnp.stack([jnp.where(first, shard, got), jnp.where(first, got, shard)])
        rows, width = shard.shape
        full = jnp.zeros((FAR, self.ring, rows, width), BF)

        def put(full, piece, far, z):
            spot = (far, lax.rem(z, self.ring), 0, 0)
            return lax.dynamic_update_slice(
                full, piece[:, None], spot, allow_negative_indices=False
            )

        full = put(full, pair, 0, self.z)
        up = down = pair
        half = self.ring // 2
        for k in range(1, half):
            up = self.along(up, 1)
            down = self.along(down, -1)
            full = put(full, up, 0, self.z - k + self.ring)
            full = put(full, down, 0, self.z + k)
        up = self.along(up[:1], 1)
        down = self.along(down[1:], -1)
        full = put(full, up, 0, self.z + half)
        full = put(full, down, 1, self.z + half)
        mine = full.reshape(-1, rows, width)
        other = self.swapped(mine, 1)
        return mine, other

    def sum_at_owner(self, blocks):
        distance = 1
        while distance < self.count:
            half = blocks.shape[0] // 2
            got = self.swapped(blocks[half:].astype(BF), distance)
            blocks = blocks[:half] + got.astype(F32)
            distance *= 2
        return blocks


def pass_back(value):
    sections = lax.axis_size("section")
    return lax.ppermute(value, "section", [(i, i - 1) for i in range(1, sections)])


def pick(choices, which):
    out = choices[-1]
    for i in range(len(choices) - 1):
        out = jnp.where(which == i, choices[i], out)
    return out


def whole_step(cotangent, stash, factor_a, factor_b, block_vals, block_rows, block_cols):
    sections = lax.axis_size("section")
    section_pos = lax.axis_index("section")
    tensor_pos = lax.axis_index("tensor")
    tensor_count = lax.axis_size("tensor")
    data = Data()
    size = block_vals.shape[-1]
    rank = factor_b.shape[-1]
    batches = stash.shape[1]
    local_blocks = stash.shape[3] // size

    sub = size * size // rank
    lanes = rank // size
    packed = block_vals[0, 0].reshape(lanes, sub, size).transpose(1, 0, 2).reshape(sub, rank)
    a_mine, a_other = data.gather(factor_a[0])
    bv_mine, bv_other = data.gather(jnp.concatenate([factor_b[0], packed], axis=0))
    turn = sections - 1 - section_pos
    meta = jnp.stack(
        [
            data.core,
            data.place,
            tensor_pos,
            tensor_pos * local_blocks,
            jnp.int32(tensor_count),
            turn,
        ]
    )
    rows, cols = block_rows[0], block_cols[0]

    ups = [[cotangent[m].T] for m in range(batches)]
    grads = [[] for _ in range(batches)]
    for stage in range(sections):
        for m in range(batches):
            u = ups[m][stage]
            partial = rank_partial(meta, u, a_mine, a_other, tensor_count)
            arrived = lax.all_to_all(partial, "tensor", 0, 0, tiled=True)
            sparse = sparse_product(meta, rows, cols, u, bv_mine, bv_other, size)
            grad = input_grad(meta, arrived, bv_mine, bv_other, sparse, size)
            grads[m].append(grad)
            if stage + 1 < sections:
                ups[m].append(pass_back(grad))

    used = [pick(ups[m], turn) for m in range(batches)]
    blocks = block_products(
        meta, rows, cols, stash[0], used[0], used[1], data.count, size
    )
    block_grad = data.sum_at_owner(blocks).swapaxes(1, 2)
    grads_in = None
    for m in range(batches):
        grads_in = finished(meta, grads[m], m, batches, grads_in)
    return grads_in[None], block_grad[None]


def solution(mesh):
    in_specs = (
        P(None, "dp", "tensor"),
        P("section", None, "dp", "tensor"),
        P("section", "dp", "tensor"),
        P("section", ("tensor", "dp"), None),
        P("section", ("dp", "tensor"), None, None),
        P("section", None),
        P("section", None),
    )
    out_specs = (P("section", None, "dp", "tensor"), P("section", ("dp", "tensor"), None, None))
    return jax.shard_map(
        whole_step, mesh=mesh, in_specs=in_specs, out_specs=out_specs, check_vma=False
    )
```

time: 394 us -> 392 us (level)
  the two profiles are of different devices: /device:TPU:40 before, /device:TPU:10 now
where the time goes in v2:
time: 392 us; the launch traced here: 390 us
  starting transfers between devices  159 us (41%)
  Pallas kernels  132 us (34%)
  waiting for transfers between devices  69.2 us (18%)
  local copies, waits for them, and re-layouts  22.1 us (6%)
  other arithmetic  5.52 us (1%)
    ppermute x16, starting transfers between devices, along(): return lax.ppermute(value, 'dp', perm)  64 us
    pallas_call x8, Pallas kernels, input_grad(): pl.pallas_call(input_kernel, in_specs=[SCALARS, HBM, HBM, HBM, HBM], out_...  48.6 us
    ppermute x6, waiting for transfers between devices, pass_back(): lax.ppermute(value, 'section', [(i, i - 1) for i in range(1, sections)])  48.3 us
    all_to_all x8, starting transfers between devices, whole_step(): arrived = lax.all_to_all(partial, 'tensor', 0, 0, tiled=True)  40.4 us
    pallas_call x8, Pallas kernels, sparse_product(): pl.pallas_call(sparse_kernel, in_specs=[SCALARS, SCALARS, SCALARS, HBM, H...  38 us
    pallas_call x8, Pallas kernels, rank_partial(): pl.pallas_call(rank_kernel, in_specs=[SCALARS, HBM, HBM, HBM], out_specs=...  37.6 us
    ppermute x9, starting transfers between devices, swapped(): lax.ppermute(value, 'dp', [(p, p ^ distance) for p in range(self.count)])  35 us
    ppermute x6, starting transfers between devices, pass_back(): lax.ppermute(value, 'section', [(i, i - 1) for i in range(1, sections)])  19.5 us
  transfers between devices with their start and end apart: 39, of which 13 were waited for; matrix products, arithmetic and copies ran while one was open for 5% of the time, Pallas kernels for 33%

profile of v2, /device:TPU:10, one launch (start us, length us, event | category | flops | bytes accessed | tf_op | source)
XLA Modules:
  0.0 389.5 jit_solution(8413464047774359583)
XLA Ops:
  0.6 6.8 %collective-permute-start = (bf16[32,2048]{1,0:T(8,128)(2,1)}, bf16[32,2048]{1,0:T(8,128)(2,1)S(1)}, u32[]{:S(2)}, u32[]{:S(2)}) collective-permute-start(bf16[32,2048]{1,0:T(8,128)(2,1)} %bitcast.143), channel_id=1, source_target_pairs={{0,64},{4,68},{8,72},{12,76},{16,80},{20,84},{24,88},{28,92},{32,9... | collective-permute-start | bytes 393224 | tf_op jit(solution)/shard_map/ppermute | solution.py:333
  9.2 2.9 collective-permute-start.10
  12.2 2.3 collective-permute-done
  15.5 4.3 %collective-permute-start.1 = (bf16[2,32,2048]{2,1,0:T(8,128)(2,1)S(1)}, bf16[2,32,2048]{2,1,0:T(8,128)(2,1)S(1)}, u32[]{:S(2)}, u32[]{:S(2)}) collective-permute-start(bf16[2,32,2048]{2,1,0:T(8,128)(2,1)S(1)} %pad_maximum_fusion.1), channel_id=1, source_target_pairs={{0,8},{4,12},{8,16},{12,20},{16,24},{20,28},{24,32},{28,36},{32,40... | collective-permute-start | bytes 786440 | tf_op jit(solution)/shard_map/ppermute | solution.py:330
  19.8 8.6 %collective-permute-start.2 = (bf16[2,32,2048]{2,1,0:T(8,128)(2,1)S(1)}, bf16[2,32,2048]{2,1,0:T(8,128)(2,1)S(1)}, u32[]{:S(2)}, u32[]{:S(2)}) collective-permute-start(bf16[2,32,2048]{2,1,0:T(8,128)(2,1)S(1)} %pad_maximum_fusion.1), channel_id=1, source_target_pairs={{0,56},{4,60},{8,0},{12,4},{16,8},{20,12},{24,16},{28,20},{32,24},... | collective-permute-start | bytes 786440 | tf_op jit(solution)/shard_map/ppermute | solution.py:330
  30.7 6.4 %collective-permute-start.12 = (bf16[2,80,1024]{2,1,0:T(8,128)(2,1)S(1)}, bf16[2,80,1024]{2,1,0:T(8,128)(2,1)S(1)}, u32[]{:S(2)}, u32[]{:S(2)}) collective-permute-start(bf16[2,80,1024]{2,1,0:T(8,128)(2,1)S(1)} %pad_maximum_fusion), channel_id=1, source_target_pairs={{0,56},{4,60},{8,0},{12,4},{16,8},{20,12},{24,16},{28,20},{32,24},... | collective-permute-start | bytes 983048 | tf_op jit(solution)/shard_map/ppermute | solution.py:330
  41.6 5.1 %collective-permute-start.4 = (bf16[2,32,2048]{2,1,0:T(8,128)(2,1)S(1)}, bf16[2,32,2048]{2,1,0:T(8,128)(2,1)S(1)}, u32[]{:S(2)}, u32[]{:S(2)}) collective-permute-start(bf16[2,32,2048]{2,1,0:T(8,128)(2,1)S(1)} %collective-permute-done.2), channel_id=1, source_target_pairs={{0,56},{4,60},{8,0},{12,4},{16,8},{20,12},{24,16},{28,20},{32,24},... | collective-permute-start | bytes 786440 | tf_op jit(solution)/shard_map/ppermute | solution.py:330
  48.8 5.1 %collective-permute-start.14 = (bf16[2,80,1024]{2,1,0:T(8,128)(2,1)S(1)}, bf16[2,80,1024]{2,1,0:T(8,128)(2,1)S(1)}, u32[]{:S(2)}, u32[]{:S(2)}) collective-permute-start(bf16[2,80,1024]{2,1,0:T(8,128)(2,1)S(1)} %collective-permute-done.12), channel_id=1, source_target_pairs={{0,56},{4,60},{8,0},{12,4},{16,8},{20,12},{24,16},{28,20},{32,24},... | collective-permute-start | bytes 983048 | tf_op jit(solution)/shard_map/ppermute | solution.py:330
  57.4 5.1 %collective-permute-start.6 = (bf16[2,32,2048]{2,1,0:T(8,128)(2,1)S(1)}, bf16[2,32,2048]{2,1,0:T(8,128)(2,1)S(1)}, u32[]{:S(2)}, u32[]{:S(2)}) collective-permute-start(bf16[2,32,2048]{2,1,0:T(8,128)(2,1)S(1)} %collective-permute-done.4), channel_id=1, source_target_pairs={{0,56},{4,60},{8,0},{12,4},{16,8},{20,12},{24,16},{28,20},{32,24},... | collective-permute-start | bytes 786440 | tf_op jit(solution)/shard_map/ppermute | solution.py:330
  64.6 5.1 %collective-permute-start.16 = (bf16[2,80,1024]{2,1,0:T(8,128)(2,1)S(1)}, bf16[2,80,1024]{2,1,0:T(8,128)(2,1)S(1)}, u32[]{:S(2)}, u32[]{:S(2)}) collective-permute-start(bf16[2,80,1024]{2,1,0:T(8,128)(2,1)S(1)} %collective-permute-done.14), channel_id=1, source_target_pairs={{0,56},{4,60},{8,0},{12,4},{16,8},{20,12},{24,16},{28,20},{32,24},... | collective-permute-start | bytes 983048 | tf_op jit(solution)/shard_map/ppermute | solution.py:330
  73.2 5.1 %collective-permute-start.8 = (bf16[1,32,2048]{2,1,0:T(8,128)(2,1)S(1)}, bf16[1,32,2048]{2,1,0:T(8,128)(2,1)S(1)}, u32[]{:S(2)}, u32[]{:S(2)}) collective-permute-start(bf16[1,32,2048]{2,1,0:T(8,128)(2,1)S(1)} %slice.70), channel_id=1, source_target_pairs={{0,56},{4,60},{8,0},{12,4},{16,8},{20,12},{24,16},{28,20},{32,24},... | collective-permute-start | bytes 393224 | tf_op jit(solution)/shard_map/ppermute | solution.py:330
  84.8 5.6 %collective-permute-start.18 = (bf16[1,80,1024]{2,1,0:T(8,128)(2,1)S(1)}, bf16[1,80,1024]{2,1,0:T(8,128)(2,1)S(1)}, u32[]{:S(2)}, u32[]{:S(2)}) collective-permute-start(bf16[1,80,1024]{2,1,0:T(8,128)(2,1)S(1)} %slice.72), channel_id=1, source_target_pairs={{0,56},{4,60},{8,0},{12,4},{16,8},{20,12},{24,16},{28,20},{32,24},... | collective-permute-start | bytes 491528 | tf_op jit(solution)/shard_map/ppermute | solution.py:330
  97.0 2.1 fusion.1
  101.8 4.7 %rank_partial.12 = bf16[4,1024,128]{2,1,0:T(8,128)(2,1)} custom-call(s32[6]{0:T(128)} %stack.41.meta_ref, bf16[2048,128]{1,0:T(8,128)(2,1)} %bitcast.134, bf16[16,32,2048]{2,1,0:T(8,128)(2,1)} %bitcast.126, bf16[16,32,2048]{2,1,0:T(8,128)(2,1)} %collective-permute-done.9.other_ref), custom_call_target="tpu_custom_call" | custom-call | flops 536870912 | bytes 4194304 | tf_op jit(solution)/shard_map/rank_partial/pallas_call | solution.py:94
  106.5 4.8 %all-to-all-start.4 = ((bf16[4,1024,128]{2,1,0:T(8,128)(2,1)}), bf16[4,1024,128]{2,1,0:T(8,128)(2,1)}, u32[]{:S(2)}, u32[]{:S(2)}) async-start(bf16[4,1024,128]{2,1,0:T(8,128)(2,1)} %rank_partial.12), calls=%async_computation.4 | async-start | bytes 2097152 | tf_op jit(solution)/shard_map/all_to_all | solution.py:421
  112.4 4.7 %rank_partial.8 = bf16[4,1024,128]{2,1,0:T(8,128)(2,1)} custom-call(s32[6]{0:T(128)} %stack.41.meta_ref, bf16[2048,128]{1,0:T(8,128)(2,1)} %bitcast.136, bf16[16,32,2048]{2,1,0:T(8,128)(2,1)} %bitcast.127, bf16[16,32,2048]{2,1,0:T(8,128)(2,1)} %collective-permute-done.9.other_ref), custom_call_target="tpu_custom_call" | custom-call | flops 536870912 | bytes 4194304 | tf_op jit(solution)/shard_map/rank_partial/pallas_call | solution.py:94
  117.1 8.9 %all-to-all-done.4.p_ref = bf16[4,1024,128]{2,1,0:T(8,128)(2,1)} async-done(((bf16[4,1024,128]{2,1,0:T(8,128)(2,1)}), bf16[4,1024,128]{2,1,0:T(8,128)(2,1)}, u32[]{:S(2)}, u32[]{:S(2)}) %all-to-all-start.4) | async-done | bytes 1048608 | tf_op jit(solution)/shard_map/all_to_all | solution.py:421
  126.0 5.7 %all-to-all-start = ((bf16[4,1024,128]{2,1,0:T(8,128)(2,1)}), bf16[4,1024,128]{2,1,0:T(8,128)(2,1)}, u32[]{:S(2)}, u32[]{:S(2)}) async-start(bf16[4,1024,128]{2,1,0:T(8,128)(2,1)} %rank_partial.8), calls=%async_computation | async-start | bytes 2097152 | tf_op jit(solution)/shard_map/all_to_all | solution.py:421
  131.6 4.8 %sparse_product.12.s_ref = f32[2048,128]{1,0:T(8,128)} custom-call(s32[6]{0:T(128)} %stack.41.meta_ref, s32[128]{0:T(128)} %bitcast.107, s32[128]{0:T(128)} %bitcast.116, bf16[2048,128]{1,0:T(8,128)(2,1)} %bitcast.135, bf16[16,80,1024]{2,1,0:T(8,128)(2,1)} %bitcast.48.mine_ref, bf16[16,80,1024]{2,1,0:T(8,128)(2,1)} %collective-permute-done.19.other_ref), custom_call_target="tpu_custom_call" | custom-call | flops 536870912 | bytes 4194304 | tf_op jit(solution)/shard_map/sparse_product/pallas_call | solution.py:155
  136.4 6.1 %input_grad.12.refs_0_ = bf16[2048,128]{1,0:T(8,128)(2,1)} custom-call(s32[6]{0:T(128)} %stack.41.meta_ref, bf16[4,1024,128]{2,1,0:T(8,128)(2,1)} %all-to-all-done.4.p_ref, bf16[16,80,1024]{2,1,0:T(8,128)(2,1)} %bitcast.48.mine_ref, bf16[16,80,1024]{2,1,0:T(8,128)(2,1)} %collective-permute-done.19.other_ref, f32[2048,128]{1,0:T(8,128)} %sparse_product.12.s_ref), custom_call_target="tpu_custom_call" | custom-call | flops 536870912 | bytes 4194304 | tf_op jit(solution)/shard_map/input_grad/pallas_call | solution.py:220
  142.5 3.5 collective-permute-start.23
  145.9 11.7 %collective-permute-done.23.u_ref = bf16[2048,128]{1,0:T(8,128)(2,1)S(1)} collective-permute-done((bf16[2048,128]{1,0:T(8,128)(2,1)}, bf16[2048,128]{1,0:T(8,128)(2,1)S(1)}, u32[]{:S(2)}, u32[]{:S(2)}) %collective-permute-start.23) | collective-permute-done | bytes 524320 | tf_op jit(solution)/shard_map/ppermute | solution.py:376
  158.5 4.7 %rank_partial.13 = bf16[4,1024,128]{2,1,0:T(8,128)(2,1)} custom-call(s32[6]{0:T(128)} %stack.41.meta_ref, bf16[2048,128]{1,0:T(8,128)(2,1)} %copy-done.9, bf16[16,32,2048]{2,1,0:T(8,128)(2,1)} %bitcast.128, bf16[16,32,2048]{2,1,0:T(8,128)(2,1)} %collective-permute-done.9.other_ref), custom_call_target="tpu_custom_call" | custom-call | flops 536870912 | bytes 4194304 | tf_op jit(solution)/shard_map/rank_partial/pallas_call | solution.py:94
  163.2 4.8 %all-to-all-start.5 = ((bf16[4,1024,128]{2,1,0:T(8,128)(2,1)}), bf16[4,1024,128]{2,1,0:T(8,128)(2,1)}, u32[]{:S(2)}, u32[]{:S(2)}) async-start(bf16[4,1024,128]{2,1,0:T(8,128)(2,1)} %rank_partial.13), calls=%async_computation.5 | async-start | bytes 2097152 | tf_op jit(solution)/shard_map/all_to_all | solution.py:421
  168.0 4.7 %sparse_product.8.s_ref = f32[2048,128]{1,0:T(8,128)} custom-call(s32[6]{0:T(128)} %stack.41.meta_ref, s32[128]{0:T(128)} %bitcast.108, s32[128]{0:T(128)} %bitcast.117, bf16[2048,128]{1,0:T(8,128)(2,1)} %bitcast.137, bf16[16,80,1024]{2,1,0:T(8,128)(2,1)} %bitcast.48.mine_ref, bf16[16,80,1024]{2,1,0:T(8,128)(2,1)} %collective-permute-done.19.other_ref), custom_call_target="tpu_custom_call" | custom-call | flops 536870912 | bytes 4194304 | tf_op jit(solution)/shard_map/sparse_product/pallas_call | solution.py:155
  172.8 6.1 %input_grad.8.refs_0_ = bf16[2048,128]{1,0:T(8,128)(2,1)} custom-call(s32[6]{0:T(128)} %stack.41.meta_ref, bf16[4,1024,128]{2,1,0:T(8,128)(2,1)} %all-to-all-done.p_ref, bf16[16,80,1024]{2,1,0:T(8,128)(2,1)} %bitcast.48.mine_ref, bf16[16,80,1024]{2,1,0:T(8,128)(2,1)} %collective-permute-done.19.other_ref, f32[2048,128]{1,0:T(8,128)} %sparse_product.8.s_ref), custom_call_target="tpu_custom_call" | custom-call | flops 536870912 | bytes 4194304 | tf_op jit(solution)/shard_map/input_grad/pallas_call | solution.py:220
  178.8 3.5 collective-permute-start.20
  182.3 10.6 %collective-permute-done.20.u_ref = bf16[2048,128]{1,0:T(8,128)(2,1)S(1)} collective-permute-done((bf16[2048,128]{1,0:T(8,128)(2,1)}, bf16[2048,128]{1,0:T(8,128)(2,1)S(1)}, u32[]{:S(2)}, u32[]{:S(2)}) %collective-permute-start.20) | collective-permute-done | bytes 524320 | tf_op jit(solution)/shard_map/ppermute | solution.py:376
  193.8 4.7 %rank_partial.9 = bf16[4,1024,128]{2,1,0:T(8,128)(2,1)} custom-call(s32[6]{0:T(128)} %stack.41.meta_ref, bf16[2048,128]{1,0:T(8,128)(2,1)} %copy-done.10, bf16[16,32,2048]{2,1,0:T(8,128)(2,1)} %bitcast.129, bf16[16,32,2048]{2,1,0:T(8,128)(2,1)} %collective-permute-done.9.other_ref), custom_call_target="tpu_custom_call" | custom-call | flops 536870912 | bytes 4194304 | tf_op jit(solution)/shard_map/rank_partial/pallas_call | solution.py:94
  198.5 4.8 %all-to-all-start.1 = ((bf16[4,1024,128]{2,1,0:T(8,128)(2,1)}), bf16[4,1024,128]{2,1,0:T(8,128)(2,1)}, u32[]{:S(2)}, u32[]{:S(2)}) async-start(bf16[4,1024,128]{2,1,0:T(8,128)(2,1)} %rank_partial.9), calls=%async_computation.1 | async-start | bytes 2097152 | tf_op jit(solution)/shard_map/all_to_all | solution.py:421
  203.3 4.7 %sparse_product.13.s_ref = f32[2048,128]{1,0:T(8,128)} custom-call(s32[6]{0:T(128)} %stack.41.meta_ref, s32[128]{0:T(128)} %bitcast.109, s32[128]{0:T(128)} %bitcast.118, bf16[2048,128]{1,0:T(8,128)(2,1)} %copy-done.9, bf16[16,80,1024]{2,1,0:T(8,128)(2,1)} %bitcast.48.mine_ref, bf16[16,80,1024]{2,1,0:T(8,128)(2,1)} %collective-permute-done.19.other_ref), custom_call_target="tpu_custom_call" | custom-call | flops 536870912 | bytes 4194304 | tf_op jit(solution)/shard_map/sparse_product/pallas_call | solution.py:155
  208.0 6.1 %input_grad.13.refs_1_ = bf16[2048,128]{1,0:T(8,128)(2,1)} custom-call(s32[6]{0:T(128)} %stack.41.meta_ref, bf16[4,1024,128]{2,1,0:T(8,128)(2,1)} %all-to-all-done.5.p_ref, bf16[16,80,1024]{2,1,0:T(8,128)(2,1)} %bitcast.48.mine_ref, bf16[16,80,1024]{2,1,0:T(8,128)(2,1)} %collective-permute-done.19.other_ref, f32[2048,128]{1,0:T(8,128)} %sparse_product.13.s_ref), custom_call_target="tpu_custom_call" | custom-call | flops 536870912 | bytes 4194304 | tf_op jit(solution)/shard_map/input_grad/pallas_call | solution.py:220
  214.1 3.5 collective-permute-start.24
  217.6 9.5 %collective-permute-done.24.u_ref = bf16[2048,128]{1,0:T(8,128)(2,1)S(1)} collective-permute-done((bf16[2048,128]{1,0:T(8,128)(2,1)}, bf16[2048,128]{1,0:T(8,128)(2,1)S(1)}, u32[]{:S(2)}, u32[]{:S(2)}) %collective-permute-start.24) | collective-permute-done | bytes 524320 | tf_op jit(solution)/shard_map/ppermute | solution.py:376
  227.9 4.7 %rank_partial.14 = bf16[4,1024,128]{2,1,0:T(8,128)(2,1)} custom-call(s32[6]{0:T(128)} %stack.41.meta_ref, bf16[2048,128]{1,0:T(8,128)(2,1)} %copy-done.12, bf16[16,32,2048]{2,1,0:T(8,128)(2,1)} %bitcast.130, bf16[16,32,2048]{2,1,0:T(8,128)(2,1)} %collective-permute-done.9.other_ref), custom_call_target="tpu_custom_call" | custom-call | flops 536870912 | bytes 4194304 | tf_op jit(solution)/shard_map/rank_partial/pallas_call | solution.py:94
  232.6 4.8 %all-to-all-start.6 = ((bf16[4,1024,128]{2,1,0:T(8,128)(2,1)}), bf16[4,1024,128]{2,1,0:T(8,128)(2,1)}, u32[]{:S(2)}, u32[]{:S(2)}) async-start(bf16[4,1024,128]{2,1,0:T(8,128)(2,1)} %rank_partial.14), calls=%async_computation.6 | async-start | bytes 2097152 | tf_op jit(solution)/shard_map/all_to_all | solution.py:421
  237.4 4.7 %sparse_product.9.s_ref = f32[2048,128]{1,0:T(8,128)} custom-call(s32[6]{0:T(128)} %stack.41.meta_ref, s32[128]{0:T(128)} %bitcast.110, s32[128]{0:T(128)} %bitcast.119, bf16[2048,128]{1,0:T(8,128)(2,1)} %copy-done.10, bf16[16,80,1024]{2,1,0:T(8,128)(2,1)} %bitcast.48.mine_ref, bf16[16,80,1024]{2,1,0:T(8,128)(2,1)} %collective-permute-done.19.other_ref), custom_call_target="tpu_custom_call" | custom-call | flops 536870912 | bytes 4194304 | tf_op jit(solution)/shard_map/sparse_product/pallas_call | solution.py:155
  242.2 6.1 %input_grad.9.refs_1_ = bf16[2048,128]{1,0:T(8,128)(2,1)} custom-call(s32[6]{0:T(128)} %stack.41.meta_ref, bf16[4,1024,128]{2,1,0:T(8,128)(2,1)} %all-to-all-done.1.p_ref, bf16[16,80,1024]{2,1,0:T(8,128)(2,1)} %bitcast.48.mine_ref, bf16[16,80,1024]{2,1,0:T(8,128)(2,1)} %collective-permute-done.19.other_ref, f32[2048,128]{1,0:T(8,128)} %sparse_product.9.s_ref), custom_call_target="tpu_custom_call" | custom-call | flops 536870912 | bytes 4194304 | tf_op jit(solution)/shard_map/input_grad/pallas_call | solution.py:220
  248.3 3.5 collective-permute-start.21
  251.7 8.5 %collective-permute-done.21.u_ref = bf16[2048,128]{1,0:T(8,128)(2,1)S(1)} collective-permute-done((bf16[2048,128]{1,0:T(8,128)(2,1)}, bf16[2048,128]{1,0:T(8,128)(2,1)S(1)}, u32[]{:S(2)}, u32[]{:S(2)}) %collective-permute-start.21) | collective-permute-done | bytes 524320 | tf_op jit(solution)/shard_map/ppermute | solution.py:376
  261.0 4.7 %rank_partial.10 = bf16[4,1024,128]{2,1,0:T(8,128)(2,1)} custom-call(s32[6]{0:T(128)} %stack.41.meta_ref, bf16[2048,128]{1,0:T(8,128)(2,1)} %copy-done.13, bf16[16,32,2048]{2,1,0:T(8,128)(2,1)} %bitcast.131, bf16[16,32,2048]{2,1,0:T(8,128)(2,1)} %collective-permute-done.9.other_ref), custom_call_target="tpu_custom_call" | custom-call | flops 536870912 | bytes 4194304 | tf_op jit(solution)/shard_map/rank_partial/pallas_call | solution.py:94
  265.7 4.8 %all-to-all-start.2 = ((bf16[4,1024,128]{2,1,0:T(8,128)(2,1)}), bf16[4,1024,128]{2,1,0:T(8,128)(2,1)}, u32[]{:S(2)}, u32[]{:S(2)}) async-start(bf16[4,1024,128]{2,1,0:T(8,128)(2,1)} %rank_partial.10), calls=%async_computation.2 | async-start | bytes 2097152 | tf_op jit(solution)/shard_map/all_to_all | solution.py:421
  270.5 4.8 %sparse_product.14.s_ref = f32[2048,128]{1,0:T(8,128)} custom-call(s32[6]{0:T(128)} %stack.41.meta_ref, s32[128]{0:T(128)} %bitcast.111, s32[128]{0:T(128)} %bitcast.120, bf16[2048,128]{1,0:T(8,128)(2,1)} %copy-done.12, bf16[16,80,1024]{2,1,0:T(8,128)(2,1)} %bitcast.48.mine_ref, bf16[16,80,1024]{2,1,0:T(8,128)(2,1)} %collective-permute-done.19.other_ref), custom_call_target="tpu_custom_call" | custom-call | flops 536870912 | bytes 4194304 | tf_op jit(solution)/shard_map/sparse_product/pallas_call | solution.py:155
  275.3 6.1 %input_grad.14.refs_2_ = bf16[2048,128]{1,0:T(8,128)(2,1)} custom-call(s32[6]{0:T(128)} %stack.41.meta_ref, bf16[4,1024,128]{2,1,0:T(8,128)(2,1)} %all-to-all-done.6.p_ref, bf16[16,80,1024]{2,1,0:T(8,128)(2,1)} %bitcast.48.mine_ref, bf16[16,80,1024]{2,1,0:T(8,128)(2,1)} %collective-permute-done.19.other_ref, f32[2048,128]{1,0:T(8,128)} %sparse_product.14.s_ref), custom_call_target="tpu_custom_call" | custom-call | flops 536870912 | bytes 4194304 | tf_op jit(solution)/shard_map/input_grad/pallas_call | solution.py:220
  281.4 3.5 collective-permute-start.25
  284.9 4.8 %sparse_product.10.s_ref = f32[2048,128]{1,0:T(8,128)} custom-call(s32[6]{0:T(128)} %stack.41.meta_ref, s32[128]{0:T(128)} %bitcast.112, s32[128]{0:T(128)} %bitcast.121, bf16[2048,128]{1,0:T(8,128)(2,1)} %copy-done.13, bf16[16,80,1024]{2,1,0:T(8,128)(2,1)} %bitcast.48.mine_ref, bf16[16,80,1024]{2,1,0:T(8,128)(2,1)} %collective-permute-done.19.other_ref), custom_call_target="tpu_custom_call" | custom-call | flops 536870912 | bytes 4194304 | tf_op jit(solution)/shard_map/sparse_product/pallas_call | solution.py:155
  289.7 6.2 %input_grad.10.refs_2_ = bf16[2048,128]{1,0:T(8,128)(2,1)} custom-call(s32[6]{0:T(128)} %stack.41.meta_ref, bf16[4,1024,128]{2,1,0:T(8,128)(2,1)} %all-to-all-done.2.p_ref, bf16[16,80,1024]{2,1,0:T(8,128)(2,1)} %bitcast.48.mine_ref, bf16[16,80,1024]{2,1,0:T(8,128)(2,1)} %collective-permute-done.19.other_ref, f32[2048,128]{1,0:T(8,128)} %sparse_product.10.s_ref), custom_call_target="tpu_custom_call" | custom-call | flops 536870912 | bytes 4194304 | tf_op jit(solution)/shard_map/input_grad/pallas_call | solution.py:220
  299.4 7.9 %collective-permute-done.22.u_ref = bf16[2048,128]{1,0:T(8,128)(2,1)} collective-permute-done((bf16[2048,128]{1,0:T(8,128)(2,1)}, bf16[2048,128]{1,0:T(8,128)(2,1)}, u32[]{:S(2)}, u32[]{:S(2)}) %collective-permute-start.22) | collective-permute-done | bytes 524320 | tf_op jit(solution)/shard_map/ppermute | solution.py:376
  308.6 2.7 block_products.1
  315.4 4.7 %rank_partial.15 = bf16[4,1024,128]{2,1,0:T(8,128)(2,1)} custom-call(s32[6]{0:T(128)} %stack.41.meta_ref, bf16[2048,128]{1,0:T(8,128)(2,1)} %collective-permute-done.25.u_ref, bf16[16,32,2048]{2,1,0:T(8,128)(2,1)} %bitcast.132, bf16[16,32,2048]{2,1,0:T(8,128)(2,1)} %collective-permute-done.9.other_ref), custom_call_target="tpu_custom_call" | custom-call | flops 536870912 | bytes 4194304 | tf_op jit(solution)/shard_map/rank_partial/pallas_call | solution.py:94
  320.1 5.0 %all-to-all-start.7 = ((bf16[4,1024,128]{2,1,0:T(8,128)(2,1)}), bf16[4,1024,128]{2,1,0:T(8,128)(2,1)}, u32[]{:S(2)}, u32[]{:S(2)}) async-start(bf16[4,1024,128]{2,1,0:T(8,128)(2,1)} %rank_partial.15), calls=%async_computation.7 | async-start | bytes 2097152 | tf_op jit(solution)/shard_map/all_to_all | solution.py:421
  326.3 4.0 %collective-permute-start.27 = (bf16[8,128,128]{2,1,0:T(8,128)(2,1)S(1)}, bf16[8,128,128]{2,1,0:T(8,128)(2,1)S(1)}, u32[]{:S(2)}, u32[]{:S(2)}) collective-permute-start(bf16[8,128,128]{2,1,0:T(8,128)(2,1)S(1)} %slice.96), channel_id=1, source_target_pairs={{0,8},{4,12},{8,0},{12,4},{16,24},{20,28},{24,16},{28,20},{32,40},... | collective-permute-start | bytes 786440 | tf_op jit(solution)/shard_map/ppermute | solution.py:333
  330.3 4.7 %rank_partial.11 = bf16[4,1024,128]{2,1,0:T(8,128)(2,1)} custom-call(s32[6]{0:T(128)} %stack.41.meta_ref, bf16[2048,128]{1,0:T(8,128)(2,1)} %collective-permute-done.22.u_ref, bf16[16,32,2048]{2,1,0:T(8,128)(2,1)} %bitcast.133, bf16[16,32,2048]{2,1,0:T(8,128)(2,1)} %collective-permute-done.9.other_ref), custom_call_target="tpu_custom_call" | custom-call | flops 536870912 | bytes 4194304 | tf_op jit(solution)/shard_map/rank_partial/pallas_call | solution.py:94
  335.0 4.5 %all-to-all-done.7.p_ref = bf16[4,1024,128]{2,1,0:T(8,128)(2,1)} async-done(((bf16[4,1024,128]{2,1,0:T(8,128)(2,1)}), bf16[4,1024,128]{2,1,0:T(8,128)(2,1)}, u32[]{:S(2)}, u32[]{:S(2)}) %all-to-all-start.7) | async-done | bytes 1048608 | tf_op jit(solution)/shard_map/all_to_all | solution.py:421
  339.5 5.7 %all-to-all-start.3 = ((bf16[4,1024,128]{2,1,0:T(8,128)(2,1)}), bf16[4,1024,128]{2,1,0:T(8,128)(2,1)}, u32[]{:S(2)}, u32[]{:S(2)}) async-start(bf16[4,1024,128]{2,1,0:T(8,128)(2,1)} %rank_partial.11), calls=%async_computation.3 | async-start | bytes 2097152 | tf_op jit(solution)/shard_map/all_to_all | solution.py:421
  345.3 5.2 %collective-permute-start.28 = (bf16[4,128,128]{2,1,0:T(8,128)(2,1)S(1)}, bf16[4,128,128]{2,1,0:T(8,128)(2,1)S(1)}, u32[]{:S(2)}, u32[]{:S(2)}) collective-permute-start(bf16[4,128,128]{2,1,0:T(8,128)(2,1)S(1)} %slice.97), channel_id=1, source_target_pairs={{0,16},{4,20},{8,24},{12,28},{16,0},{20,4},{24,8},{28,12},{32,48},... | collective-permute-start | bytes 393224 | tf_op jit(solution)/shard_map/ppermute | solution.py:333
  350.4 4.7 %sparse_product.15.s_ref = f32[2048,128]{1,0:T(8,128)} custom-call(s32[6]{0:T(128)} %stack.41.meta_ref, s32[128]{0:T(128)} %bitcast.113, s32[128]{0:T(128)} %bitcast.122, bf16[2048,128]{1,0:T(8,128)(2,1)} %collective-permute-done.25.u_ref, bf16[16,80,1024]{2,1,0:T(8,128)(2,1)} %bitcast.48.mine_ref, bf16[16,80,1024]{2,1,0:T(8,128)(2,1)} %collective-permute-done.19.other_ref), custom_call_target="tpu_custom_call" | custom-call | flops 536870912 | bytes 4194304 | tf_op jit(solution)/shard_map/sparse_product/pallas_call | solution.py:155
  356.0 4.6 %collective-permute-start.29 = (bf16[2,128,128]{2,1,0:T(8,128)(2,1)S(1)}, bf16[2,128,128]{2,1,0:T(8,128)(2,1)S(1)}, u32[]{:S(2)}, u32[]{:S(2)}) collective-permute-start(bf16[2,128,128]{2,1,0:T(8,128)(2,1)S(1)} %slice.98), channel_id=1, source_target_pairs={{0,32},{4,36},{8,40},{12,44},{16,48},{20,52},{24,56},{28,60},{32,0... | collective-permute-start | bytes 196616 | tf_op jit(solution)/shard_map/ppermute | solution.py:333
  360.7 4.8 %sparse_product.11.s_ref = f32[2048,128]{1,0:T(8,128)} custom-call(s32[6]{0:T(128)} %stack.41.meta_ref, s32[128]{0:T(128)} %bitcast.114, s32[128]{0:T(128)} %bitcast.123, bf16[2048,128]{1,0:T(8,128)(2,1)} %collective-permute-done.22.u_ref, bf16[16,80,1024]{2,1,0:T(8,128)(2,1)} %bitcast.48.mine_ref, bf16[16,80,1024]{2,1,0:T(8,128)(2,1)} %collective-permute-done.19.other_ref), custom_call_target="tpu_custom_call" | custom-call | flops 536870912 | bytes 4194304 | tf_op jit(solution)/shard_map/sparse_product/pallas_call | solution.py:155
  365.4 6.0 %input_grad.15.refs_3_ = bf16[2048,128]{1,0:T(8,128)(2,1)} custom-call(s32[6]{0:T(128)} %stack.41.meta_ref, bf16[4,1024,128]{2,1,0:T(8,128)(2,1)} %all-to-all-done.7.p_ref, bf16[16,80,1024]{2,1,0:T(8,128)(2,1)} %bitcast.48.mine_ref, bf16[16,80,1024]{2,1,0:T(8,128)(2,1)} %collective-permute-done.19.other_ref, f32[2048,128]{1,0:T(8,128)} %sparse_product.15.s_ref), custom_call_target="tpu_custom_call" | custom-call | flops 536870912 | bytes 4194304 | tf_op jit(solution)/shard_map/input_grad/pallas_call | solution.py:220
  371.5 2.7 finished.2.refs_4_
  374.2 5.7 %collective-permute-start.30 = (bf16[1,128,128]{2,1,0:T(8,128)(2,1)S(1)}, bf16[1,128,128]{2,1,0:T(8,128)(2,1)S(1)}, u32[]{:S(2)}, u32[]{:S(2)}) collective-permute-start(bf16[1,128,128]{2,1,0:T(8,128)(2,1)S(1)} %slice.99), channel_id=1, source_target_pairs={{0,64},{4,68},{8,72},{12,76},{16,80},{20,84},{24,88},{28,92},{32,9... | collective-permute-start | bytes 98312 | tf_op jit(solution)/shard_map/ppermute | solution.py:333
  380.0 6.1 %input_grad.11.refs_3_ = bf16[2048,128]{1,0:T(8,128)(2,1)} custom-call(s32[6]{0:T(128)} %stack.41.meta_ref, bf16[4,1024,128]{2,1,0:T(8,128)(2,1)} %all-to-all-done.3.p_ref, bf16[16,80,1024]{2,1,0:T(8,128)(2,1)} %bitcast.48.mine_ref, bf16[16,80,1024]{2,1,0:T(8,128)(2,1)} %collective-permute-done.19.other_ref, f32[2048,128]{1,0:T(8,128)} %sparse_product.11.s_ref), custom_call_target="tpu_custom_call" | custom-call | flops 536870912 | bytes 4194304 | tf_op jit(solution)/shard_map/input_grad/pallas_call | solution.py:220
  386.0 2.7 finished.3
  (124 shorter events, 51.9 us)
Async XLA Ops:
  0.6 13.9 %collective-permute-start = (bf16[32,2048]{1,0:T(8,128)(2,1)}, bf16[32,2048]{1,0:T(8,128)(2,1)S(1)}, u32[]{:S(2)}, u32[]{:S(2)}) collective-permute-start(bf16[32,2048]{1,0:T(8,128)(2,1)} %bitcast.143), channel_id=1, source_target_pairs={{0,64},{4,68},{8,72},{12,76},{16,80},{20,84},{24,88},{28,92},{32,9... | collective-permute-start | bytes 393224 | tf_op jit(solution)/shard_map/ppermute | solution.py:333
  7.5 21.2 %copy-start.17 = (bf16[1,64,1024]{2,1,0:T(8,128)(2,1)S(1)}, bf16[1,64,1024]{2,1,0:T(8,128)(2,1)}, u32[]{:S(2)}) copy-start(bf16[1,64,1024]{2,1,0:T(8,128)(2,1)} %param.10) | copy-start | bytes 393220
  9.2 19.5 %collective-permute-start.10 = (bf16[80,1024]{1,0:T(8,128)(2,1)S(1)}, bf16[80,1024]{1,0:T(8,128)(2,1)S(1)}, u32[]{:S(2)}, u32[]{:S(2)}) collective-permute-start(bf16[80,1024]{1,0:T(8,128)(2,1)S(1)} %pad_maximum_fusion.2), channel_id=1, source_target_pairs={{0,64},{4,68},{8,72},{12,76},{16,80},{20,84},{24,88},{28,92},{32,9... | collective-permute-start | bytes 491528 | tf_op jit(solution)/shard_map/ppermute | solution.py:333
  15.5 24.2 %collective-permute-start.1 = (bf16[2,32,2048]{2,1,0:T(8,128)(2,1)S(1)}, bf16[2,32,2048]{2,1,0:T(8,128)(2,1)S(1)}, u32[]{:S(2)}, u32[]{:S(2)}) collective-permute-start(bf16[2,32,2048]{2,1,0:T(8,128)(2,1)S(1)} %pad_maximum_fusion.1), channel_id=1, source_target_pairs={{0,8},{4,12},{8,16},{12,20},{16,24},{20,28},{24,32},{28,36},{32,40... | collective-permute-start | bytes 786440 | tf_op jit(solution)/shard_map/ppermute | solution.py:330
  19.8 21.8 %collective-permute-start.2 = (bf16[2,32,2048]{2,1,0:T(8,128)(2,1)S(1)}, bf16[2,32,2048]{2,1,0:T(8,128)(2,1)S(1)}, u32[]{:S(2)}, u32[]{:S(2)}) collective-permute-start(bf16[2,32,2048]{2,1,0:T(8,128)(2,1)S(1)} %pad_maximum_fusion.1), channel_id=1, source_target_pairs={{0,56},{4,60},{8,0},{12,4},{16,8},{20,12},{24,16},{28,20},{32,24},... | collective-permute-start | bytes 786440 | tf_op jit(solution)/shard_map/ppermute | solution.py:330
  28.8 18.1 %collective-permute-start.11 = (bf16[2,80,1024]{2,1,0:T(8,128)(2,1)S(1)}, bf16[2,80,1024]{2,1,0:T(8,128)(2,1)S(1)}, u32[]{:S(2)}, u32[]{:S(2)}) collective-permute-start(bf16[2,80,1024]{2,1,0:T(8,128)(2,1)S(1)} %pad_maximum_fusion), channel_id=1, source_target_pairs={{0,8},{4,12},{8,16},{12,20},{16,24},{20,28},{24,32},{28,36},{32,40... | collective-permute-start | bytes 983048 | tf_op jit(solution)/shard_map/ppermute | solution.py:330
  30.7 18.1 %collective-permute-start.12 = (bf16[2,80,1024]{2,1,0:T(8,128)(2,1)S(1)}, bf16[2,80,1024]{2,1,0:T(8,128)(2,1)S(1)}, u32[]{:S(2)}, u32[]{:S(2)}) collective-permute-start(bf16[2,80,1024]{2,1,0:T(8,128)(2,1)S(1)} %pad_maximum_fusion), channel_id=1, source_target_pairs={{0,56},{4,60},{8,0},{12,4},{16,8},{20,12},{24,16},{28,20},{32,24},... | collective-permute-start | bytes 983048 | tf_op jit(solution)/shard_map/ppermute | solution.py:330
  39.7 15.8 %collective-permute-start.3 = (bf16[2,32,2048]{2,1,0:T(8,128)(2,1)S(1)}, bf16[2,32,2048]{2,1,0:T(8,128)(2,1)S(1)}, u32[]{:S(2)}, u32[]{:S(2)}) collective-permute-start(bf16[2,32,2048]{2,1,0:T(8,128)(2,1)S(1)} %collective-permute-done.1), channel_id=1, source_target_pairs={{0,8},{4,12},{8,16},{12,20},{16,24},{20,28},{24,32},{28,36},{32,40... | collective-permute-start | bytes 786440 | tf_op jit(solution)/shard_map/ppermute | solution.py:330
  41.6 15.7 %collective-permute-start.4 = (bf16[2,32,2048]{2,1,0:T(8,128)(2,1)S(1)}, bf16[2,32,2048]{2,1,0:T(8,128)(2,1)S(1)}, u32[]{:S(2)}, u32[]{:S(2)}) collective-permute-start(bf16[2,32,2048]{2,1,0:T(8,128)(2,1)S(1)} %collective-permute-done.2), channel_id=1, source_target_pairs={{0,56},{4,60},{8,0},{12,4},{16,8},{20,12},{24,16},{28,20},{32,24},... | collective-permute-start | bytes 786440 | tf_op jit(solution)/shard_map/ppermute | solution.py:330
  46.9 15.7 %collective-permute-start.13 = (bf16[2,80,1024]{2,1,0:T(8,128)(2,1)S(1)}, bf16[2,80,1024]{2,1,0:T(8,128)(2,1)S(1)}, u32[]{:S(2)}, u32[]{:S(2)}) collective-permute-start(bf16[2,80,1024]{2,1,0:T(8,128)(2,1)S(1)} %collective-permute-done.11), channel_id=1, source_target_pairs={{0,8},{4,12},{8,16},{12,20},{16,24},{20,28},{24,32},{28,36},{32,40... | collective-permute-start | bytes 983048 | tf_op jit(solution)/shard_map/ppermute | solution.py:330
  48.8 15.7 %collective-permute-start.14 = (bf16[2,80,1024]{2,1,0:T(8,128)(2,1)S(1)}, bf16[2,80,1024]{2,1,0:T(8,128)(2,1)S(1)}, u32[]{:S(2)}, u32[]{:S(2)}) collective-permute-start(bf16[2,80,1024]{2,1,0:T(8,128)(2,1)S(1)} %collective-permute-done.12), channel_id=1, source_target_pairs={{0,56},{4,60},{8,0},{12,4},{16,8},{20,12},{24,16},{28,20},{32,24},... | collective-permute-start | bytes 983048 | tf_op jit(solution)/shard_map/ppermute | solution.py:330
  55.5 15.7 %collective-permute-start.5 = (bf16[2,32,2048]{2,1,0:T(8,128)(2,1)S(1)}, bf16[2,32,2048]{2,1,0:T(8,128)(2,1)S(1)}, u32[]{:S(2)}, u32[]{:S(2)}) collective-permute-start(bf16[2,32,2048]{2,1,0:T(8,128)(2,1)S(1)} %collective-permute-done.3), channel_id=1, source_target_pairs={{0,8},{4,12},{8,16},{12,20},{16,24},{20,28},{24,32},{28,36},{32,40... | collective-permute-start | bytes 786440 | tf_op jit(solution)/shard_map/ppermute | solution.py:330
  57.4 15.8 %collective-permute-start.6 = (bf16[2,32,2048]{2,1,0:T(8,128)(2,1)S(1)}, bf16[2,32,2048]{2,1,0:T(8,128)(2,1)S(1)}, u32[]{:S(2)}, u32[]{:S(2)}) collective-permute-start(bf16[2,32,2048]{2,1,0:T(8,128)(2,1)S(1)} %collective-permute-done.4), channel_id=1, source_target_pairs={{0,56},{4,60},{8,0},{12,4},{16,8},{20,12},{24,16},{28,20},{32,24},... | collective-permute-start | bytes 786440 | tf_op jit(solution)/shard_map/ppermute | solution.py:330
  62.6 20.2 %collective-permute-start.15 = (bf16[2,80,1024]{2,1,0:T(8,128)(2,1)S(1)}, bf16[2,80,1024]{2,1,0:T(8,128)(2,1)S(1)}, u32[]{:S(2)}, u32[]{:S(2)}) collective-permute-start(bf16[2,80,1024]{2,1,0:T(8,128)(2,1)S(1)} %collective-permute-done.13), channel_id=1, source_target_pairs={{0,8},{4,12},{8,16},{12,20},{16,24},{20,28},{24,32},{28,36},{32,40... | collective-permute-start | bytes 983048 | tf_op jit(solution)/shard_map/ppermute | solution.py:330
  64.6 20.2 %collective-permute-start.16 = (bf16[2,80,1024]{2,1,0:T(8,128)(2,1)S(1)}, bf16[2,80,1024]{2,1,0:T(8,128)(2,1)S(1)}, u32[]{:S(2)}, u32[]{:S(2)}) collective-permute-start(bf16[2,80,1024]{2,1,0:T(8,128)(2,1)S(1)} %collective-permute-done.14), channel_id=1, source_target_pairs={{0,56},{4,60},{8,0},{12,4},{16,8},{20,12},{24,16},{28,20},{32,24},... | collective-permute-start | bytes 983048 | tf_op jit(solution)/shard_map/ppermute | solution.py:330
  71.2 8.1 %collective-permute-start.7 = (bf16[1,32,2048]{2,1,0:T(8,128)(2,1)S(1)}, bf16[1,32,2048]{2,1,0:T(8,128)(2,1)S(1)}, u32[]{:S(2)}, u32[]{:S(2)}) collective-permute-start(bf16[1,32,2048]{2,1,0:T(8,128)(2,1)S(1)} %slice.69), channel_id=1, source_target_pairs={{0,8},{4,12},{8,16},{12,20},{16,24},{20,28},{24,32},{28,36},{32,40... | collective-permute-start | bytes 393224 | tf_op jit(solution)/shard_map/ppermute | solution.py:330
  73.2 7.6 %collective-permute-start.8 = (bf16[1,32,2048]{2,1,0:T(8,128)(2,1)S(1)}, bf16[1,32,2048]{2,1,0:T(8,128)(2,1)S(1)}, u32[]{:S(2)}, u32[]{:S(2)}) collective-permute-start(bf16[1,32,2048]{2,1,0:T(8,128)(2,1)S(1)} %slice.70), channel_id=1, source_target_pairs={{0,56},{4,60},{8,0},{12,4},{16,8},{20,12},{24,16},{28,20},{32,24},... | collective-permute-start | bytes 393224 | tf_op jit(solution)/shard_map/ppermute | solution.py:330
  80.8 18.3 %copy-start.6 = (bf16[2,8,32,2048]{3,2,1,0:T(8,128)(2,1)}, bf16[2,8,32,2048]{3,2,1,0:T(8,128)(2,1)S(1)}, u32[]{:S(2)}) copy-start(bf16[2,8,32,2048]{3,2,1,0:T(8,128)(2,1)S(1)} %bitcast_dynamic-update-slice_fusion.16) | copy-start | bytes 6291460
  80.8 21.0 %collective-permute-start.9 = (bf16[16,32,2048]{2,1,0:T(8,128)(2,1)S(1)}, bf16[16,32,2048]{2,1,0:T(8,128)(2,1)}, u32[]{:S(2)}, u32[]{:S(2)}) collective-permute-start(bf16[16,32,2048]{2,1,0:T(8,128)(2,1)S(1)} %bitcast.125), channel_id=1, source_target_pairs={{0,4},{4,0},{8,12},{12,8},{16,20},{20,16},{24,28},{28,24},{32,36},... | collective-permute-start | bytes 6291464 | tf_op jit(solution)/shard_map/ppermute | solution.py:333
  82.8 10.4 %collective-permute-start.17 = (bf16[1,80,1024]{2,1,0:T(8,128)(2,1)S(1)}, bf16[1,80,1024]{2,1,0:T(8,128)(2,1)S(1)}, u32[]{:S(2)}, u32[]{:S(2)}) collective-permute-start(bf16[1,80,1024]{2,1,0:T(8,128)(2,1)S(1)} %slice.71), channel_id=1, source_target_pairs={{0,8},{4,12},{8,16},{12,20},{16,24},{20,28},{24,32},{28,36},{32,40... | collective-permute-start | bytes 491528 | tf_op jit(solution)/shard_map/ppermute | solution.py:330
  84.8 9.7 %collective-permute-start.18 = (bf16[1,80,1024]{2,1,0:T(8,128)(2,1)S(1)}, bf16[1,80,1024]{2,1,0:T(8,128)(2,1)S(1)}, u32[]{:S(2)}, u32[]{:S(2)}) collective-permute-start(bf16[1,80,1024]{2,1,0:T(8,128)(2,1)S(1)} %slice.72), channel_id=1, source_target_pairs={{0,56},{4,60},{8,0},{12,4},{16,8},{20,12},{24,16},{28,20},{32,24},... | collective-permute-start | bytes 491528 | tf_op jit(solution)/shard_map/ppermute | solution.py:330
  95.1 36.5 %collective-permute-start.19 = (bf16[16,80,1024]{2,1,0:T(8,128)(2,1)}, bf16[16,80,1024]{2,1,0:T(8,128)(2,1)}, u32[]{:S(2)}, u32[]{:S(2)}) collective-permute-start(bf16[16,80,1024]{2,1,0:T(8,128)(2,1)} %bitcast.48.mine_ref), channel_id=1, source_target_pairs={{0,4},{4,0},{8,12},{12,8},{16,20},{20,16},{24,28},{28,24},{32,36},... | collective-permute-start | bytes 7864328 | tf_op jit(solution)/shard_map/ppermute | solution.py:333
  106.5 19.5 %all-to-all-start.4 = ((bf16[4,1024,128]{2,1,0:T(8,128)(2,1)}), bf16[4,1024,128]{2,1,0:T(8,128)(2,1)}, u32[]{:S(2)}, u32[]{:S(2)}) async-start(bf16[4,1024,128]{2,1,0:T(8,128)(2,1)} %rank_partial.12), calls=%async_computation.4 | async-start | bytes 2097152 | tf_op jit(solution)/shard_map/all_to_all | solution.py:421
  126.0 37.3 %all-to-all-start = ((bf16[4,1024,128]{2,1,0:T(8,128)(2,1)}), bf16[4,1024,128]{2,1,0:T(8,128)(2,1)}, u32[]{:S(2)}, u32[]{:S(2)}) async-start(bf16[4,1024,128]{2,1,0:T(8,128)(2,1)} %rank_partial.8), calls=%async_computation | async-start | bytes 2097152 | tf_op jit(solution)/shard_map/all_to_all | solution.py:421
  142.5 15.2 %collective-permute-start.23 = (bf16[2048,128]{1,0:T(8,128)(2,1)}, bf16[2048,128]{1,0:T(8,128)(2,1)S(1)}, u32[]{:S(2)}, u32[]{:S(2)}) collective-permute-start(bf16[2048,128]{1,0:T(8,128)(2,1)} %input_grad.12.refs_0_), channel_id=1, source_target_pairs={{128,0},{256,128},{384,256},{129,1},{257,129},{385,257},{130,2},{2... | collective-permute-start | bytes 1572872 | tf_op jit(solution)/shard_map/ppermute | solution.py:376
  157.7 0.8 copy-start.9
  163.2 35.2 %all-to-all-start.5 = ((bf16[4,1024,128]{2,1,0:T(8,128)(2,1)}), bf16[4,1024,128]{2,1,0:T(8,128)(2,1)}, u32[]{:S(2)}, u32[]{:S(2)}) async-start(bf16[4,1024,128]{2,1,0:T(8,128)(2,1)} %rank_partial.13), calls=%async_computation.5 | async-start | bytes 2097152 | tf_op jit(solution)/shard_map/all_to_all | solution.py:421
  178.8 14.1 %collective-permute-start.20 = (bf16[2048,128]{1,0:T(8,128)(2,1)}, bf16[2048,128]{1,0:T(8,128)(2,1)S(1)}, u32[]{:S(2)}, u32[]{:S(2)}) collective-permute-start(bf16[2048,128]{1,0:T(8,128)(2,1)} %input_grad.8.refs_0_), channel_id=1, source_target_pairs={{128,0},{256,128},{384,256},{129,1},{257,129},{385,257},{130,2},{2... | collective-permute-start | bytes 1572872 | tf_op jit(solution)/shard_map/ppermute | solution.py:376
  193.0 0.8 copy-start.10
  198.5 34.1 %all-to-all-start.1 = ((bf16[4,1024,128]{2,1,0:T(8,128)(2,1)}), bf16[4,1024,128]{2,1,0:T(8,128)(2,1)}, u32[]{:S(2)}, u32[]{:S(2)}) async-start(bf16[4,1024,128]{2,1,0:T(8,128)(2,1)} %rank_partial.9), calls=%async_computation.1 | async-start | bytes 2097152 | tf_op jit(solution)/shard_map/all_to_all | solution.py:421
  214.1 13.0 %collective-permute-start.24 = (bf16[2048,128]{1,0:T(8,128)(2,1)}, bf16[2048,128]{1,0:T(8,128)(2,1)S(1)}, u32[]{:S(2)}, u32[]{:S(2)}) collective-permute-start(bf16[2048,128]{1,0:T(8,128)(2,1)} %input_grad.13.refs_1_), channel_id=1, source_target_pairs={{128,0},{256,128},{384,256},{129,1},{257,129},{385,257},{130,2},{2... | collective-permute-start | bytes 1572872 | tf_op jit(solution)/shard_map/ppermute | solution.py:376
  227.1 0.8 copy-start.12
  232.6 33.1 %all-to-all-start.6 = ((bf16[4,1024,128]{2,1,0:T(8,128)(2,1)}), bf16[4,1024,128]{2,1,0:T(8,128)(2,1)}, u32[]{:S(2)}, u32[]{:S(2)}) async-start(bf16[4,1024,128]{2,1,0:T(8,128)(2,1)} %rank_partial.14), calls=%async_computation.6 | async-start | bytes 2097152 | tf_op jit(solution)/shard_map/all_to_all | solution.py:421
  248.3 12.0 %collective-permute-start.21 = (bf16[2048,128]{1,0:T(8,128)(2,1)}, bf16[2048,128]{1,0:T(8,128)(2,1)S(1)}, u32[]{:S(2)}, u32[]{:S(2)}) collective-permute-start(bf16[2048,128]{1,0:T(8,128)(2,1)} %input_grad.9.refs_1_), channel_id=1, source_target_pairs={{128,0},{256,128},{384,256},{129,1},{257,129},{385,257},{130,2},{2... | collective-permute-start | bytes 1572872 | tf_op jit(solution)/shard_map/ppermute | solution.py:376
  260.2 0.8 copy-start.13
  265.7 23.9 %all-to-all-start.2 = ((bf16[4,1024,128]{2,1,0:T(8,128)(2,1)}), bf16[4,1024,128]{2,1,0:T(8,128)(2,1)}, u32[]{:S(2)}, u32[]{:S(2)}) async-start(bf16[4,1024,128]{2,1,0:T(8,128)(2,1)} %rank_partial.10), calls=%async_computation.2 | async-start | bytes 2097152 | tf_op jit(solution)/shard_map/all_to_all | solution.py:421
  281.4 16.6 %collective-permute-start.25 = (bf16[2048,128]{1,0:T(8,128)(2,1)}, bf16[2048,128]{1,0:T(8,128)(2,1)}, u32[]{:S(2)}, u32[]{:S(2)}) collective-permute-start(bf16[2048,128]{1,0:T(8,128)(2,1)} %input_grad.14.refs_2_), channel_id=1, source_target_pairs={{128,0},{256,128},{384,256},{129,1},{257,129},{385,257},{130,2},{2... | collective-permute-start | bytes 1572872 | tf_op jit(solution)/shard_map/ppermute | solution.py:376
  289.6 8.4 %copy-start.7 = (bf16[1,128,2048]{1,2,0:T(8,128)(2,1)S(1)}, bf16[1,128,2048]{1,2,0:T(8,128)(2,1)}, u32[]{:S(2)}) copy-start(bf16[1,128,2048]{1,2,0:T(8,128)(2,1)} %copy.29) | copy-start | bytes 1572868
  295.8 11.5 %copy-start.8 = (bf16[1,128,2048]{1,2,0:T(8,128)(2,1)S(1)}, bf16[1,128,2048]{1,2,0:T(8,128)(2,1)}, u32[]{:S(2)}) copy-start(bf16[1,128,2048]{1,2,0:T(8,128)(2,1)} %copy.28) | copy-start | bytes 1572868
  295.9 11.5 %collective-permute-start.22 = (bf16[2048,128]{1,0:T(8,128)(2,1)}, bf16[2048,128]{1,0:T(8,128)(2,1)}, u32[]{:S(2)}, u32[]{:S(2)}) collective-permute-start(bf16[2048,128]{1,0:T(8,128)(2,1)} %input_grad.10.refs_2_), channel_id=1, source_target_pairs={{128,0},{256,128},{384,256},{129,1},{257,129},{385,257},{130,2},{2... | collective-permute-start | bytes 1572872 | tf_op jit(solution)/shard_map/ppermute | solution.py:376
  297.9 9.5 %copy-start.11 = (bf16[2048,128]{1,0:T(8,128)(2,1)S(1)}, bf16[2048,128]{1,0:T(8,128)(2,1)}, u32[]{:S(2)}) copy-start(bf16[2048,128]{1,0:T(8,128)(2,1)} %copy-done.10) | copy-start | bytes 1572868
  297.9 9.5 %copy-start.14 = (bf16[2048,128]{1,0:T(8,128)(2,1)S(1)}, bf16[2048,128]{1,0:T(8,128)(2,1)}, u32[]{:S(2)}) copy-start(bf16[2048,128]{1,0:T(8,128)(2,1)} %copy-done.13) | copy-start | bytes 1572868
  297.9 10.6 %copy-start.2 = (bf16[1,2,128,2048]{3,2,1,0:T(8,128)(2,1)S(1)}, bf16[1,2,128,2048]{3,2,1,0:T(8,128)(2,1)}, u32[]{:S(2)}) copy-start(bf16[1,2,128,2048]{3,2,1,0:T(8,128)(2,1)} %param.8) | copy-start | bytes 3145732
  298.0 10.6 %copy-start.3 = (s32[6]{0:T(128)S(1)}, s32[6]{0:T(128)}, u32[]{:S(2)}) copy-start(s32[6]{0:T(128)} %stack.41.meta_ref) | copy-start | bytes 76
  298.0 10.6 %copy-start.4 = (s32[1,128]{1,0:T(1,128)S(1)}, s32[1,128]{1,0:T(1,128)}, u32[]{:S(2)}) copy-start(s32[1,128]{1,0:T(1,128)} %param.12) | copy-start | bytes 1540
  298.0 10.6 %copy-start.5 = (s32[1,128]{1,0:T(1,128)S(1)}, s32[1,128]{1,0:T(1,128)}, u32[]{:S(2)}) copy-start(s32[1,128]{1,0:T(1,128)} %param.13) | copy-start | bytes 1540
  311.2 1.3 copy-start
  313.5 11.6 %collective-permute-start.26 = (bf16[16,128,128]{2,1,0:T(8,128)(2,1)}, bf16[16,128,128]{2,1,0:T(8,128)(2,1)S(1)}, u32[]{:S(2)}, u32[]{:S(2)}) collective-permute-start(bf16[16,128,128]{2,1,0:T(8,128)(2,1)} %slice.95), channel_id=1, source_target_pairs={{0,4},{4,0},{8,12},{12,8},{16,20},{20,16},{24,28},{28,24},{32,36},... | collective-permute-start | bytes 1572872 | tf_op jit(solution)/shard_map/ppermute | solution.py:333
  320.1 5.0 %copy-start.1 = (f32[32,128,128]{2,1,0:T(8,128)S(1)}, f32[32,128,128]{2,1,0:T(8,128)}, u32[]{:S(2)}) copy-start(f32[32,128,128]{2,1,0:T(8,128)} %copy-done) | copy-start | bytes 6291460
  320.1 19.4 %all-to-all-start.7 = ((bf16[4,1024,128]{2,1,0:T(8,128)(2,1)}), bf16[4,1024,128]{2,1,0:T(8,128)(2,1)}, u32[]{:S(2)}, u32[]{:S(2)}) async-start(bf16[4,1024,128]{2,1,0:T(8,128)(2,1)} %rank_partial.15), calls=%async_computation.7 | async-start | bytes 2097152 | tf_op jit(solution)/shard_map/all_to_all | solution.py:421
  325.2 1.0 copy-start.15
  326.3 18.9 %collective-permute-start.27 = (bf16[8,128,128]{2,1,0:T(8,128)(2,1)S(1)}, bf16[8,128,128]{2,1,0:T(8,128)(2,1)S(1)}, u32[]{:S(2)}, u32[]{:S(2)}) collective-permute-start(bf16[8,128,128]{2,1,0:T(8,128)(2,1)S(1)} %slice.96), channel_id=1, source_target_pairs={{0,8},{4,12},{8,0},{12,4},{16,24},{20,28},{24,16},{28,20},{32,40},... | collective-permute-start | bytes 786440 | tf_op jit(solution)/shard_map/ppermute | solution.py:333
  335.0 10.2 %copy-start.16 = (f32[16,128,128]{2,1,0:T(8,128)S(1)}, f32[16,128,128]{2,1,0:T(8,128)}, u32[]{:S(2)}) copy-start(f32[16,128,128]{2,1,0:T(8,128)} %copy-done.15) | copy-start | bytes 3145732
  339.5 40.5 %all-to-all-start.3 = ((bf16[4,1024,128]{2,1,0:T(8,128)(2,1)}), bf16[4,1024,128]{2,1,0:T(8,128)(2,1)}, u32[]{:S(2)}, u32[]{:S(2)}) async-start(bf16[4,1024,128]{2,1,0:T(8,128)(2,1)} %rank_partial.11), calls=%async_computation.3 | async-start | bytes 2097152 | tf_op jit(solution)/shard_map/all_to_all | solution.py:421
  345.3 10.7 %collective-permute-start.28 = (bf16[4,128,128]{2,1,0:T(8,128)(2,1)S(1)}, bf16[4,128,128]{2,1,0:T(8,128)(2,1)S(1)}, u32[]{:S(2)}, u32[]{:S(2)}) collective-permute-start(bf16[4,128,128]{2,1,0:T(8,128)(2,1)S(1)} %slice.97), channel_id=1, source_target_pairs={{0,16},{4,20},{8,24},{12,28},{16,0},{20,4},{24,8},{28,12},{32,48},... | collective-permute-start | bytes 393224 | tf_op jit(solution)/shard_map/ppermute | solution.py:333
  356.0 18.2 %collective-permute-start.29 = (bf16[2,128,128]{2,1,0:T(8,128)(2,1)S(1)}, bf16[2,128,128]{2,1,0:T(8,128)(2,1)S(1)}, u32[]{:S(2)}, u32[]{:S(2)}) collective-permute-start(bf16[2,128,128]{2,1,0:T(8,128)(2,1)S(1)} %slice.98), channel_id=1, source_target_pairs={{0,32},{4,36},{8,40},{12,44},{16,48},{20,52},{24,56},{28,60},{32,0... | collective-permute-start | bytes 196616 | tf_op jit(solution)/shard_map/ppermute | solution.py:333
  374.2 14.5 %collective-permute-start.30 = (bf16[1,128,128]{2,1,0:T(8,128)(2,1)S(1)}, bf16[1,128,128]{2,1,0:T(8,128)(2,1)S(1)}, u32[]{:S(2)}, u32[]{:S(2)}) collective-permute-start(bf16[1,128,128]{2,1,0:T(8,128)(2,1)S(1)} %slice.99), channel_id=1, source_target_pairs={{0,64},{4,68},{8,72},{12,76},{16,80},{20,84},{24,88},{28,92},{32,9... | collective-permute-start | bytes 98312 | tf_op jit(solution)/shard_map/ppermute | solution.py:333

commit v3 on v2

--- a/solution.py
+++ b/solution.py
@@ -25,6 +25,7 @@
     return pl.ds(pl.multiple_of(pos * size, size), size)
 
 
+HELD = 40
 SCALARS = pl.BlockSpec(memory_space=pltpu.SMEM)
 
 
@@ -110,8 +111,55 @@
     )(meta, u, mine, other)
 
 
-def sparse_kernel(meta_ref, rows_ref, cols_ref, u_ref, mine_ref, other_ref, o_ref, *scratch):
-    u, joined, terms, total, u_sem, sems, out_sem = scratch
+def held_kernel(u_ref, a_ref, o_ref, u, result, u_sem, out_sems):
+    whole = pltpu.make_async_copy(u_ref, u, u_sem)
+    whole.start()
+    chunks, part, _ = result.shape
+    copies = o_ref.shape[0]
+    step = a_ref.shape[0] // chunks
+
+    def store(i, j):
+        return pltpu.make_async_copy(
+            result.at[i], o_ref.at[j, pl.ds(i * part, part)], out_sems.at[i, j]
+        )
+
+    whole.wait()
+    for i in range(chunks):
+        weight = a_ref[i * step : (i + 1) * step].reshape(part, -1)
+        result[i] = times(weight, u[...]).astype(BF)
+        for j in range(copies):
+            store(i, j).start()
+    for i in range(chunks):
+        for j in range(copies):
+            store(i, j).wait()
+
+
+def rank_held(u, weight, copies):
+    width, tokens = u.shape
+    pieces, cores, rows, _ = weight.shape
+    rank = pieces * cores * rows
+    chunks = 2
+    return pl.pallas_call(
+        held_kernel,
+        in_specs=[HBM, VMEM],
+        out_specs=HBM,
+        out_shape=pltpu.HBM((copies, rank, tokens), BF),
+        scratch_shapes=[
+            pltpu.VMEM(u.shape, BF),
+            pltpu.VMEM((chunks, rank // chunks, tokens), BF),
+            pltpu.SemaphoreType.DMA,
+            pltpu.SemaphoreType.DMA((chunks, copies)),
+        ],
+        cost_estimate=cost(2 * tokens * width * rank, 2 * width * rank),
+        compiler_params=granted(HELD),
+        name="rank_held",
+    )(u, weight)
+
+
+def sparse_kernel(
+    hold, meta_ref, rows_ref, cols_ref, u_ref, mine_ref, other_ref, a_mine, a_other, o_ref, *rest
+):
+    u, joined, terms, total, u_sem, sems, out_sem, held_sems = rest[-8:]
     blocks, size, _ = terms.shape
     _, _, _, sub, width = joined.shape
     whole = pltpu.make_async_copy(u_ref, u, u_sem)
@@ -119,6 +167,14 @@
     rows = pl.ds(mine_ref.shape[1] - sub, sub)
     wait = shard_copies(meta_ref[0], mine_ref, other_ref, joined, sems, rows)
     shift, base, group = meta_ref[2], meta_ref[3], meta_ref[4]
+    if hold:
+        core = meta_ref[0]
+        held = [
+            pltpu.make_async_copy(ref, rest[0].at[:, at], held_sems.at[side])
+            for side, (ref, at) in enumerate(((a_mine, core), (a_other, 1 - core)))
+        ]
+        for copy in held:
+            copy.start()
     total[...] = jnp.zeros_like(total)
     whole.wait()
     wait(0)
@@ -146,17 +202,22 @@
     back = pltpu.make_async_copy(total, o_ref, out_sem)
     back.start()
     back.wait()
-
-
-def sparse_product(meta, rows, cols, u, mine, other, size):
+    if hold:
+        for copy in held:
+            copy.wait()
+
+
+def sparse_product(meta, rows, cols, u, mine, other, a_mine, a_other, size, hold):
     width, tokens = u.shape
+    a_pieces, a_rows, _ = a_mine.shape
     pieces, _, rank = mine.shape
     sub = size * size // rank
-    return pl.pallas_call(
-        sparse_kernel,
-        in_specs=[SCALARS, SCALARS, SCALARS, HBM, HBM, HBM],
-        out_specs=HBM,
-        out_shape=pltpu.HBM((width, tokens), F32),
+    held = [pltpu.VMEM((a_pieces, CORES, a_rows, width), BF)] if hold else []
+    out = pl.pallas_call(
+        functools.partial(sparse_kernel, hold),
+        in_specs=[SCALARS, SCALARS, SCALARS, HBM, HBM, HBM, HBM, HBM],
+        out_specs=[HBM] + [VMEM] * len(held),
+        out_shape=[pltpu.HBM((width, tokens), F32)] + held,
         scratch_shapes=[
             pltpu.VMEM(u.shape, BF),
             pltpu.VMEM((1, pieces, CORES, sub, rank), BF),
@@ -165,11 +226,13 @@
             pltpu.SemaphoreType.DMA,
             pltpu.SemaphoreType.DMA((1, CORES)),
             pltpu.SemaphoreType.DMA,
+            pltpu.SemaphoreType.DMA((CORES,)),
         ],
         cost_estimate=cost(2 * tokens * width * rank, 2 * width * rank),
-        compiler_params=granted(63),
+        compiler_params=granted(HELD),
         name="sparse_product",
-    )(meta, rows, cols, u, mine, other)
+    )(meta, rows, cols, u, mine, other, a_mine, a_other)
+    return out if hold else (out[0], None)
 
 
 def input_kernel(meta_ref, p_ref, mine_ref, other_ref, s_ref, o_ref, *scratch):
@@ -180,10 +243,10 @@
     ]
     for arrival in arrivals:
         arrival.start()
+    last = pltpu.make_async_copy(s_ref, sparse, sparse_sem)
+    last.start()
     rows = pl.ds(0, joined.shape[3])
     wait = shard_copies(meta_ref[0], mine_ref, other_ref, joined, sems, rows)
-    last = pltpu.make_async_copy(s_ref, sparse, sparse_sem)
-    last.start()
     total = None
     for i, arrival in enumerate(arrivals):
         arrival.wait()
@@ -414,12 +477,20 @@
 
     ups = [[cotangent[m].T] for m in range(batches)]
     grads = [[] for _ in range(batches)]
+    held = None
     for stage in range(sections):
         for m in range(batches):
             u = ups[m][stage]
-            partial = rank_partial(meta, u, a_mine, a_other, tensor_count)
+            if held is None or stage == 0:
+                partial = rank_partial(meta, u, a_mine, a_other, tensor_count)
+            else:
+                partial = rank_held(u, held, tensor_count)
             arrived = lax.all_to_all(partial, "tensor", 0, 0, tiled=True)
-            sparse = sparse_product(meta, rows, cols, u, bv_mine, bv_other, size)
+            last = stage + 1 == sections and m + 1 == batches
+            hold = not last and (stage, m) != (0, 0)
+            sparse, held = sparse_product(
+                meta, rows, cols, u, bv_mine, bv_other, a_mine, a_other, size, hold
+            )
             grad = input_grad(meta, arrived, bv_mine, bv_other, sparse, size)
             grads[m].append(grad)
             if stage + 1 < sections:

time: 392 us -> 365 us (0.931)
  waiting for transfers between devices: 69.2 us -> 40.9 us
  local copies, waits for them, and re-layouts: 22.1 us -> 37.2 us
  Pallas kernels: 132 us -> 117 us
    ppermute x6, waiting for transfers between devices: 48.3 us -> 19 us  [pass_back(): lax.ppermute(value, 'section', [(i, i - 1) for i in range(1, sections)])]
    pallas_call x8 -> x2, Pallas kernels: 37.6 us -> 9.54 us  [rank_partial(): pl.pallas_call(rank_kernel, in_specs=[SCALARS, HBM, HBM, HBM], out_specs=...]
    unnamed x39 -> x79, local copies, waits for them, and re-layouts: 9.44 us -> 24.4 us
    pallas_call x8 -> x14, Pallas kernels: 38 us -> 51.3 us  [the longest x8 36.1 us: sparse_product(): pl.pallas_call(functools.partial(sparse_kernel, hold), in_specs=[SCALARS,...]
    ppermute x9, waiting for transfers between devices: 3.15 us -> 7.93 us  [swapped(): lax.ppermute(value, 'dp', [(p, p ^ distance) for p in range(self.count)])]
  transfers between devices with their start and end apart: 39 -> 39, of which waited for: 13 -> 13; matrix products, arithmetic and copies ran while one was open for 5% -> 6% of each run, Pallas kernels for 33% -> 31%
where the time goes in v3:
time: 365 us; the launch traced here: 363 us
  starting transfers between devices  159 us (44%)
  Pallas kernels  117 us (32%)
  waiting for transfers between devices  40.9 us (11%)
  local copies, waits for them, and re-layouts  37.2 us (10%)
  other arithmetic  6.79 us (2%)
    ppermute x16, starting transfers between devices, along(): return lax.ppermute(value, 'dp', perm)  63.9 us
    pallas_call x8, Pallas kernels, input_grad(): pl.pallas_call(input_kernel, in_specs=[SCALARS, HBM, HBM, HBM, HBM], out_...  47.8 us
    all_to_all x8, starting transfers between devices, whole_step(): arrived = lax.all_to_all(partial, 'tensor', 0, 0, tiled=True)  40.3 us
    pallas_call x8, Pallas kernels, sparse_product(): pl.pallas_call(functools.partial(sparse_kernel, hold), in_specs=[SCALARS,...  36.1 us
    ppermute x9, starting transfers between devices, swapped(): lax.ppermute(value, 'dp', [(p, p ^ distance) for p in range(self.count)])  35.3 us
    unnamed x79, local copies, waits for them, and re-layouts  24.4 us
    ppermute x6, starting transfers between devices, pass_back(): lax.ppermute(value, 'section', [(i, i - 1) for i in range(1, sections)])  19.6 us
    ppermute x6, waiting for transfers between devices, pass_back(): lax.ppermute(value, 'section', [(i, i - 1) for i in range(1, sections)])  19 us
  transfers between devices with their start and end apart: 39, of which 13 were waited for; matrix products, arithmetic and copies ran while one was open for 6% of the time, Pallas kernels for 31%

profile of v3, /device:TPU:10, one launch (start us, length us, event | category | flops | bytes accessed | tf_op | source)
XLA Modules:
  0.0 362.6 jit_solution(5115239584779664863)
XLA Ops:
  0.6 7.0 %collective-permute-start = (bf16[32,2048]{1,0:T(8,128)(2,1)}, bf16[32,2048]{1,0:T(8,128)(2,1)S(1)}, u32[]{:S(2)}, u32[]{:S(2)}) collective-permute-start(bf16[32,2048]{1,0:T(8,128)(2,1)} %bitcast.145), channel_id=1, source_target_pairs={{0,64},{4,68},{8,72},{12,76},{16,80},{20,84},{24,88},{28,92},{32,9... | collective-permute-start | bytes 393224 | tf_op jit(solution)/shard_map/ppermute | solution.py:396
  9.3 2.9 collective-permute-start.10
  12.3 2.4 collective-permute-done
  15.6 4.3 %collective-permute-start.1 = (bf16[2,32,2048]{2,1,0:T(8,128)(2,1)S(1)}, bf16[2,32,2048]{2,1,0:T(8,128)(2,1)S(1)}, u32[]{:S(2)}, u32[]{:S(2)}) collective-permute-start(bf16[2,32,2048]{2,1,0:T(8,128)(2,1)S(1)} %pad_maximum_fusion.1), channel_id=1, source_target_pairs={{0,8},{4,12},{8,16},{12,20},{16,24},{20,28},{24,32},{28,36},{32,40... | collective-permute-start | bytes 786440 | tf_op jit(solution)/shard_map/ppermute | solution.py:393
  19.9 8.6 %collective-permute-start.2 = (bf16[2,32,2048]{2,1,0:T(8,128)(2,1)S(1)}, bf16[2,32,2048]{2,1,0:T(8,128)(2,1)S(1)}, u32[]{:S(2)}, u32[]{:S(2)}) collective-permute-start(bf16[2,32,2048]{2,1,0:T(8,128)(2,1)S(1)} %pad_maximum_fusion.1), channel_id=1, source_target_pairs={{0,56},{4,60},{8,0},{12,4},{16,8},{20,12},{24,16},{28,20},{32,24},... | collective-permute-start | bytes 786440 | tf_op jit(solution)/shard_map/ppermute | solution.py:393
  30.9 6.4 %collective-permute-start.12 = (bf16[2,80,1024]{2,1,0:T(8,128)(2,1)S(1)}, bf16[2,80,1024]{2,1,0:T(8,128)(2,1)S(1)}, u32[]{:S(2)}, u32[]{:S(2)}) collective-permute-start(bf16[2,80,1024]{2,1,0:T(8,128)(2,1)S(1)} %pad_maximum_fusion), channel_id=1, source_target_pairs={{0,56},{4,60},{8,0},{12,4},{16,8},{20,12},{24,16},{28,20},{32,24},... | collective-permute-start | bytes 983048 | tf_op jit(solution)/shard_map/ppermute | solution.py:393
  41.9 5.1 %collective-permute-start.4 = (bf16[2,32,2048]{2,1,0:T(8,128)(2,1)S(1)}, bf16[2,32,2048]{2,1,0:T(8,128)(2,1)S(1)}, u32[]{:S(2)}, u32[]{:S(2)}) collective-permute-start(bf16[2,32,2048]{2,1,0:T(8,128)(2,1)S(1)} %collective-permute-done.2), channel_id=1, source_target_pairs={{0,56},{4,60},{8,0},{12,4},{16,8},{20,12},{24,16},{28,20},{32,24},... | collective-permute-start | bytes 786440 | tf_op jit(solution)/shard_map/ppermute | solution.py:393
  49.0 5.1 %collective-permute-start.14 = (bf16[2,80,1024]{2,1,0:T(8,128)(2,1)S(1)}, bf16[2,80,1024]{2,1,0:T(8,128)(2,1)S(1)}, u32[]{:S(2)}, u32[]{:S(2)}) collective-permute-start(bf16[2,80,1024]{2,1,0:T(8,128)(2,1)S(1)} %collective-permute-done.12), channel_id=1, source_target_pairs={{0,56},{4,60},{8,0},{12,4},{16,8},{20,12},{24,16},{28,20},{32,24},... | collective-permute-start | bytes 983048 | tf_op jit(solution)/shard_map/ppermute | solution.py:393
  57.6 5.1 %collective-permute-start.6 = (bf16[2,32,2048]{2,1,0:T(8,128)(2,1)S(1)}, bf16[2,32,2048]{2,1,0:T(8,128)(2,1)S(1)}, u32[]{:S(2)}, u32[]{:S(2)}) collective-permute-start(bf16[2,32,2048]{2,1,0:T(8,128)(2,1)S(1)} %collective-permute-done.4), channel_id=1, source_target_pairs={{0,56},{4,60},{8,0},{12,4},{16,8},{20,12},{24,16},{28,20},{32,24},... | collective-permute-start | bytes 786440 | tf_op jit(solution)/shard_map/ppermute | solution.py:393
  64.8 5.1 %collective-permute-start.16 = (bf16[2,80,1024]{2,1,0:T(8,128)(2,1)S(1)}, bf16[2,80,1024]{2,1,0:T(8,128)(2,1)S(1)}, u32[]{:S(2)}, u32[]{:S(2)}) collective-permute-start(bf16[2,80,1024]{2,1,0:T(8,128)(2,1)S(1)} %collective-permute-done.14), channel_id=1, source_target_pairs={{0,56},{4,60},{8,0},{12,4},{16,8},{20,12},{24,16},{28,20},{32,24},... | collective-permute-start | bytes 983048 | tf_op jit(solution)/shard_map/ppermute | solution.py:393
  73.4 5.1 %collective-permute-start.8 = (bf16[1,32,2048]{2,1,0:T(8,128)(2,1)S(1)}, bf16[1,32,2048]{2,1,0:T(8,128)(2,1)S(1)}, u32[]{:S(2)}, u32[]{:S(2)}) collective-permute-start(bf16[1,32,2048]{2,1,0:T(8,128)(2,1)S(1)} %slice.70), channel_id=1, source_target_pairs={{0,56},{4,60},{8,0},{12,4},{16,8},{20,12},{24,16},{28,20},{32,24},... | collective-permute-start | bytes 393224 | tf_op jit(solution)/shard_map/ppermute | solution.py:393
  85.0 5.6 %collective-permute-start.18 = (bf16[1,80,1024]{2,1,0:T(8,128)(2,1)S(1)}, bf16[1,80,1024]{2,1,0:T(8,128)(2,1)S(1)}, u32[]{:S(2)}, u32[]{:S(2)}) collective-permute-start(bf16[1,80,1024]{2,1,0:T(8,128)(2,1)S(1)} %slice.72), channel_id=1, source_target_pairs={{0,56},{4,60},{8,0},{12,4},{16,8},{20,12},{24,16},{28,20},{32,24},... | collective-permute-start | bytes 491528 | tf_op jit(solution)/shard_map/ppermute | solution.py:393
  97.3 2.1 fusion.1
  102.0 4.7 %rank_partial.3 = bf16[4,1024,128]{2,1,0:T(8,128)(2,1)} custom-call(s32[6]{0:T(128)} %stack.41.meta_ref, bf16[2048,128]{1,0:T(8,128)(2,1)} %bitcast.117, bf16[16,32,2048]{2,1,0:T(8,128)(2,1)} %bitcast.107, bf16[16,32,2048]{2,1,0:T(8,128)(2,1)} %collective-permute-done.9.other_ref.a_other), custom_call_target="tpu_custom_call" | custom-call | flops 536870912 | bytes 4194304 | tf_op jit(solution)/shard_map/rank_partial/pallas_call | solution.py:95
  106.8 4.8 %all-to-all-start.1 = ((bf16[4,1024,128]{2,1,0:T(8,128)(2,1)}), bf16[4,1024,128]{2,1,0:T(8,128)(2,1)}, u32[]{:S(2)}, u32[]{:S(2)}) async-start(bf16[4,1024,128]{2,1,0:T(8,128)(2,1)} %rank_partial.3), calls=%async_computation.1 | async-start | bytes 2097152 | tf_op jit(solution)/shard_map/all_to_all | solution.py:488
  112.6 4.8 %rank_partial.2 = bf16[4,1024,128]{2,1,0:T(8,128)(2,1)} custom-call(s32[6]{0:T(128)} %stack.41.meta_ref, bf16[2048,128]{1,0:T(8,128)(2,1)} %bitcast.119, bf16[16,32,2048]{2,1,0:T(8,128)(2,1)} %bitcast.108, bf16[16,32,2048]{2,1,0:T(8,128)(2,1)} %collective-permute-done.9.other_ref.a_other), custom_call_target="tpu_custom_call" | custom-call | flops 536870912 | bytes 4194304 | tf_op jit(solution)/shard_map/rank_partial/pallas_call | solution.py:95
  117.5 8.7 %all-to-all-done.1.p_ref = bf16[4,1024,128]{2,1,0:T(8,128)(2,1)} async-done(((bf16[4,1024,128]{2,1,0:T(8,128)(2,1)}), bf16[4,1024,128]{2,1,0:T(8,128)(2,1)}, u32[]{:S(2)}, u32[]{:S(2)}) %all-to-all-start.1) | async-done | bytes 1048608 | tf_op jit(solution)/shard_map/all_to_all | solution.py:488
  126.2 5.7 %all-to-all-start = ((bf16[4,1024,128]{2,1,0:T(8,128)(2,1)}), bf16[4,1024,128]{2,1,0:T(8,128)(2,1)}, u32[]{:S(2)}, u32[]{:S(2)}) async-start(bf16[4,1024,128]{2,1,0:T(8,128)(2,1)} %rank_partial.2), calls=%async_computation | async-start | bytes 2097152 | tf_op jit(solution)/shard_map/all_to_all | solution.py:488
  131.9 4.5 %sparse_product.9.s_ref = f32[2048,128]{1,0:T(8,128)} custom-call(s32[6]{0:T(128)S(1)} %copy-done.27, s32[128]{0:T(128)S(1)} %bitcast.122, s32[128]{0:T(128)S(1)} %bitcast.131, bf16[2048,128]{1,0:T(8,128)(2,1)S(1)} %bitcast.118, bf16[16,80,1024]{2,1,0:T(8,128)(2,1)} %bitcast.48.mine_ref, bf16[16,80,1024]{2,1,0:T(8,128)(2,1)} %collective-permute-done.19.other_ref, ...), custom_call_target="tpu_custom_call" | custom-call | flops 536870912 | bytes 4194304 | tf_op jit(solution)/shard_map/sparse_product/pallas_call | solution.py:216
  136.4 6.0 %input_grad.9.refs_0_ = bf16[2048,128]{1,0:T(8,128)(2,1)} custom-call(s32[6]{0:T(128)} %stack.41.meta_ref, bf16[4,1024,128]{2,1,0:T(8,128)(2,1)} %all-to-all-done.1.p_ref, bf16[16,80,1024]{2,1,0:T(8,128)(2,1)} %bitcast.48.mine_ref, bf16[16,80,1024]{2,1,0:T(8,128)(2,1)} %collective-permute-done.19.other_ref, f32[2048,128]{1,0:T(8,128)} %sparse_product.9.s_ref), custom_call_target="tpu_custom_call" | custom-call | flops 536870912 | bytes 4194304 | tf_op jit(solution)/shard_map/input_grad/pallas_call | solution.py:283
  142.4 3.5 collective-permute-start.21
  148.5 4.5 %sparse_product.8 = (f32[2048,128]{1,0:T(8,128)}, bf16[16,2,32,2048]{3,2,1,0:T(8,128)(2,1)S(1)}) custom-call(s32[6]{0:T(128)S(1)} %copy-done.28, s32[128]{0:T(128)S(1)} %bitcast.123, s32[128]{0:T(128)S(1)} %bitcast.132, bf16[2048,128]{1,0:T(8,128)(2,1)S(1)} %bitcast.120, bf16[16,80,1024]{2,1,0:T(8,128)(2,1)} %bitcast.48.mine_ref, ...), custom_call_target="tpu_custom_call" | custom-call | flops 536870912 | bytes 4194304 | tf_op jit(solution)/shard_map/sparse_product/pallas_call | solution.py:216
  153.0 4.6 %collective-permute-done.21.u_ref = bf16[2048,128]{1,0:T(8,128)(2,1)S(1)} collective-permute-done((bf16[2048,128]{1,0:T(8,128)(2,1)}, bf16[2048,128]{1,0:T(8,128)(2,1)S(1)}, u32[]{:S(2)}, u32[]{:S(2)}) %collective-permute-start.21) | collective-permute-done | bytes 524320 | tf_op jit(solution)/shard_map/ppermute | solution.py:439
  157.6 2.4 rank_held.7
  160.7 4.8 %all-to-all-start.3 = ((bf16[4,1024,128]{2,1,0:T(8,128)(2,1)}), bf16[4,1024,128]{2,1,0:T(8,128)(2,1)}, u32[]{:S(2)}, u32[]{:S(2)}) async-start(bf16[4,1024,128]{2,1,0:T(8,128)(2,1)} %rank_held.7), calls=%async_computation.3 | async-start | bytes 2097152 | tf_op jit(solution)/shard_map/all_to_all | solution.py:488
  165.5 6.0 %input_grad.8.refs_0_ = bf16[2048,128]{1,0:T(8,128)(2,1)} custom-call(s32[6]{0:T(128)} %stack.41.meta_ref, bf16[4,1024,128]{2,1,0:T(8,128)(2,1)} %all-to-all-done.p_ref, bf16[16,80,1024]{2,1,0:T(8,128)(2,1)} %bitcast.48.mine_ref, bf16[16,80,1024]{2,1,0:T(8,128)(2,1)} %collective-permute-done.19.other_ref, f32[2048,128]{1,0:T(8,128)} %get-tuple-element.14.s_ref), custom_call_target="tpu_custom_call" | custom-call | flops 536870912 | bytes 4194304 | tf_op jit(solution)/shard_map/input_grad/pallas_call | solution.py:283
  171.6 3.5 collective-permute-start.20
  177.7 4.5 %sparse_product.10 = (f32[2048,128]{1,0:T(8,128)}, bf16[16,2,32,2048]{3,2,1,0:T(8,128)(2,1)S(1)}) custom-call(s32[6]{0:T(128)S(1)} %copy-done.29, s32[128]{0:T(128)S(1)} %bitcast.124, s32[128]{0:T(128)S(1)} %bitcast.133, bf16[2048,128]{1,0:T(8,128)(2,1)S(1)} %copy-done.15, bf16[16,80,1024]{2,1,0:T(8,128)(2,1)} %bitcast.48.mine_ref, ...), custom_call_target="tpu_custom_call" | custom-call | flops 536870912 | bytes 4194304 | tf_op jit(solution)/shard_map/sparse_product/pallas_call | solution.py:216
  182.2 3.4 collective-permute-done.20.u_ref
  185.7 2.3 rank_held.6
  188.8 4.8 %all-to-all-start.2 = ((bf16[4,1024,128]{2,1,0:T(8,128)(2,1)}), bf16[4,1024,128]{2,1,0:T(8,128)(2,1)}, u32[]{:S(2)}, u32[]{:S(2)}) async-start(bf16[4,1024,128]{2,1,0:T(8,128)(2,1)} %rank_held.6), calls=%async_computation.2 | async-start | bytes 2097152 | tf_op jit(solution)/shard_map/all_to_all | solution.py:488
  193.6 6.0 %input_grad.11.refs_1_ = bf16[2048,128]{1,0:T(8,128)(2,1)} custom-call(s32[6]{0:T(128)} %stack.41.meta_ref, bf16[4,1024,128]{2,1,0:T(8,128)(2,1)} %all-to-all-done.3.p_ref, bf16[16,80,1024]{2,1,0:T(8,128)(2,1)} %bitcast.48.mine_ref, bf16[16,80,1024]{2,1,0:T(8,128)(2,1)} %collective-permute-done.19.other_ref, f32[2048,128]{1,0:T(8,128)} %get-tuple-element.18.s_ref), custom_call_target="tpu_custom_call" | custom-call | flops 536870912 | bytes 4194304 | tf_op jit(solution)/shard_map/input_grad/pallas_call | solution.py:283
  199.7 3.5 collective-permute-start.23
  205.8 4.5 %sparse_product.11 = (f32[2048,128]{1,0:T(8,128)}, bf16[16,2,32,2048]{3,2,1,0:T(8,128)(2,1)S(1)}) custom-call(s32[6]{0:T(128)S(1)} %copy-done.30, s32[128]{0:T(128)S(1)} %bitcast.125, s32[128]{0:T(128)S(1)} %bitcast.134, bf16[2048,128]{1,0:T(8,128)(2,1)S(1)} %copy-done.17, bf16[16,80,1024]{2,1,0:T(8,128)(2,1)} %bitcast.48.mine_ref, ...), custom_call_target="tpu_custom_call" | custom-call | flops 536870912 | bytes 4194304 | tf_op jit(solution)/shard_map/sparse_product/pallas_call | solution.py:216
  210.3 2.2 collective-permute-done.23.u_ref
  212.6 2.4 rank_held.9
  215.8 4.8 %all-to-all-start.5 = ((bf16[4,1024,128]{2,1,0:T(8,128)(2,1)}), bf16[4,1024,128]{2,1,0:T(8,128)(2,1)}, u32[]{:S(2)}, u32[]{:S(2)}) async-start(bf16[4,1024,128]{2,1,0:T(8,128)(2,1)} %rank_held.9), calls=%async_computation.5 | async-start | bytes 2097152 | tf_op jit(solution)/shard_map/all_to_all | solution.py:488
  220.6 6.0 %input_grad.10.refs_1_ = bf16[2048,128]{1,0:T(8,128)(2,1)} custom-call(s32[6]{0:T(128)} %stack.41.meta_ref, bf16[4,1024,128]{2,1,0:T(8,128)(2,1)} %all-to-all-done.2.p_ref, bf16[16,80,1024]{2,1,0:T(8,128)(2,1)} %bitcast.48.mine_ref, bf16[16,80,1024]{2,1,0:T(8,128)(2,1)} %collective-permute-done.19.other_ref, f32[2048,128]{1,0:T(8,128)} %get-tuple-element.16.s_ref), custom_call_target="tpu_custom_call" | custom-call | flops 536870912 | bytes 4194304 | tf_op jit(solution)/shard_map/input_grad/pallas_call | solution.py:283
  226.6 3.6 %collective-permute-start.22 = (bf16[2048,128]{1,0:T(8,128)(2,1)}, bf16[2048,128]{1,0:T(8,128)(2,1)S(1)}, u32[]{:S(2)}, u32[]{:S(2)}) collective-permute-start(bf16[2048,128]{1,0:T(8,128)(2,1)} %input_grad.10.refs_1_), channel_id=1, source_target_pairs={{128,0},{256,128},{384,256},{129,1},{257,129},{385,257},{130,2},{2... | collective-permute-start | bytes 1572872 | tf_op jit(solution)/shard_map/ppermute | solution.py:439
  232.9 4.5 %sparse_product.12 = (f32[2048,128]{1,0:T(8,128)}, bf16[16,2,32,2048]{3,2,1,0:T(8,128)(2,1)S(1)}) custom-call(s32[6]{0:T(128)S(1)} %copy-done.31, s32[128]{0:T(128)S(1)} %bitcast.126, s32[128]{0:T(128)S(1)} %bitcast.135, bf16[2048,128]{1,0:T(8,128)(2,1)S(1)} %copy-done.20, bf16[16,80,1024]{2,1,0:T(8,128)(2,1)} %bitcast.48.mine_ref, ...), custom_call_target="tpu_custom_call" | custom-call | flops 536870912 | bytes 4194304 | tf_op jit(solution)/shard_map/sparse_product/pallas_call | solution.py:216
  238.3 2.4 rank_held.8
  241.5 4.8 %all-to-all-start.4 = ((bf16[4,1024,128]{2,1,0:T(8,128)(2,1)}), bf16[4,1024,128]{2,1,0:T(8,128)(2,1)}, u32[]{:S(2)}, u32[]{:S(2)}) async-start(bf16[4,1024,128]{2,1,0:T(8,128)(2,1)} %rank_held.8), calls=%async_computation.4 | async-start | bytes 2097152 | tf_op jit(solution)/shard_map/all_to_all | solution.py:488
  246.3 6.0 %input_grad.13.refs_2_ = bf16[2048,128]{1,0:T(8,128)(2,1)} custom-call(s32[6]{0:T(128)} %stack.41.meta_ref, bf16[4,1024,128]{2,1,0:T(8,128)(2,1)} %all-to-all-done.5.p_ref, bf16[16,80,1024]{2,1,0:T(8,128)(2,1)} %bitcast.48.mine_ref, bf16[16,80,1024]{2,1,0:T(8,128)(2,1)} %collective-permute-done.19.other_ref, f32[2048,128]{1,0:T(8,128)} %get-tuple-element.22.s_ref), custom_call_target="tpu_custom_call" | custom-call | flops 536870912 | bytes 4194304 | tf_op jit(solution)/shard_map/input_grad/pallas_call | solution.py:283
  252.3 3.5 collective-permute-start.25
  258.4 4.5 %sparse_product.13 = (f32[2048,128]{1,0:T(8,128)}, bf16[16,2,32,2048]{3,2,1,0:T(8,128)(2,1)S(1)}) custom-call(s32[6]{0:T(128)S(1)} %copy-done.32, s32[128]{0:T(128)S(1)} %bitcast.127, s32[128]{0:T(128)S(1)} %bitcast.136, bf16[2048,128]{1,0:T(8,128)(2,1)S(1)} %copy-done.22, bf16[16,80,1024]{2,1,0:T(8,128)(2,1)} %bitcast.48.mine_ref, ...), custom_call_target="tpu_custom_call" | custom-call | flops 536870912 | bytes 4194304 | tf_op jit(solution)/shard_map/sparse_product/pallas_call | solution.py:216
  265.0 5.9 %input_grad.12.refs_2_ = bf16[2048,128]{1,0:T(8,128)(2,1)} custom-call(s32[6]{0:T(128)} %stack.41.meta_ref, bf16[4,1024,128]{2,1,0:T(8,128)(2,1)} %all-to-all-done.4.p_ref, bf16[16,80,1024]{2,1,0:T(8,128)(2,1)} %bitcast.48.mine_ref, bf16[16,80,1024]{2,1,0:T(8,128)(2,1)} %collective-permute-done.19.other_ref, f32[2048,128]{1,0:T(8,128)} %get-tuple-element.20.s_ref), custom_call_target="tpu_custom_call" | custom-call | flops 536870912 | bytes 4194304 | tf_op jit(solution)/shard_map/input_grad/pallas_call | solution.py:283
  270.9 2.1 collective-permute-start.24
  274.5 7.9 %collective-permute-done.24.u_ref = bf16[2048,128]{1,0:T(8,128)(2,1)S(1)} collective-permute-done((bf16[2048,128]{1,0:T(8,128)(2,1)}, bf16[2048,128]{1,0:T(8,128)(2,1)S(1)}, u32[]{:S(2)}, u32[]{:S(2)}) %collective-permute-start.24) | collective-permute-done | bytes 524320 | tf_op jit(solution)/shard_map/ppermute | solution.py:439
  282.5 2.7 block_products.1
  289.3 3.3 rank_held.11
  292.6 4.9 %all-to-all-start.7 = ((bf16[4,1024,128]{2,1,0:T(8,128)(2,1)}), bf16[4,1024,128]{2,1,0:T(8,128)(2,1)}, u32[]{:S(2)}, u32[]{:S(2)}) async-start(bf16[4,1024,128]{2,1,0:T(8,128)(2,1)} %rank_held.11), calls=%async_computation.7 | async-start | bytes 2097152 | tf_op jit(solution)/shard_map/all_to_all | solution.py:488
  299.9 4.1 %collective-permute-start.27 = (bf16[8,128,128]{2,1,0:T(8,128)(2,1)S(1)}, bf16[8,128,128]{2,1,0:T(8,128)(2,1)S(1)}, u32[]{:S(2)}, u32[]{:S(2)}) collective-permute-start(bf16[8,128,128]{2,1,0:T(8,128)(2,1)S(1)} %slice.96), channel_id=1, source_target_pairs={{0,8},{4,12},{8,0},{12,4},{16,24},{20,28},{24,16},{28,20},{32,40},... | collective-permute-start | bytes 786440 | tf_op jit(solution)/shard_map/ppermute | solution.py:396
  304.1 4.6 %sparse_product.14 = (f32[2048,128]{1,0:T(8,128)}, bf16[16,2,32,2048]{3,2,1,0:T(8,128)(2,1)S(1)}) custom-call(s32[6]{0:T(128)S(1)} %copy-done.33, s32[128]{0:T(128)S(1)} %bitcast.129, s32[128]{0:T(128)S(1)} %bitcast.138, bf16[2048,128]{1,0:T(8,128)(2,1)} %collective-permute-done.25.u_ref, bf16[16,80,1024]{2,1,0:T(8,128)(2,1)} %bitcast.48.mine_ref, ...), custom_call_target="tpu_custom_call" | custom-call | flops 536870912 | bytes 4194304 | tf_op jit(solution)/shard_map/sparse_product/pallas_call | solution.py:216
  308.7 2.4 rank_held.10
  312.0 5.7 %all-to-all-start.6 = ((bf16[4,1024,128]{2,1,0:T(8,128)(2,1)}), bf16[4,1024,128]{2,1,0:T(8,128)(2,1)}, u32[]{:S(2)}, u32[]{:S(2)}) async-start(bf16[4,1024,128]{2,1,0:T(8,128)(2,1)} %rank_held.10), calls=%async_computation.6 | async-start | bytes 2097152 | tf_op jit(solution)/shard_map/all_to_all | solution.py:488
  318.8 5.2 %collective-permute-start.28 = (bf16[4,128,128]{2,1,0:T(8,128)(2,1)S(1)}, bf16[4,128,128]{2,1,0:T(8,128)(2,1)S(1)}, u32[]{:S(2)}, u32[]{:S(2)}) collective-permute-start(bf16[4,128,128]{2,1,0:T(8,128)(2,1)S(1)} %slice.97), channel_id=1, source_target_pairs={{0,16},{4,20},{8,24},{12,28},{16,0},{20,4},{24,8},{28,12},{32,48},... | collective-permute-start | bytes 393224 | tf_op jit(solution)/shard_map/ppermute | solution.py:396
  324.0 5.5 %collective-permute-done.28 = bf16[4,128,128]{2,1,0:T(8,128)(2,1)S(1)} collective-permute-done((bf16[4,128,128]{2,1,0:T(8,128)(2,1)S(1)}, bf16[4,128,128]{2,1,0:T(8,128)(2,1)S(1)}, u32[]{:S(2)}, u32[]{:S(2)}) %collective-permute-start.28) | collective-permute-done | bytes 131104 | tf_op jit(solution)/shard_map/ppermute | solution.py:396
  329.6 4.7 %collective-permute-start.29 = (bf16[2,128,128]{2,1,0:T(8,128)(2,1)S(1)}, bf16[2,128,128]{2,1,0:T(8,128)(2,1)S(1)}, u32[]{:S(2)}, u32[]{:S(2)}) collective-permute-start(bf16[2,128,128]{2,1,0:T(8,128)(2,1)S(1)} %slice.98), channel_id=1, source_target_pairs={{0,32},{4,36},{8,40},{12,44},{16,48},{20,52},{24,56},{28,60},{32,0... | collective-permute-start | bytes 196616 | tf_op jit(solution)/shard_map/ppermute | solution.py:396
  334.2 4.5 %sparse_product.15.s_ref = f32[2048,128]{1,0:T(8,128)} custom-call(s32[6]{0:T(128)S(1)} %copy-done.33, s32[128]{0:T(128)S(1)} %bitcast.130, s32[128]{0:T(128)S(1)} %bitcast.139, bf16[2048,128]{1,0:T(8,128)(2,1)S(1)} %copy-done.13, bf16[16,80,1024]{2,1,0:T(8,128)(2,1)} %bitcast.48.mine_ref, bf16[16,80,1024]{2,1,0:T(8,128)(2,1)} %collective-permute-done.19.other_ref, ...), custom_call_target="tpu_custom_call" | custom-call | flops 536870912 | bytes 4194304 | tf_op jit(solution)/shard_map/sparse_product/pallas_call | solution.py:216
  338.7 5.9 %input_grad.15.refs_3_ = bf16[2048,128]{1,0:T(8,128)(2,1)} custom-call(s32[6]{0:T(128)} %stack.41.meta_ref, bf16[4,1024,128]{2,1,0:T(8,128)(2,1)} %all-to-all-done.7.p_ref, bf16[16,80,1024]{2,1,0:T(8,128)(2,1)} %bitcast.48.mine_ref, bf16[16,80,1024]{2,1,0:T(8,128)(2,1)} %collective-permute-done.19.other_ref, f32[2048,128]{1,0:T(8,128)} %get-tuple-element.25.s_ref), custom_call_target="tpu_custom_call" | custom-call | flops 536870912 | bytes 4194304 | tf_op jit(solution)/shard_map/input_grad/pallas_call | solution.py:283
  344.6 2.7 finished.2.refs_4_
  347.4 5.7 %collective-permute-start.30 = (bf16[1,128,128]{2,1,0:T(8,128)(2,1)S(1)}, bf16[1,128,128]{2,1,0:T(8,128)(2,1)S(1)}, u32[]{:S(2)}, u32[]{:S(2)}) collective-permute-start(bf16[1,128,128]{2,1,0:T(8,128)(2,1)S(1)} %slice.99), channel_id=1, source_target_pairs={{0,64},{4,68},{8,72},{12,76},{16,80},{20,84},{24,88},{28,92},{32,9... | collective-permute-start | bytes 98312 | tf_op jit(solution)/shard_map/ppermute | solution.py:396
  353.2 5.9 %input_grad.14.refs_3_ = bf16[2048,128]{1,0:T(8,128)(2,1)} custom-call(s32[6]{0:T(128)} %stack.41.meta_ref, bf16[4,1024,128]{2,1,0:T(8,128)(2,1)} %all-to-all-done.6.p_ref, bf16[16,80,1024]{2,1,0:T(8,128)(2,1)} %bitcast.48.mine_ref, bf16[16,80,1024]{2,1,0:T(8,128)(2,1)} %collective-permute-done.19.other_ref, f32[2048,128]{1,0:T(8,128)} %sparse_product.15.s_ref), custom_call_target="tpu_custom_call" | custom-call | flops 536870912 | bytes 4194304 | tf_op jit(solution)/shard_map/input_grad/pallas_call | solution.py:283
  359.1 2.7 finished.3
  (164 shorter events, 67.2 us)
Async XLA Ops:
  0.6 28.2 %copy-start.37 = (bf16[1,64,1024]{2,1,0:T(8,128)(2,1)S(1)}, bf16[1,64,1024]{2,1,0:T(8,128)(2,1)}, u32[]{:S(2)}) copy-start(bf16[1,64,1024]{2,1,0:T(8,128)(2,1)} %param.10) | copy-start | bytes 393220
  0.6 14.0 %collective-permute-start = (bf16[32,2048]{1,0:T(8,128)(2,1)}, bf16[32,2048]{1,0:T(8,128)(2,1)S(1)}, u32[]{:S(2)}, u32[]{:S(2)}) collective-permute-start(bf16[32,2048]{1,0:T(8,128)(2,1)} %bitcast.145), channel_id=1, source_target_pairs={{0,64},{4,68},{8,72},{12,76},{16,80},{20,84},{24,88},{28,92},{32,9... | collective-permute-start | bytes 393224 | tf_op jit(solution)/shard_map/ppermute | solution.py:396
  9.3 19.5 %collective-permute-start.10 = (bf16[80,1024]{1,0:T(8,128)(2,1)S(1)}, bf16[80,1024]{1,0:T(8,128)(2,1)S(1)}, u32[]{:S(2)}, u32[]{:S(2)}) collective-permute-start(bf16[80,1024]{1,0:T(8,128)(2,1)S(1)} %pad_maximum_fusion.2), channel_id=1, source_target_pairs={{0,64},{4,68},{8,72},{12,76},{16,80},{20,84},{24,88},{28,92},{32,9... | collective-permute-start | bytes 491528 | tf_op jit(solution)/shard_map/ppermute | solution.py:396
  15.6 24.3 %collective-permute-start.1 = (bf16[2,32,2048]{2,1,0:T(8,128)(2,1)S(1)}, bf16[2,32,2048]{2,1,0:T(8,128)(2,1)S(1)}, u32[]{:S(2)}, u32[]{:S(2)}) collective-permute-start(bf16[2,32,2048]{2,1,0:T(8,128)(2,1)S(1)} %pad_maximum_fusion.1), channel_id=1, source_target_pairs={{0,8},{4,12},{8,16},{12,20},{16,24},{20,28},{24,32},{28,36},{32,40... | collective-permute-start | bytes 786440 | tf_op jit(solution)/shard_map/ppermute | solution.py:393
  19.9 21.9 %collective-permute-start.2 = (bf16[2,32,2048]{2,1,0:T(8,128)(2,1)S(1)}, bf16[2,32,2048]{2,1,0:T(8,128)(2,1)S(1)}, u32[]{:S(2)}, u32[]{:S(2)}) collective-permute-start(bf16[2,32,2048]{2,1,0:T(8,128)(2,1)S(1)} %pad_maximum_fusion.1), channel_id=1, source_target_pairs={{0,56},{4,60},{8,0},{12,4},{16,8},{20,12},{24,16},{28,20},{32,24},... | collective-permute-start | bytes 786440 | tf_op jit(solution)/shard_map/ppermute | solution.py:393
  28.9 18.1 %collective-permute-start.11 = (bf16[2,80,1024]{2,1,0:T(8,128)(2,1)S(1)}, bf16[2,80,1024]{2,1,0:T(8,128)(2,1)S(1)}, u32[]{:S(2)}, u32[]{:S(2)}) collective-permute-start(bf16[2,80,1024]{2,1,0:T(8,128)(2,1)S(1)} %pad_maximum_fusion), channel_id=1, source_target_pairs={{0,8},{4,12},{8,16},{12,20},{16,24},{20,28},{24,32},{28,36},{32,40... | collective-permute-start | bytes 983048 | tf_op jit(solution)/shard_map/ppermute | solution.py:393
  30.9 18.1 %collective-permute-start.12 = (bf16[2,80,1024]{2,1,0:T(8,128)(2,1)S(1)}, bf16[2,80,1024]{2,1,0:T(8,128)(2,1)S(1)}, u32[]{:S(2)}, u32[]{:S(2)}) collective-permute-start(bf16[2,80,1024]{2,1,0:T(8,128)(2,1)S(1)} %pad_maximum_fusion), channel_id=1, source_target_pairs={{0,56},{4,60},{8,0},{12,4},{16,8},{20,12},{24,16},{28,20},{32,24},... | collective-permute-start | bytes 983048 | tf_op jit(solution)/shard_map/ppermute | solution.py:393
  39.9 15.7 %collective-permute-start.3 = (bf16[2,32,2048]{2,1,0:T(8,128)(2,1)S(1)}, bf16[2,32,2048]{2,1,0:T(8,128)(2,1)S(1)}, u32[]{:S(2)}, u32[]{:S(2)}) collective-permute-start(bf16[2,32,2048]{2,1,0:T(8,128)(2,1)S(1)} %collective-permute-done.1), channel_id=1, source_target_pairs={{0,8},{4,12},{8,16},{12,20},{16,24},{20,28},{24,32},{28,36},{32,40... | collective-permute-start | bytes 786440 | tf_op jit(solution)/shard_map/ppermute | solution.py:393
  41.9 15.7 %collective-permute-start.4 = (bf16[2,32,2048]{2,1,0:T(8,128)(2,1)S(1)}, bf16[2,32,2048]{2,1,0:T(8,128)(2,1)S(1)}, u32[]{:S(2)}, u32[]{:S(2)}) collective-permute-start(bf16[2,32,2048]{2,1,0:T(8,128)(2,1)S(1)} %collective-permute-done.2), channel_id=1, source_target_pairs={{0,56},{4,60},{8,0},{12,4},{16,8},{20,12},{24,16},{28,20},{32,24},... | collective-permute-start | bytes 786440 | tf_op jit(solution)/shard_map/ppermute | solution.py:393
  47.1 15.7 %collective-permute-start.13 = (bf16[2,80,1024]{2,1,0:T(8,128)(2,1)S(1)}, bf16[2,80,1024]{2,1,0:T(8,128)(2,1)S(1)}, u32[]{:S(2)}, u32[]{:S(2)}) collective-permute-start(bf16[2,80,1024]{2,1,0:T(8,128)(2,1)S(1)} %collective-permute-done.11), channel_id=1, source_target_pairs={{0,8},{4,12},{8,16},{12,20},{16,24},{20,28},{24,32},{28,36},{32,40... | collective-permute-start | bytes 983048 | tf_op jit(solution)/shard_map/ppermute | solution.py:393
  49.0 15.7 %collective-permute-start.14 = (bf16[2,80,1024]{2,1,0:T(8,128)(2,1)S(1)}, bf16[2,80,1024]{2,1,0:T(8,128)(2,1)S(1)}, u32[]{:S(2)}, u32[]{:S(2)}) collective-permute-start(bf16[2,80,1024]{2,1,0:T(8,128)(2,1)S(1)} %collective-permute-done.12), channel_id=1, source_target_pairs={{0,56},{4,60},{8,0},{12,4},{16,8},{20,12},{24,16},{28,20},{32,24},... | collective-permute-start | bytes 983048 | tf_op jit(solution)/shard_map/ppermute | solution.py:393
  55.7 15.8 %collective-permute-start.5 = (bf16[2,32,2048]{2,1,0:T(8,128)(2,1)S(1)}, bf16[2,32,2048]{2,1,0:T(8,128)(2,1)S(1)}, u32[]{:S(2)}, u32[]{:S(2)}) collective-permute-start(bf16[2,32,2048]{2,1,0:T(8,128)(2,1)S(1)} %collective-permute-done.3), channel_id=1, source_target_pairs={{0,8},{4,12},{8,16},{12,20},{16,24},{20,28},{24,32},{28,36},{32,40... | collective-permute-start | bytes 786440 | tf_op jit(solution)/shard_map/ppermute | solution.py:393
  57.6 15.8 %collective-permute-start.6 = (bf16[2,32,2048]{2,1,0:T(8,128)(2,1)S(1)}, bf16[2,32,2048]{2,1,0:T(8,128)(2,1)S(1)}, u32[]{:S(2)}, u32[]{:S(2)}) collective-permute-start(bf16[2,32,2048]{2,1,0:T(8,128)(2,1)S(1)} %collective-permute-done.4), channel_id=1, source_target_pairs={{0,56},{4,60},{8,0},{12,4},{16,8},{20,12},{24,16},{28,20},{32,24},... | collective-permute-start | bytes 786440 | tf_op jit(solution)/shard_map/ppermute | solution.py:393
  62.8 20.2 %collective-permute-start.15 = (bf16[2,80,1024]{2,1,0:T(8,128)(2,1)S(1)}, bf16[2,80,1024]{2,1,0:T(8,128)(2,1)S(1)}, u32[]{:S(2)}, u32[]{:S(2)}) collective-permute-start(bf16[2,80,1024]{2,1,0:T(8,128)(2,1)S(1)} %collective-permute-done.13), channel_id=1, source_target_pairs={{0,8},{4,12},{8,16},{12,20},{16,24},{20,28},{24,32},{28,36},{32,40... | collective-permute-start | bytes 983048 | tf_op jit(solution)/shard_map/ppermute | solution.py:393
  64.8 20.2 %collective-permute-start.16 = (bf16[2,80,1024]{2,1,0:T(8,128)(2,1)S(1)}, bf16[2,80,1024]{2,1,0:T(8,128)(2,1)S(1)}, u32[]{:S(2)}, u32[]{:S(2)}) collective-permute-start(bf16[2,80,1024]{2,1,0:T(8,128)(2,1)S(1)} %collective-permute-done.14), channel_id=1, source_target_pairs={{0,56},{4,60},{8,0},{12,4},{16,8},{20,12},{24,16},{28,20},{32,24},... | collective-permute-start | bytes 983048 | tf_op jit(solution)/shard_map/ppermute | solution.py:393
  71.4 8.1 %collective-permute-start.7 = (bf16[1,32,2048]{2,1,0:T(8,128)(2,1)S(1)}, bf16[1,32,2048]{2,1,0:T(8,128)(2,1)S(1)}, u32[]{:S(2)}, u32[]{:S(2)}) collective-permute-start(bf16[1,32,2048]{2,1,0:T(8,128)(2,1)S(1)} %slice.69), channel_id=1, source_target_pairs={{0,8},{4,12},{8,16},{12,20},{16,24},{20,28},{24,32},{28,36},{32,40... | collective-permute-start | bytes 393224 | tf_op jit(solution)/shard_map/ppermute | solution.py:393
  73.4 7.6 %collective-permute-start.8 = (bf16[1,32,2048]{2,1,0:T(8,128)(2,1)S(1)}, bf16[1,32,2048]{2,1,0:T(8,128)(2,1)S(1)}, u32[]{:S(2)}, u32[]{:S(2)}) collective-permute-start(bf16[1,32,2048]{2,1,0:T(8,128)(2,1)S(1)} %slice.70), channel_id=1, source_target_pairs={{0,56},{4,60},{8,0},{12,4},{16,8},{20,12},{24,16},{28,20},{32,24},... | collective-permute-start | bytes 393224 | tf_op jit(solution)/shard_map/ppermute | solution.py:393
  81.1 20.4 %copy-start = (bf16[2,8,32,2048]{3,2,1,0:T(8,128)(2,1)}, bf16[2,8,32,2048]{3,2,1,0:T(8,128)(2,1)S(1)}, u32[]{:S(2)}) copy-start(bf16[2,8,32,2048]{3,2,1,0:T(8,128)(2,1)S(1)} %bitcast_dynamic-update-slice_fusion.16) | copy-start | bytes 6291460
  81.1 21.0 %collective-permute-start.9 = (bf16[16,32,2048]{2,1,0:T(8,128)(2,1)S(1)}, bf16[16,32,2048]{2,1,0:T(8,128)(2,1)}, u32[]{:S(2)}, u32[]{:S(2)}) collective-permute-start(bf16[16,32,2048]{2,1,0:T(8,128)(2,1)S(1)} %bitcast.106), channel_id=1, source_target_pairs={{0,4},{4,0},{8,12},{12,8},{16,20},{20,16},{24,28},{28,24},{32,36},... | collective-permute-start | bytes 6291464 | tf_op jit(solution)/shard_map/ppermute | solution.py:396
  83.0 10.4 %collective-permute-start.17 = (bf16[1,80,1024]{2,1,0:T(8,128)(2,1)S(1)}, bf16[1,80,1024]{2,1,0:T(8,128)(2,1)S(1)}, u32[]{:S(2)}, u32[]{:S(2)}) collective-permute-start(bf16[1,80,1024]{2,1,0:T(8,128)(2,1)S(1)} %slice.71), channel_id=1, source_target_pairs={{0,8},{4,12},{8,16},{12,20},{16,24},{20,28},{24,32},{28,36},{32,40... | collective-permute-start | bytes 491528 | tf_op jit(solution)/shard_map/ppermute | solution.py:393
  85.0 9.7 %collective-permute-start.18 = (bf16[1,80,1024]{2,1,0:T(8,128)(2,1)S(1)}, bf16[1,80,1024]{2,1,0:T(8,128)(2,1)S(1)}, u32[]{:S(2)}, u32[]{:S(2)}) collective-permute-start(bf16[1,80,1024]{2,1,0:T(8,128)(2,1)S(1)} %slice.72), channel_id=1, source_target_pairs={{0,56},{4,60},{8,0},{12,4},{16,8},{20,12},{24,16},{28,20},{32,24},... | collective-permute-start | bytes 491528 | tf_op jit(solution)/shard_map/ppermute | solution.py:393
  95.3 36.5 %collective-permute-start.19 = (bf16[16,80,1024]{2,1,0:T(8,128)(2,1)}, bf16[16,80,1024]{2,1,0:T(8,128)(2,1)}, u32[]{:S(2)}, u32[]{:S(2)}) collective-permute-start(bf16[16,80,1024]{2,1,0:T(8,128)(2,1)} %bitcast.48.mine_ref), channel_id=1, source_target_pairs={{0,4},{4,0},{8,12},{12,8},{16,20},{20,16},{24,28},{28,24},{32,36},... | collective-permute-start | bytes 7864328 | tf_op jit(solution)/shard_map/ppermute | solution.py:396
  106.8 19.4 %all-to-all-start.1 = ((bf16[4,1024,128]{2,1,0:T(8,128)(2,1)}), bf16[4,1024,128]{2,1,0:T(8,128)(2,1)}, u32[]{:S(2)}, u32[]{:S(2)}) async-start(bf16[4,1024,128]{2,1,0:T(8,128)(2,1)} %rank_partial.3), calls=%async_computation.1 | async-start | bytes 2097152 | tf_op jit(solution)/shard_map/all_to_all | solution.py:488
  112.6 19.2 %copy-start.8 = (bf16[1,128,2048]{1,2,0:T(8,128)(2,1)S(1)}, bf16[1,128,2048]{1,2,0:T(8,128)(2,1)}, u32[]{:S(2)}) copy-start(bf16[1,128,2048]{1,2,0:T(8,128)(2,1)} %copy.29) | copy-start | bytes 1572868
  112.6 19.2 %copy-start.27 = (s32[6]{0:T(128)S(1)}, s32[6]{0:T(128)}, u32[]{:S(2)}) copy-start(s32[6]{0:T(128)} %stack.41.meta_ref) | copy-start | bytes 76
  112.6 19.2 %copy-start.34 = (s32[1,128]{1,0:T(1,128)S(1)}, s32[1,128]{1,0:T(1,128)}, u32[]{:S(2)}) copy-start(s32[1,128]{1,0:T(1,128)} %param.12) | copy-start | bytes 1540
  112.6 19.2 %copy-start.35 = (s32[1,128]{1,0:T(1,128)S(1)}, s32[1,128]{1,0:T(1,128)}, u32[]{:S(2)}) copy-start(s32[1,128]{1,0:T(1,128)} %param.13) | copy-start | bytes 1540
  117.5 14.4 %copy-start.1 = (bf16[2,8,32,2048]{3,2,1,0:T(8,128)(2,1)S(1)}, bf16[2,8,32,2048]{3,2,1,0:T(8,128)(2,1)}, u32[]{:S(2)}) copy-start(bf16[2,8,32,2048]{3,2,1,0:T(8,128)(2,1)} %copy-done) | copy-start | bytes 6291460
  126.2 34.6 %all-to-all-start = ((bf16[4,1024,128]{2,1,0:T(8,128)(2,1)}), bf16[4,1024,128]{2,1,0:T(8,128)(2,1)}, u32[]{:S(2)}, u32[]{:S(2)}) async-start(bf16[4,1024,128]{2,1,0:T(8,128)(2,1)} %rank_partial.2), calls=%async_computation | async-start | bytes 2097152 | tf_op jit(solution)/shard_map/all_to_all | solution.py:488
  136.4 9.5 %copy-start.28 = (s32[6]{0:T(128)S(1)}, s32[6]{0:T(128)}, u32[]{:S(2)}) copy-start(s32[6]{0:T(128)} %stack.41.meta_ref) | copy-start | bytes 76
  142.4 15.2 %collective-permute-start.21 = (bf16[2048,128]{1,0:T(8,128)(2,1)}, bf16[2048,128]{1,0:T(8,128)(2,1)S(1)}, u32[]{:S(2)}, u32[]{:S(2)}) collective-permute-start(bf16[2048,128]{1,0:T(8,128)(2,1)} %input_grad.9.refs_0_), channel_id=1, source_target_pairs={{128,0},{256,128},{384,256},{129,1},{257,129},{385,257},{130,2},{2... | collective-permute-start | bytes 1572872 | tf_op jit(solution)/shard_map/ppermute | solution.py:439
  145.9 1.6 copy-start.2
  160.7 28.1 %all-to-all-start.3 = ((bf16[4,1024,128]{2,1,0:T(8,128)(2,1)}), bf16[4,1024,128]{2,1,0:T(8,128)(2,1)}, u32[]{:S(2)}, u32[]{:S(2)}) async-start(bf16[4,1024,128]{2,1,0:T(8,128)(2,1)} %rank_held.7), calls=%async_computation.3 | async-start | bytes 2097152 | tf_op jit(solution)/shard_map/all_to_all | solution.py:488
  165.5 9.5 %copy-start.29 = (s32[6]{0:T(128)S(1)}, s32[6]{0:T(128)}, u32[]{:S(2)}) copy-start(s32[6]{0:T(128)} %stack.41.meta_ref) | copy-start | bytes 76
  171.6 14.1 %collective-permute-start.20 = (bf16[2048,128]{1,0:T(8,128)(2,1)}, bf16[2048,128]{1,0:T(8,128)(2,1)S(1)}, u32[]{:S(2)}, u32[]{:S(2)}) collective-permute-start(bf16[2048,128]{1,0:T(8,128)(2,1)} %input_grad.8.refs_0_), channel_id=1, source_target_pairs={{128,0},{256,128},{384,256},{129,1},{257,129},{385,257},{130,2},{2... | collective-permute-start | bytes 1572872 | tf_op jit(solution)/shard_map/ppermute | solution.py:439
  188.8 26.9 %all-to-all-start.2 = ((bf16[4,1024,128]{2,1,0:T(8,128)(2,1)}), bf16[4,1024,128]{2,1,0:T(8,128)(2,1)}, u32[]{:S(2)}, u32[]{:S(2)}) async-start(bf16[4,1024,128]{2,1,0:T(8,128)(2,1)} %rank_held.6), calls=%async_computation.2 | async-start | bytes 2097152 | tf_op jit(solution)/shard_map/all_to_all | solution.py:488
  193.6 9.5 %copy-start.30 = (s32[6]{0:T(128)S(1)}, s32[6]{0:T(128)}, u32[]{:S(2)}) copy-start(s32[6]{0:T(128)} %stack.41.meta_ref) | copy-start | bytes 76
  199.7 12.9 %collective-permute-start.23 = (bf16[2048,128]{1,0:T(8,128)(2,1)}, bf16[2048,128]{1,0:T(8,128)(2,1)S(1)}, u32[]{:S(2)}, u32[]{:S(2)}) collective-permute-start(bf16[2048,128]{1,0:T(8,128)(2,1)} %input_grad.11.refs_1_), channel_id=1, source_target_pairs={{128,0},{256,128},{384,256},{129,1},{257,129},{385,257},{130,2},{2... | collective-permute-start | bytes 1572872 | tf_op jit(solution)/shard_map/ppermute | solution.py:439
  203.2 1.6 copy-start.4
  215.8 25.7 %all-to-all-start.5 = ((bf16[4,1024,128]{2,1,0:T(8,128)(2,1)}), bf16[4,1024,128]{2,1,0:T(8,128)(2,1)}, u32[]{:S(2)}, u32[]{:S(2)}) async-start(bf16[4,1024,128]{2,1,0:T(8,128)(2,1)} %rank_held.9), calls=%async_computation.5 | async-start | bytes 2097152 | tf_op jit(solution)/shard_map/all_to_all | solution.py:488
  220.6 9.7 %copy-start.31 = (s32[6]{0:T(128)S(1)}, s32[6]{0:T(128)}, u32[]{:S(2)}) copy-start(s32[6]{0:T(128)} %stack.41.meta_ref) | copy-start | bytes 76
  226.6 11.7 %collective-permute-start.22 = (bf16[2048,128]{1,0:T(8,128)(2,1)}, bf16[2048,128]{1,0:T(8,128)(2,1)S(1)}, u32[]{:S(2)}, u32[]{:S(2)}) collective-permute-start(bf16[2048,128]{1,0:T(8,128)(2,1)} %input_grad.10.refs_1_), channel_id=1, source_target_pairs={{128,0},{256,128},{384,256},{129,1},{257,129},{385,257},{130,2},{2... | collective-permute-start | bytes 1572872 | tf_op jit(solution)/shard_map/ppermute | solution.py:439
  241.5 23.5 %all-to-all-start.4 = ((bf16[4,1024,128]{2,1,0:T(8,128)(2,1)}), bf16[4,1024,128]{2,1,0:T(8,128)(2,1)}, u32[]{:S(2)}, u32[]{:S(2)}) async-start(bf16[4,1024,128]{2,1,0:T(8,128)(2,1)} %rank_held.8), calls=%async_computation.4 | async-start | bytes 2097152 | tf_op jit(solution)/shard_map/all_to_all | solution.py:488
  246.3 9.5 %copy-start.32 = (s32[6]{0:T(128)S(1)}, s32[6]{0:T(128)}, u32[]{:S(2)}) copy-start(s32[6]{0:T(128)} %stack.41.meta_ref) | copy-start | bytes 76
  252.3 20.7 %collective-permute-start.25 = (bf16[2048,128]{1,0:T(8,128)(2,1)}, bf16[2048,128]{1,0:T(8,128)(2,1)}, u32[]{:S(2)}, u32[]{:S(2)}) collective-permute-start(bf16[2048,128]{1,0:T(8,128)(2,1)} %input_grad.13.refs_2_), channel_id=1, source_target_pairs={{128,0},{256,128},{384,256},{129,1},{257,129},{385,257},{130,2},{2... | collective-permute-start | bytes 1572872 | tf_op jit(solution)/shard_map/ppermute | solution.py:439
  255.8 1.6 copy-start.6
  263.0 2.0 copy-start.24
  270.9 11.4 %copy-start.10 = (bf16[1,128,2048]{1,2,0:T(8,128)(2,1)S(1)}, bf16[1,128,2048]{1,2,0:T(8,128)(2,1)}, u32[]{:S(2)}) copy-start(bf16[1,128,2048]{1,2,0:T(8,128)(2,1)} %copy.28) | copy-start | bytes 1572868
  270.9 11.4 %copy-start.18 = (bf16[2048,128]{1,0:T(8,128)(2,1)S(1)}, bf16[2048,128]{1,0:T(8,128)(2,1)}, u32[]{:S(2)}) copy-start(bf16[2048,128]{1,0:T(8,128)(2,1)} %copy-done.16) | copy-start | bytes 1572868
  270.9 11.4 %copy-start.23 = (bf16[2048,128]{1,0:T(8,128)(2,1)S(1)}, bf16[2048,128]{1,0:T(8,128)(2,1)}, u32[]{:S(2)}) copy-start(bf16[2048,128]{1,0:T(8,128)(2,1)} %copy-done.21) | copy-start | bytes 1572868
  270.9 11.4 %collective-permute-start.24 = (bf16[2048,128]{1,0:T(8,128)(2,1)}, bf16[2048,128]{1,0:T(8,128)(2,1)S(1)}, u32[]{:S(2)}, u32[]{:S(2)}) collective-permute-start(bf16[2048,128]{1,0:T(8,128)(2,1)} %input_grad.12.refs_2_), channel_id=1, source_target_pairs={{128,0},{256,128},{384,256},{129,1},{257,129},{385,257},{130,2},{2... | collective-permute-start | bytes 1572872 | tf_op jit(solution)/shard_map/ppermute | solution.py:439
  273.0 9.5 %copy-start.26 = (bf16[1,2,128,2048]{3,2,1,0:T(8,128)(2,1)S(1)}, bf16[1,2,128,2048]{3,2,1,0:T(8,128)(2,1)}, u32[]{:S(2)}) copy-start(bf16[1,2,128,2048]{3,2,1,0:T(8,128)(2,1)} %param.8) | copy-start | bytes 3145732
  273.0 9.5 %copy-start.33 = (s32[6]{0:T(128)S(1)}, s32[6]{0:T(128)}, u32[]{:S(2)}) copy-start(s32[6]{0:T(128)} %stack.41.meta_ref) | copy-start | bytes 76
  282.3 2.8 copy-start.12
  282.5 6.8 %copy-start.25 = (bf16[16,2,32,2048]{3,2,1,0:T(8,128)(2,1)S(1)}, bf16[16,2,32,2048]{3,2,1,0:T(8,128)(2,1)}, u32[]{:S(2)}) copy-start(bf16[16,2,32,2048]{3,2,1,0:T(8,128)(2,1)} %copy-done.24) | copy-start | bytes 12582916
  287.4 10.2 %collective-permute-start.26 = (bf16[16,128,128]{2,1,0:T(8,128)(2,1)}, bf16[16,128,128]{2,1,0:T(8,128)(2,1)S(1)}, u32[]{:S(2)}, u32[]{:S(2)}) collective-permute-start(bf16[16,128,128]{2,1,0:T(8,128)(2,1)} %slice.95), channel_id=1, source_target_pairs={{0,4},{4,0},{8,12},{12,8},{16,20},{20,16},{24,28},{28,24},{32,36},... | collective-permute-start | bytes 1572872 | tf_op jit(solution)/shard_map/ppermute | solution.py:396
  292.6 11.4 %copy-start.7 = (bf16[2,8,32,2048]{3,2,1,0:T(8,128)(2,1)S(1)}, bf16[2,8,32,2048]{3,2,1,0:T(8,128)(2,1)}, u32[]{:S(2)}) copy-start(bf16[2,8,32,2048]{3,2,1,0:T(8,128)(2,1)} %copy-done) | copy-start | bytes 6291460
  292.6 19.3 %all-to-all-start.7 = ((bf16[4,1024,128]{2,1,0:T(8,128)(2,1)}), bf16[4,1024,128]{2,1,0:T(8,128)(2,1)}, u32[]{:S(2)}, u32[]{:S(2)}) async-start(bf16[4,1024,128]{2,1,0:T(8,128)(2,1)} %rank_held.11), calls=%async_computation.7 | async-start | bytes 2097152 | tf_op jit(solution)/shard_map/all_to_all | solution.py:488
  299.9 8.8 %copy-start.13 = (bf16[2048,128]{1,0:T(8,128)(2,1)S(1)}, bf16[2048,128]{1,0:T(8,128)(2,1)}, u32[]{:S(2)}) copy-start(bf16[2048,128]{1,0:T(8,128)(2,1)} %copy-done.12) | copy-start | bytes 1572868
  299.9 17.7 %collective-permute-start.27 = (bf16[8,128,128]{2,1,0:T(8,128)(2,1)S(1)}, bf16[8,128,128]{2,1,0:T(8,128)(2,1)S(1)}, u32[]{:S(2)}, u32[]{:S(2)}) collective-permute-start(bf16[8,128,128]{2,1,0:T(8,128)(2,1)S(1)} %slice.96), channel_id=1, source_target_pairs={{0,8},{4,12},{8,0},{12,4},{16,24},{20,28},{24,16},{28,20},{32,40},... | collective-permute-start | bytes 786440 | tf_op jit(solution)/shard_map/ppermute | solution.py:396
  312.0 41.2 %all-to-all-start.6 = ((bf16[4,1024,128]{2,1,0:T(8,128)(2,1)}), bf16[4,1024,128]{2,1,0:T(8,128)(2,1)}, u32[]{:S(2)}, u32[]{:S(2)}) async-start(bf16[4,1024,128]{2,1,0:T(8,128)(2,1)} %rank_held.10), calls=%async_computation.6 | async-start | bytes 2097152 | tf_op jit(solution)/shard_map/all_to_all | solution.py:488
  318.8 10.7 %collective-permute-start.28 = (bf16[4,128,128]{2,1,0:T(8,128)(2,1)S(1)}, bf16[4,128,128]{2,1,0:T(8,128)(2,1)S(1)}, u32[]{:S(2)}, u32[]{:S(2)}) collective-permute-start(bf16[4,128,128]{2,1,0:T(8,128)(2,1)S(1)} %slice.97), channel_id=1, source_target_pairs={{0,16},{4,20},{8,24},{12,28},{16,0},{20,4},{24,8},{28,12},{32,48},... | collective-permute-start | bytes 393224 | tf_op jit(solution)/shard_map/ppermute | solution.py:396
  329.6 17.8 %collective-permute-start.29 = (bf16[2,128,128]{2,1,0:T(8,128)(2,1)S(1)}, bf16[2,128,128]{2,1,0:T(8,128)(2,1)S(1)}, u32[]{:S(2)}, u32[]{:S(2)}) collective-permute-start(bf16[2,128,128]{2,1,0:T(8,128)(2,1)S(1)} %slice.98), channel_id=1, source_target_pairs={{0,32},{4,36},{8,40},{12,44},{16,48},{20,52},{24,56},{28,60},{32,0... | collective-permute-start | bytes 196616 | tf_op jit(solution)/shard_map/ppermute | solution.py:396
  347.4 14.4 %collective-permute-start.30 = (bf16[1,128,128]{2,1,0:T(8,128)(2,1)S(1)}, bf16[1,128,128]{2,1,0:T(8,128)(2,1)S(1)}, u32[]{:S(2)}, u32[]{:S(2)}) collective-permute-start(bf16[1,128,128]{2,1,0:T(8,128)(2,1)S(1)} %slice.99), channel_id=1, source_target_pairs={{0,64},{4,68},{8,72},{12,76},{16,80},{20,84},{24,88},{28,92},{32,9... | collective-permute-start | bytes 98312 | tf_op jit(solution)/shard_map/ppermute | solution.py:396
  (13 other events, 13.9 us)
